TPU v7x, 128 devices: a whole 4x4x4 slice. The times are simulated.
128 devices in a mesh: row: 16 (over y_lo, z, core), col: 8 (over x, y_hi).
Axes of the slice: x: 4, y: 4 (y_hi: 2, y_lo: 2; y = y_hi * 2 + y_lo), z: 4, core: 2. Of those that a mesh axis runs over, the one named last changes fastest.
Arguments:
- potential: float32 [512, 512, 512], P(('row', 'col')), may hold values from -6 to 6
- basis_left: bfloat16 [8192, 128, 384], P(('row', 'col')), may hold values from -1.1953125 to 1.1953125
- basis_right: bfloat16 [8192, 128, 384], P(('row', 'col')), may hold values from -1.1953125 to 1.1953125
- core_matrix: bfloat16 [8192, 8192], P('row', 'col'), may hold values from -3 to 3
- density: bfloat16 [8192, 8192], P('row', 'col'), as said below
- pattern: int32 [64, 64], replicated, may hold values from 0 to 1, as said below
- pair_atoms: int32 [8192, 2], P(('row', 'col')), may hold values from 0 to 63, as said below
- cube_offsets: int32 [8192, 3], P(('row', 'col')), may hold values from 0 to 504, as said below
- live_count: int32 [128], P(('row', 'col')), may hold values from 32 to 64, as said below
Outputs:
- hamiltonian: bfloat16 [8192, 8192], P('row', 'col')
- product: float32 [8192, 8192], P('row', 'col')
Inputs may be any that keep to these rules, and one draw needn't show every extreme that they name: `pattern`: symmetric; every diagonal block is 1. density is symmetric. `pair_atoms`: the owner of block (i, j) is (i // 4, j // 8) on a 16 x 8 grid. Among the 64 entry slots of one slab at most 1 name blocks of one owner, and in every draw one owner is named by a live entry of every slab. `cube_offsets`: column 0 is at most 2, column 1 at most 504, column 2 at most 504. `live_count`: some slab uses all its slots.
All inputs are finite; a program needn't handle non-finite values.
Results may differ from a plain program's by a relative error of at most 0.0092.
Values may be sent and summed in bfloat16 or wider, within the bound.
No kernel may reach another device: no remote copies, remote signals or barrier semaphores. Data moves between devices by JAX's collectives and lax.ppermute only.
A program may use at most 192 MiB of HBM per device.

v0:
```python
import functools

import jax
import jax.numpy as jnp
from jax import lax
from jax.experimental import pallas as pl
from jax.experimental.pallas import tpu as pltpu
from jax.sharding import Mesh
from jax.sharding import PartitionSpec as P


NB = 128
ENTRIES = 64
DEVICES = 128
ATOM_ROWS = 4
ATOM_COLS = 8
CELLS = 384
ROW = ("yl", "z", "c")
COL = ("x", "yh")
ALL = ("yl", "z", "c", "x", "yh")


SMEM = pl.BlockSpec(memory_space=pltpu.SMEM)


def shift(array, axis, step):
    size = lax.axis_size(axis)
    return lax.ppermute(array, axis, [(i, (i + step) % size) for i in range(size)])


def turned_pair(slab, first_plane, y0, z0):
    tile = z0 >> 7
    within = z0 & 127
    tile_after = jnp.minimum(tile + 1, 3)
    lane = lax.broadcasted_iota(jnp.int32, (8, 128), 1)
    from_low = (lane & 63) + within < 128
    planes = []
    for k in range(2):
        turn = (128 + 64 * k - within) & 127
        plane = 2048 * (first_plane + k) + y0
        here = pltpu.roll(slab[pl.ds(plane + 512 * tile, 8), :], turn, 1)
        after = pltpu.roll(slab[pl.ds(plane + 512 * tile_after, 8), :], turn, 1)
        planes.append(jnp.where(from_low, here, after))
    return jnp.where(lane < 64, planes[0], planes[1])


def as_rows(windows):
    lane = lax.broadcasted_iota(jnp.int32, windows.shape, 1)
    sub = lax.broadcasted_iota(jnp.int32, windows.shape, 0) & 7
    for bit in range(3):
        windows = jnp.where((sub >> bit) & 1 == 1, pltpu.roll(windows, 8 << bit, 1), windows)
    windows = jnp.where((lane >> 3) & 7 == sub, windows, 0.0)
    return jnp.sum(windows.reshape(-1, 8, 128), axis=1)


def load_columns(potential, slab, sem):
    copies = [
        pltpu.make_async_copy(
            potential.at[p, :, 128 * t : 128 * t + 128],
            slab.at[(p * 4 + t) * 512 : (p * 4 + t) * 512 + 512, :],
            sem.at[p * 4 + t],
        )
        for p in range(4)
        for t in range(4)
    ]
    for copy in copies:
        copy.start()
    for copy in copies:
        copy.wait()


def edge_kernel(prev_ref, next_ref, potential, prev_out, next_out, slab, held, sem):
    load_columns(potential, slab, sem)

    @pl.loop(0, ENTRIES, unroll=8)
    def _(e):
        row = pl.multiple_of(e * 8, 8)
        held[0, pl.ds(row, 8), :] = turned_pair(slab, 0, prev_ref[e], prev_ref[ENTRIES + e])
        held[1, pl.ds(row, 8), :] = turned_pair(slab, 2, next_ref[e], next_ref[ENTRIES + e])

    prev_out[...] = as_rows(held[0])
    next_out[...] = as_rows(held[1])


def own_kernel(own_ref, potential, out, slab, held, sem):
    load_columns(potential, slab, sem)

    @pl.loop(0, ENTRIES, unroll=8)
    def _(e):
        row = pl.multiple_of(e * 8, 8)
        for k in range(2):
            held[k, pl.ds(row, 8), :] = turned_pair(slab, 2 * k, own_ref[e], own_ref[ENTRIES + e])

    for k in range(2):
        out[k] = as_rows(held[k])


CUT_SCRATCH = [
    pltpu.VMEM((16 * 512, 128), jnp.float32),
    pltpu.VMEM((2, ENTRIES * 8, 128), jnp.float32),
    pltpu.SemaphoreType.DMA((16,)),
]


def cut_edges(prev_yz, next_yz, potential):
    shape = jax.ShapeDtypeStruct((ENTRIES, 128), jnp.float32)
    return pl.pallas_call(
        edge_kernel,
        out_shape=(shape, shape),
        in_specs=[SMEM, SMEM, pl.BlockSpec(memory_space=pl.ANY)],
        scratch_shapes=CUT_SCRATCH,
        name="cut_edges",
    )(prev_yz, next_yz, potential)


def cut_own(yz, potential):
    return pl.pallas_call(
        own_kernel,
        out_shape=jax.ShapeDtypeStruct((2, ENTRIES, 128), jnp.float32),
        in_specs=[SMEM, pl.BlockSpec(memory_space=pl.ANY)],
        scratch_shapes=CUT_SCRATCH,
        name="cut_own",
    )(yz, potential)


GROUP = 8


TAIL = 8


def partial_kernel(owner_ref, mark_ref, cubes, left, right, out):
    step = pl.program_id(0)

    @pl.when(step == 0)
    def _():
        out[:, NB:, :] = jnp.zeros((DEVICES, TAIL, NB), jnp.bfloat16)

    for g in range(GROUP):
        e = step * GROUP + g
        weighted = (left[g].astype(jnp.float32) * cubes[g : g + 1, :]).astype(jnp.bfloat16)
        block = lax.dot_general(
            weighted, right[g], (((1,), (1,)), ((), ())), preferred_element_type=jnp.float32
        )
        owner = owner_ref[e]
        out[owner, :NB, :] = block.astype(jnp.bfloat16)
        out[owner, NB:, :] = jnp.full((TAIL, NB), mark_ref[e].astype(jnp.float32)).astype(
            jnp.bfloat16
        )


def partial_blocks(owner, mark, cubes, left, right):
    return pl.pallas_call(
        partial_kernel,
        grid_spec=pltpu.PrefetchScalarGridSpec(
            num_scalar_prefetch=2,
            grid=(ENTRIES // GROUP,),
            in_specs=[
                pl.BlockSpec((GROUP, CELLS), lambda i, *_: (i, 0)),
                pl.BlockSpec((GROUP, NB, CELLS), lambda i, *_: (i, 0, 0)),
                pl.BlockSpec((GROUP, NB, CELLS), lambda i, *_: (i, 0, 0)),
            ],
            out_specs=pl.BlockSpec((DEVICES, NB + TAIL, NB), lambda i, *_: (0, 0, 0)),
        ),
        out_shape=jax.ShapeDtypeStruct((DEVICES, NB + TAIL, NB), jnp.bfloat16),
        name="partial_blocks",
    )(owner, mark, cubes, left, right)


SUM_GROUP = 16


def sum_kernel(pattern_ref, core_ref, core, received, full, mine, theirs, total):
    step = pl.program_id(0)

    @pl.when(step == 0)
    def _():
        total[: ATOM_ROWS * NB, :] = core[...].astype(jnp.float32)

    marks = [
        jnp.max(received[g, NB:, :].astype(jnp.float32)).astype(jnp.int32)
        for g in range(SUM_GROUP)
    ]
    for g, mark in enumerate(marks):
        where = jnp.where(mark > 0, mark - 1, ATOM_ROWS * ATOM_COLS)
        rows = pl.ds(pl.multiple_of((where >> 3) * NB, NB), NB)
        cols = pl.ds(pl.multiple_of((where & 7) * NB, NB), NB)
        total[rows, cols] += received[g, :NB, :].astype(jnp.float32)

    @pl.when(step == pl.num_programs(0) - 1)
    def _():
        c = core_ref[0]
        for i in range(ATOM_ROWS):
            rows = slice(i * NB, i * NB + NB)
            for j in range(ATOM_COLS):
                cols = slice(j * NB, j * NB + NB)
                keep = pattern_ref[i * ATOM_COLS + j] > 0
                full[rows, cols] = jnp.where(keep, total[rows, cols], 0.0).astype(jnp.bfloat16)
        mine[...] = full[:, pl.ds(pl.multiple_of(c * 512, 512), 512)]
        theirs[...] = full[:, pl.ds(pl.multiple_of((1 - c) * 512, 512), 512)]


def hamiltonian_tile(pattern_tile, core_index, core, received):
    rows, cols = core.shape
    whole = lambda i, *_: (0, 0)
    half = pl.BlockSpec((rows, cols // 2), whole)
    half_shape = jax.ShapeDtypeStruct((rows, cols // 2), jnp.bfloat16)
    return pl.pallas_call(
        sum_kernel,
        grid_spec=pltpu.PrefetchScalarGridSpec(
            num_scalar_prefetch=2,
            grid=(DEVICES // SUM_GROUP,),
            in_specs=[
                pl.BlockSpec((rows, cols), whole),
                pl.BlockSpec((SUM_GROUP, NB + TAIL, NB), lambda i, *_: (i, 0, 0)),
            ],
            out_specs=[pl.BlockSpec((rows, cols), whole), half, half],
            scratch_shapes=[pltpu.VMEM((rows + NB, cols), jnp.float32)],
        ),
        out_shape=(jax.ShapeDtypeStruct((rows, cols), jnp.bfloat16), half_shape, half_shape),
        name="sum_blocks",
    )(pattern_tile, core_index, core, received)


def product_kernel(work, has_acc, place, *refs):
    count = len(work)
    pieces, tiles = refs[:count], refs[count : count + 4]
    acc = refs[count + 4] if has_acc else None
    out, columns, rows, column_sem, row_sem = refs[-5:]
    x, yh, yl, z, way = (place[i] for i in range(5))

    for k, (side, steps, turn) in enumerate(work):
        pltpu.make_async_copy(pieces[k], columns.at[k], column_sem.at[k]).start()
        block = ((x - way * steps) & 3) * 2 + ((yh + turn) & 1)
        plane = ((way if side == "own" else -way) * (z - block)) & 3
        far = ((block >> 2) + yl) & 1
        base = 0 if side == "own" else 2
        for which in range(2):

            @pl.when(far == which)
            def _(k=k, base=base, which=which, plane=plane):
                pltpu.make_async_copy(
                    tiles[base + which].at[plane], rows.at[k], row_sem.at[k]
                ).start()

    out[...] = acc[...] if has_acc else jnp.zeros_like(out)

    @pl.loop(0, count)
    def _(k):
        pltpu.make_async_copy(pieces[0], columns.at[k], column_sem.at[k]).wait()
        pltpu.make_async_copy(tiles[0].at[0], rows.at[k], row_sem.at[k]).wait()
        out[...] += jnp.dot(columns[k], rows[k], preferred_element_type=jnp.float32)


def multiply(place, acc, work, density):
    pieces = [w[3] for w in work]
    count = len(work)
    work = tuple(w[:3] for w in work)
    given = [] if acc is None else [acc]
    vmem = pl.BlockSpec(memory_space=pltpu.VMEM)
    return pl.pallas_call(
        functools.partial(product_kernel, work, acc is not None),
        in_specs=[SMEM] + [pl.BlockSpec(memory_space=pl.ANY)] * (count + 4) + [vmem] * len(given),
        out_specs=vmem,
        scratch_shapes=[
            pltpu.VMEM((count, 512, 512), jnp.bfloat16),
            pltpu.VMEM((count, 512, 1024), jnp.bfloat16),
            pltpu.SemaphoreType.DMA((count,)),
            pltpu.SemaphoreType.DMA((count,)),
        ],
        out_shape=jax.ShapeDtypeStruct((512, 1024), jnp.float32),
        name="product",
    )(place, *pieces, *density, *given)


def block_mask(values, pattern_tile, block_size):
    row_blocks, col_blocks = pattern_tile.shape
    shaped = values.reshape(row_blocks, block_size, col_blocks, block_size)
    selected = (pattern_tile > 0)[:, None, :, None]
    kept = jnp.where(selected, shaped, jnp.zeros((), values.dtype))
    return kept.reshape(row_blocks * block_size, col_blocks * block_size)


def turn(array, axis, step):
    axes = ("z", "c") if axis == "z" else ("c", "x")
    pairs = []
    for c in range(2):
        for i in range(4):
            to = (i + (step if c == 0 else -step)) % 4
            pairs.append((i * 2 + c, to * 2 + c) if axis == "z" else (c * 4 + i, c * 4 + to))
    return lax.ppermute(array, axes, pairs)


def steps(
    potential, basis_left, basis_right, core_matrix, density, pattern, pair_atoms, cube_offsets,
    live_count,
):
    x, yh = lax.axis_index("x"), lax.axis_index("yh")
    yl, z, c = lax.axis_index("yl"), lax.axis_index("z"), lax.axis_index("c")

    yz = jnp.concatenate([cube_offsets[:, 1], cube_offsets[:, 2]])
    prev_yz = shift(yz, ALL, 1)
    next_yz = shift(yz, ALL, -1)

    corner = (lax.axis_index(ROW) * ATOM_ROWS, lax.axis_index(COL) * ATOM_COLS)
    pattern_tile = lax.dynamic_slice(pattern, corner, (ATOM_ROWS, ATOM_COLS))
    d = block_mask(density, pattern_tile, NB)
    dy = shift(d, "yl", 1)
    d_1, d_2 = turn(d, "z", 1), turn(d, "z", -1)

    for_prev, for_next = cut_edges(prev_yz, next_yz, potential)
    high = shift(for_prev, ALL, -1)
    low = shift(for_next, ALL, 1)
    own = cut_own(yz, potential)
    extended = jnp.concatenate([low, own[0], own[1], high], axis=1)
    along = cube_offsets[:, :1]
    cubes = jnp.where(
        along == 0,
        extended[:, :384],
        jnp.where(along == 1, extended[:, 64:448], extended[:, 128:]),
    )

    ordinal = jnp.arange(ENTRIES, dtype=jnp.int32)
    first, second = pair_atoms[:, 0], pair_atoms[:, 1]
    owner = first // ATOM_ROWS * 8 + second // ATOM_COLS
    local = first % ATOM_ROWS * ATOM_COLS + second % ATOM_COLS
    mark = jnp.where(ordinal < live_count[0], local + 1, 0)
    outgoing = partial_blocks(owner, mark, cubes, basis_left, basis_right)
    received = lax.all_to_all(outgoing, ALL, 0, 0, tiled=True)

    d_o = turn(d_1, "z", 1)
    dy_1, dy_2 = turn(dy, "z", 1), turn(dy, "z", -1)
    near = jnp.stack([d, d_1, d_o, d_2])
    near_other = shift(near, "c", 1)
    core_index = c.reshape(1).astype(jnp.int32)
    hamiltonian, ha, hb = hamiltonian_tile(
        pattern_tile.reshape(-1), core_index, core_matrix, received
    )
    dy_o = turn(dy_1, "z", 1)
    away = jnp.stack([dy, dy_1, dy_o, dy_2])
    away_other = shift(away, "c", 1)
    tiles = (near, away, near_other, away_other)

    hb_1, hb_2 = turn(hb, "x", 1), turn(hb, "x", -1)
    ha_y = shift(ha, "yh", 1)
    ha_1, ha_2 = turn(ha, "x", 1), turn(ha, "x", -1)
    hb_y = shift(hb, "yh", 1)
    hb_o = turn(hb_1, "x", 1)
    hb_y1, hb_y2 = shift(hb_1, "yh", 1), shift(hb_2, "yh", 1)
    ha_y1, ha_y2 = turn(ha_y, "x", 1), turn(ha_y, "x", -1)
    ha_o = turn(ha_1, "x", 1)
    hb_yo = shift(hb_o, "yh", 1)
    ha_yo = turn(ha_y1, "x", 1)

    place = jnp.stack([x, yh, yl, z, 1 - 2 * c]).astype(jnp.int32)
    out = multiply(
        place,
        None,
        [
            ("own", 0, 0, ha),
            ("other", 0, 0, hb),
            ("other", 1, 0, hb_1),
            ("other", -1, 0, hb_2),
            ("own", 0, 1, ha_y),
            ("own", 1, 0, ha_1),
            ("own", -1, 0, ha_2),
            ("other", 0, 1, hb_y),
        ],
        tiles,
    )
    out = multiply(
        place,
        out,
        [
            ("other", 2, 0, hb_o),
            ("own", 1, 1, ha_y1),
            ("own", -1, 1, ha_y2),
            ("own", 2, 0, ha_o),
            ("other", 1, 1, hb_y1),
            ("other", -1, 1, hb_y2),
        ],
        tiles,
    )
    out = multiply(
        place, out, [("own", 2, 1, ha_yo), ("other", 2, 1, hb_yo)], tiles
    )
    return hamiltonian, out


def solution(mesh):
    split = Mesh(mesh.devices.reshape(2, 4, 2, 4, 2), ALL)
    placed = (
        P(ALL, None, None),
        P(ALL, None, None),
        P(ALL, None, None),
        P(ROW, COL),
        P(ROW, COL),
        P(),
        P(ALL, None),
        P(ALL, None),
        P(ALL),
    )
    return jax.shard_map(
        steps,
        mesh=split,
        in_specs=placed,
        out_specs=(P(ROW, COL), P(ROW, COL)),
        check_vma=False,
    )
```

profile of v0, /device:TPU:0, one launch (start us, length us, event | category | flops | bytes accessed | tf_op | source)
XLA Modules:
  0.0 236.8 jit_solution(1947577400909348608)
XLA Ops:
  0.6 0.8 broadcast_compare_fusion
  1.6 1.5 bitcast_select_fusion
  3.1 1.8 collective-permute-start.13
  4.9 1.9 collective-permute-start.10
  6.8 2.1 collective-permute-start.12
  8.9 0.8 slice_bitcast_fusion.3
  9.8 2.9 %collective-permute-start = (s32[128]{0:T(128)S(1)}, s32[128]{0:T(128)S(1)}, u32[]{:S(2)}, u32[]{:S(2)}) collective-permute-start(s32[128]{0:T(128)S(1)} %pad_add_fusion.own_ref), channel_id=1, source_target_pairs={{0,1},{1,2},{2,3},{3,4},{4,5},{5,6},{6,7},{7,8},{8,9},{9,10},{10,1... | collective-permute-start | bytes 1544 | tf_op jit(solution)/shard_map/ppermute | solution.py:28
  12.7 4.3 %collective-permute-start.1 = (s32[128]{0:T(128)S(1)}, s32[128]{0:T(128)S(1)}, u32[]{:S(2)}, u32[]{:S(2)}) collective-permute-start(s32[128]{0:T(128)S(1)} %pad_add_fusion.own_ref), channel_id=1, source_target_pairs={{0,127},{1,0},{2,1},{3,2},{4,3},{5,4},{6,5},{7,6},{8,7},{9,8},{10,... | collective-permute-start | bytes 1544 | tf_op jit(solution)/shard_map/ppermute | solution.py:28
  17.0 5.4 %cut_own.1 = f32[2,64,128]{2,1,0:T(8,128)} custom-call(s32[128]{0:T(128)} %copy-done.9, f32[4,512,512]{2,1,0:T(8,128)} %potential.3), custom_call_target="tpu_custom_call" | custom-call | tf_op jit(solution)/shard_map/cut_own/pallas_call | solution.py:117
  22.4 0.8 slice_bitcast_fusion.1
  23.2 4.9 %collective-permute-done.13 = bf16[512,1024]{1,0:T(8,128)(2,1)S(1)} collective-permute-done((bf16[512,1024]{1,0:T(8,128)(2,1)S(1)}, bf16[512,1024]{1,0:T(8,128)(2,1)S(1)}, u32[]{:S(2)}, u32[]{:S(2)}) %collective-permute-start.13) | collective-permute-done | bytes 1048608 | tf_op jit(solution)/shard_map/ppermute | solution.py:28
  28.1 2.1 collective-permute-start.14
  30.2 0.7 compare_bitcast_fusion.1
  32.6 5.4 %cut_edges.1 = (f32[64,128]{1,0:T(8,128)}, f32[64,128]{1,0:T(8,128)}) custom-call(s32[128]{0:T(128)} %copy-done.8, s32[128]{0:T(128)} %copy-done.10, f32[4,512,512]{2,1,0:T(8,128)} %potential.3), custom_call_target="tpu_custom_call" | custom-call | tf_op jit(solution)/shard_map/cut_edges/pallas_call | solution.py:107
  38.0 3.3 %collective-permute-start.2 = (f32[64,128]{1,0:T(8,128)}, f32[64,128]{1,0:T(8,128)S(1)}, u32[]{:S(2)}, u32[]{:S(2)}) collective-permute-start(f32[64,128]{1,0:T(8,128)} %get-tuple-element.7), channel_id=1, source_target_pairs={{0,1},{1,2},{2,3},{3,4},{4,5},{5,6},{6,7},{7,8},{8,9},{9,10},{10,1... | collective-permute-start | bytes 98312 | tf_op jit(solution)/shard_map/ppermute | solution.py:28
  41.3 4.0 %collective-permute-start.3 = (f32[64,128]{1,0:T(8,128)}, f32[64,128]{1,0:T(8,128)S(1)}, u32[]{:S(2)}, u32[]{:S(2)}) collective-permute-start(f32[64,128]{1,0:T(8,128)} %get-tuple-element.8), channel_id=1, source_target_pairs={{0,127},{1,0},{2,1},{3,2},{4,3},{5,4},{6,5},{7,6},{8,7},{9,8},{10,... | collective-permute-start | bytes 98312 | tf_op jit(solution)/shard_map/ppermute | solution.py:28
  45.8 1.0 collective-permute-start.11
  47.4 0.8 fusion.1.cubes
  48.2 11.1 %partial_blocks.1 = bf16[128,136,128]{2,1,0:T(8,128)(2,1)} custom-call(s32[64]{0:T(128)} %get-tuple-element.21.owner_ref, s32[64]{0:T(128)} %get-tuple-element.20.mark_ref, f32[64,384]{1,0:T(8,128)} %fusion.1.cubes, bf16[64,128,384]{2,1,0:T(8,128)(2,1)} %left.1, bf16[64,128,384]{2,1,0:T(8,128)(2,1)} %right.1), custom_call_target="tpu_custom_call" | custom-call | tf_op jit(solution)/shard_map/partial_blocks/pallas_call | solution.py:153
  59.3 9.9 %all-to-all-start = ((bf16[128,136,128]{2,1,0:T(8,128)(2,1)}), bf16[128,136,128]{2,1,0:T(8,128)(2,1)}, u32[]{:S(2)}, u32[]{:S(2)}) async-start(bf16[128,136,128]{2,1,0:T(8,128)(2,1)} %partial_blocks.1), calls=%async_computation | async-start | bytes 8912896 | tf_op jit(solution)/shard_map/all_to_all | solution.py:329
  69.2 2.8 %collective-permute-start.16 = (bf16[512,1024]{1,0:T(8,128)(2,1)S(1)}, bf16[512,1024]{1,0:T(8,128)(2,1)S(1)}, u32[]{:S(2)}, u32[]{:S(2)}) collective-permute-start(bf16[512,1024]{1,0:T(8,128)(2,1)S(1)} %collective-permute-done.13), channel_id=1, source_target_pairs={{0,48},{16,0},{32,16},{48,32},{8,24},{24,40},{40,56},{56,8},{1,49}... | collective-permute-start | bytes 3145736 | tf_op jit(solution)/shard_map/ppermute | solution.py:291
  72.1 3.5 %pad_maximum_fusion.refs_8_.refs_6_.refs_2_ = bf16[4,512,1024]{2,1,0:T(8,128)(2,1)} fusion(bf16[1,512,1024]{2,1,0:T(8,128)(2,1)} %bitcast.18, bf16[1,512,1024]{2,1,0:T(8,128)(2,1)} %bitcast.17, bf16[1,512,1024]{2,1,0:T(8,128)(2,1)S(1)} %bitcast.69, bf16[1,512,1024]{2,1,0:T(8,128)(2,1)S(1)} %bitcast.66), kind=kLoop, calls=%fused_computation | loop fusion | flops 6291456 | bytes 8388608 | tf_op jit(solution)/shard_map/stack | solution.py:333
  75.7 64.9 %collective-permute-done.16 = bf16[512,1024]{1,0:T(8,128)(2,1)S(1)} collective-permute-done((bf16[512,1024]{1,0:T(8,128)(2,1)S(1)}, bf16[512,1024]{1,0:T(8,128)(2,1)S(1)}, u32[]{:S(2)}, u32[]{:S(2)}) %collective-permute-start.16) | collective-permute-done | bytes 1048608 | tf_op jit(solution)/shard_map/ppermute | solution.py:291
  140.6 1.8 collective-permute-done.15
  142.3 3.3 %pad_maximum_fusion.1.refs_9_.refs_7_.refs_3_ = bf16[4,512,1024]{2,1,0:T(8,128)(2,1)} fusion(bf16[1,512,1024]{2,1,0:T(8,128)(2,1)S(1)} %bitcast.70, bf16[1,512,1024]{2,1,0:T(8,128)(2,1)S(1)} %bitcast.71, bf16[1,512,1024]{2,1,0:T(8,128)(2,1)} %bitcast.20, bf16[1,512,1024]{2,1,0:T(8,128)(2,1)S(1)} %bitcast.68), kind=kLoop, calls=%fused_computation.1 | loop fusion | flops 6291456 | bytes 8388608 | tf_op jit(solution)/shard_map/stack | solution.py:340
  146.2 8.9 %sum_blocks.1 = (bf16[512,1024]{1,0:T(8,128)(2,1)}, bf16[512,512]{1,0:T(8,128)(2,1)}, bf16[512,512]{1,0:T(8,128)(2,1)}) custom-call(s32[32]{0:T(128)} %reshape.20.pattern_ref, s32[1]{0:T(128)} %bitcast.core_ref, bf16[512,1024]{1,0:T(8,128)(2,1)} %core.1, bf16[128,136,128]{2,1,0:T(8,128)(2,1)} %all-to-all-done.received), custom_call_target="tpu_custom_call" | custom-call | tf_op jit(solution)/shard_map/sum_blocks/pallas_call | solution.py:208
  155.1 2.8 %collective-permute-start.4 = (bf16[512,512]{1,0:T(8,128)(2,1)}, bf16[512,512]{1,0:T(8,128)(2,1)S(1)}, u32[]{:S(2)}, u32[]{:S(2)}) collective-permute-start(bf16[512,512]{1,0:T(8,128)(2,1)} %get-tuple-element.10.refs_0_), channel_id=1, source_target_pairs={{0,1},{1,0},{2,3},{3,2},{4,5},{5,4},{6,7},{7,6},{8,9},{9,8},{10,11... | collective-permute-start | bytes 1572872 | tf_op jit(solution)/shard_map/ppermute | solution.py:28
  157.9 1.5 collective-permute-start.7
  159.4 1.5 collective-permute-start.20
  160.9 10.3 %collective-permute-done.4.refs_4_ = bf16[512,512]{1,0:T(8,128)(2,1)S(1)} collective-permute-done((bf16[512,512]{1,0:T(8,128)(2,1)}, bf16[512,512]{1,0:T(8,128)(2,1)S(1)}, u32[]{:S(2)}, u32[]{:S(2)}) %collective-permute-start.4) | collective-permute-done | bytes 524320 | tf_op jit(solution)/shard_map/ppermute | solution.py:28
  171.2 2.7 %collective-permute-start.23 = (bf16[512,512]{1,0:T(8,128)(2,1)}, bf16[512,512]{1,0:T(8,128)(2,1)S(1)}, u32[]{:S(2)}, u32[]{:S(2)}) collective-permute-start(bf16[512,512]{1,0:T(8,128)(2,1)} %get-tuple-element.11.refs_1_), channel_id=1, source_target_pairs={{0,6},{2,0},{4,2},{6,4},{8,10},{10,12},{12,14},{14,8},{1,7},{3,1},... | collective-permute-start | bytes 1572872 | tf_op jit(solution)/shard_map/ppermute | solution.py:291
  173.9 0.9 collective-permute-start.25
  174.8 2.7 %collective-permute-start.26 = (bf16[512,512]{1,0:T(8,128)(2,1)}, bf16[512,512]{1,0:T(8,128)(2,1)S(1)}, u32[]{:S(2)}, u32[]{:S(2)}) collective-permute-start(bf16[512,512]{1,0:T(8,128)(2,1)} %get-tuple-element.11.refs_1_), channel_id=1, source_target_pairs={{0,1},{1,0},{2,3},{3,2},{4,5},{5,4},{6,7},{7,6},{8,9},{9,8},{10,11... | collective-permute-start | bytes 1572872 | tf_op jit(solution)/shard_map/ppermute | solution.py:28
  177.5 3.4 %collective-permute-done.23.refs_3_ = bf16[512,512]{1,0:T(8,128)(2,1)S(1)} collective-permute-done((bf16[512,512]{1,0:T(8,128)(2,1)}, bf16[512,512]{1,0:T(8,128)(2,1)S(1)}, u32[]{:S(2)}, u32[]{:S(2)}) %collective-permute-start.23) | collective-permute-done | bytes 524320 | tf_op jit(solution)/shard_map/ppermute | solution.py:291
  180.9 1.2 collective-permute-start.5
  182.1 8.7 %collective-permute-done.25.refs_6_ = bf16[512,512]{1,0:T(8,128)(2,1)S(1)} collective-permute-done((bf16[512,512]{1,0:T(8,128)(2,1)}, bf16[512,512]{1,0:T(8,128)(2,1)S(1)}, u32[]{:S(2)}, u32[]{:S(2)}) %collective-permute-start.25) | collective-permute-done | bytes 524320 | tf_op jit(solution)/shard_map/ppermute | solution.py:291
  190.8 1.1 collective-permute-start.8
  191.9 2.6 %collective-permute-start.19 = (bf16[512,512]{1,0:T(8,128)(2,1)S(1)}, bf16[512,512]{1,0:T(8,128)(2,1)S(1)}, u32[]{:S(2)}, u32[]{:S(2)}) collective-permute-start(bf16[512,512]{1,0:T(8,128)(2,1)S(1)} %collective-permute-done.4.refs_4_), channel_id=1, source_target_pairs={{0,6},{2,0},{4,2},{6,4},{8,10},{10,12},{12,14},{14,8},{1,7},{3,1},... | collective-permute-start | bytes 1572872 | tf_op jit(solution)/shard_map/ppermute | solution.py:291
  194.4 2.9 %collective-permute-start.22 = (bf16[512,512]{1,0:T(8,128)(2,1)S(1)}, bf16[512,512]{1,0:T(8,128)(2,1)}, u32[]{:S(2)}, u32[]{:S(2)}) collective-permute-start(bf16[512,512]{1,0:T(8,128)(2,1)S(1)} %collective-permute-done.7.refs_2_), channel_id=1, source_target_pairs={{0,1},{1,0},{2,3},{3,2},{4,5},{5,4},{6,7},{7,6},{8,9},{9,8},{10,11... | collective-permute-start | bytes 1572872 | tf_op jit(solution)/shard_map/ppermute | solution.py:28
  197.4 5.8 %collective-permute-done.8.refs_0_ = bf16[512,512]{1,0:T(8,128)(2,1)} collective-permute-done((bf16[512,512]{1,0:T(8,128)(2,1)S(1)}, bf16[512,512]{1,0:T(8,128)(2,1)}, u32[]{:S(2)}, u32[]{:S(2)}) %collective-permute-start.8) | collective-permute-done | bytes 524320 | tf_op jit(solution)/shard_map/ppermute | solution.py:291
  203.6 0.8 copy-done.6
  204.4 2.7 %collective-permute-start.24 = (bf16[512,512]{1,0:T(8,128)(2,1)S(1)}, bf16[512,512]{1,0:T(8,128)(2,1)}, u32[]{:S(2)}, u32[]{:S(2)}) collective-permute-start(bf16[512,512]{1,0:T(8,128)(2,1)S(1)} %collective-permute-done.23.refs_3_), channel_id=1, source_target_pairs={{0,1},{1,0},{2,3},{3,2},{4,5},{5,4},{6,7},{7,6},{8,9},{9,8},{10,11... | collective-permute-start | bytes 1572872 | tf_op jit(solution)/shard_map/ppermute | solution.py:28
  207.1 2.4 collective-permute-start.6
  209.5 0.6 collective-permute-start.9
  210.1 0.7 stack.50.place
  210.8 10.2 %product.3.refs_10_ = f32[512,1024]{1,0:T(8,128)} custom-call(s32[5]{0:T(128)} %stack.50.place, bf16[512,512]{1,0:T(8,128)(2,1)} %get-tuple-element.10.refs_0_, bf16[512,512]{1,0:T(8,128)(2,1)} %get-tuple-element.11.refs_1_, bf16[512,512]{1,0:T(8,128)(2,1)} %copy-done.1, bf16[512,512]{1,0:T(8,128)(2,1)} %copy-done.3, bf16[512,512]{1,0:T(8,128)(2,1)} %copy-done, ...), custom_call_target="tpu_custom_call" | custom-call | tf_op jit(solution)/shard_map/product/pallas_call | solution.py:261
  221.0 9.4 %product.4.refs_6_ = f32[512,1024]{1,0:T(8,128)} custom-call(s32[5]{0:T(128)} %stack.50.place, bf16[512,512]{1,0:T(8,128)(2,1)} %collective-permute-done.8.refs_0_, bf16[512,512]{1,0:T(8,128)(2,1)} %collective-permute-done.5.refs_1_, bf16[512,512]{1,0:T(8,128)(2,1)} %copy-done.6, bf16[512,512]{1,0:T(8,128)(2,1)} %collective-permute-done.21.refs_3_, ...), custom_call_target="tpu_custom_call" | custom-call | tf_op jit(solution)/shard_map/product/pallas_call | solution.py:261
  230.9 5.7 %product.5 = f32[512,1024]{1,0:T(8,128)} custom-call(s32[5]{0:T(128)} %stack.50.place, bf16[512,512]{1,0:T(8,128)(2,1)} %collective-permute-done.6.refs_0_, bf16[512,512]{1,0:T(8,128)(2,1)} %collective-permute-done.9.refs_1_, bf16[4,512,1024]{2,1,0:T(8,128)(2,1)} %pad_maximum_fusion.refs_8_.refs_6_.refs_2_, ...), custom_call_target="tpu_custom_call" | custom-call | tf_op jit(solution)/shard_map/product/pallas_call | solution.py:261
  (50 shorter events, 4.2 us)
Async XLA Ops:
  3.1 24.9 %collective-permute-start.13 = (bf16[512,1024]{1,0:T(8,128)(2,1)S(1)}, bf16[512,1024]{1,0:T(8,128)(2,1)S(1)}, u32[]{:S(2)}, u32[]{:S(2)}) collective-permute-start(bf16[512,1024]{1,0:T(8,128)(2,1)S(1)} %bitcast_select_fusion), channel_id=1, source_target_pairs={{0,64},{64,0},{1,65},{65,1},{2,66},{66,2},{3,67},{67,3},{4,68},{68... | collective-permute-start | bytes 3145736 | tf_op jit(solution)/shard_map/ppermute | solution.py:28
  4.9 40.9 %collective-permute-start.10 = (bf16[512,1024]{1,0:T(8,128)(2,1)S(1)}, bf16[512,1024]{1,0:T(8,128)(2,1)S(1)}, u32[]{:S(2)}, u32[]{:S(2)}) collective-permute-start(bf16[512,1024]{1,0:T(8,128)(2,1)S(1)} %bitcast_select_fusion), channel_id=1, source_target_pairs={{0,16},{16,32},{32,48},{48,0},{8,56},{24,8},{40,24},{56,40},{1,17}... | collective-permute-start | bytes 3145736 | tf_op jit(solution)/shard_map/ppermute | solution.py:291
  6.8 65.3 %collective-permute-start.12 = (bf16[512,1024]{1,0:T(8,128)(2,1)S(1)}, bf16[512,1024]{1,0:T(8,128)(2,1)}, u32[]{:S(2)}, u32[]{:S(2)}) collective-permute-start(bf16[512,1024]{1,0:T(8,128)(2,1)S(1)} %bitcast_select_fusion), channel_id=1, source_target_pairs={{0,48},{16,0},{32,16},{48,32},{8,24},{24,40},{40,56},{56,8},{1,49}... | collective-permute-start | bytes 3145736 | tf_op jit(solution)/shard_map/ppermute | solution.py:291
  9.8 7.2 %copy-start.9 = (s32[128]{0:T(128)}, s32[128]{0:T(128)S(1)}, u32[]{:S(2)}) copy-start(s32[128]{0:T(128)S(1)} %pad_add_fusion.own_ref) | copy-start | bytes 1540
  9.8 35.5 %copy-start.7 = (s32[64,2]{0,1:T(2,128)S(1)}, s32[64,2]{0,1:T(2,128)}, u32[]{:S(2)}) copy-start(s32[64,2]{0,1:T(2,128)} %param.15) | copy-start | bytes 1540
  9.8 21.7 %collective-permute-start = (s32[128]{0:T(128)S(1)}, s32[128]{0:T(128)S(1)}, u32[]{:S(2)}, u32[]{:S(2)}) collective-permute-start(s32[128]{0:T(128)S(1)} %pad_add_fusion.own_ref), channel_id=1, source_target_pairs={{0,1},{1,2},{2,3},{3,4},{4,5},{5,6},{6,7},{7,8},{8,9},{9,10},{10,1... | collective-permute-start | bytes 1544 | tf_op jit(solution)/shard_map/ppermute | solution.py:28
  12.7 18.8 %collective-permute-start.1 = (s32[128]{0:T(128)S(1)}, s32[128]{0:T(128)S(1)}, u32[]{:S(2)}, u32[]{:S(2)}) collective-permute-start(s32[128]{0:T(128)S(1)} %pad_add_fusion.own_ref), channel_id=1, source_target_pairs={{0,127},{1,0},{2,1},{3,2},{4,3},{5,4},{6,5},{7,6},{8,7},{9,8},{10,... | collective-permute-start | bytes 1544 | tf_op jit(solution)/shard_map/ppermute | solution.py:28
  28.1 44.0 %collective-permute-start.14 = (bf16[512,1024]{1,0:T(8,128)(2,1)S(1)}, bf16[512,1024]{1,0:T(8,128)(2,1)}, u32[]{:S(2)}, u32[]{:S(2)}) collective-permute-start(bf16[512,1024]{1,0:T(8,128)(2,1)S(1)} %collective-permute-done.13), channel_id=1, source_target_pairs={{0,16},{16,32},{32,48},{48,0},{8,56},{24,8},{40,24},{56,40},{1,17}... | collective-permute-start | bytes 3145736 | tf_op jit(solution)/shard_map/ppermute | solution.py:291
  31.5 0.6 copy-start.8
  32.1 0.5 copy-start.10
  38.0 9.4 %collective-permute-start.2 = (f32[64,128]{1,0:T(8,128)}, f32[64,128]{1,0:T(8,128)S(1)}, u32[]{:S(2)}, u32[]{:S(2)}) collective-permute-start(f32[64,128]{1,0:T(8,128)} %get-tuple-element.7), channel_id=1, source_target_pairs={{0,1},{1,2},{2,3},{3,4},{4,5},{5,6},{6,7},{7,8},{8,9},{9,10},{10,1... | collective-permute-start | bytes 98312 | tf_op jit(solution)/shard_map/ppermute | solution.py:28
  41.3 6.2 %collective-permute-start.3 = (f32[64,128]{1,0:T(8,128)}, f32[64,128]{1,0:T(8,128)S(1)}, u32[]{:S(2)}, u32[]{:S(2)}) collective-permute-start(f32[64,128]{1,0:T(8,128)} %get-tuple-element.8), channel_id=1, source_target_pairs={{0,127},{1,0},{2,1},{3,2},{4,3},{5,4},{6,5},{7,6},{8,7},{9,8},{10,... | collective-permute-start | bytes 98312 | tf_op jit(solution)/shard_map/ppermute | solution.py:28
  45.8 26.3 %collective-permute-start.11 = (bf16[512,1024]{1,0:T(8,128)(2,1)S(1)}, bf16[512,1024]{1,0:T(8,128)(2,1)}, u32[]{:S(2)}, u32[]{:S(2)}) collective-permute-start(bf16[512,1024]{1,0:T(8,128)(2,1)S(1)} %collective-permute-done.10), channel_id=1, source_target_pairs={{0,16},{16,32},{32,48},{48,0},{8,56},{24,8},{40,24},{56,40},{1,17}... | collective-permute-start | bytes 3145736 | tf_op jit(solution)/shard_map/ppermute | solution.py:291
  59.3 86.9 %all-to-all-start = ((bf16[128,136,128]{2,1,0:T(8,128)(2,1)}), bf16[128,136,128]{2,1,0:T(8,128)(2,1)}, u32[]{:S(2)}, u32[]{:S(2)}) async-start(bf16[128,136,128]{2,1,0:T(8,128)(2,1)} %partial_blocks.1), calls=%async_computation | async-start | bytes 8912896 | tf_op jit(solution)/shard_map/all_to_all | solution.py:329
  69.2 71.3 %collective-permute-start.16 = (bf16[512,1024]{1,0:T(8,128)(2,1)S(1)}, bf16[512,1024]{1,0:T(8,128)(2,1)S(1)}, u32[]{:S(2)}, u32[]{:S(2)}) collective-permute-start(bf16[512,1024]{1,0:T(8,128)(2,1)S(1)} %collective-permute-done.13), channel_id=1, source_target_pairs={{0,48},{16,0},{32,16},{48,32},{8,24},{24,40},{40,56},{56,8},{1,49}... | collective-permute-start | bytes 3145736 | tf_op jit(solution)/shard_map/ppermute | solution.py:291
  72.1 70.2 %collective-permute-start.15 = (bf16[512,1024]{1,0:T(8,128)(2,1)}, bf16[512,1024]{1,0:T(8,128)(2,1)S(1)}, u32[]{:S(2)}, u32[]{:S(2)}) collective-permute-start(bf16[512,1024]{1,0:T(8,128)(2,1)} %collective-permute-done.14), channel_id=1, source_target_pairs={{0,16},{16,32},{32,48},{48,0},{8,56},{24,8},{40,24},{56,40},{1,17}... | collective-permute-start | bytes 3145736 | tf_op jit(solution)/shard_map/ppermute | solution.py:291
  75.6 131.5 %collective-permute-start.17 = (bf16[4,512,1024]{2,1,0:T(8,128)(2,1)}, bf16[4,512,1024]{2,1,0:T(8,128)(2,1)}, u32[]{:S(2)}, u32[]{:S(2)}) collective-permute-start(bf16[4,512,1024]{2,1,0:T(8,128)(2,1)} %pad_maximum_fusion.refs_8_.refs_6_.refs_2_), channel_id=1, source_target_pairs={{0,8},{8,0},{1,9},{9,1},{2,10},{10,2},{3,11},{11,3},{4,12},{12,4},... | collective-permute-start | bytes 12582920 | tf_op jit(solution)/shard_map/ppermute | solution.py:28
  145.6 63.9 %collective-permute-start.18 = (bf16[4,512,1024]{2,1,0:T(8,128)(2,1)}, bf16[4,512,1024]{2,1,0:T(8,128)(2,1)}, u32[]{:S(2)}, u32[]{:S(2)}) collective-permute-start(bf16[4,512,1024]{2,1,0:T(8,128)(2,1)} %pad_maximum_fusion.1.refs_9_.refs_7_.refs_3_), channel_id=1, source_target_pairs={{0,8},{8,0},{1,9},{9,1},{2,10},{10,2},{3,11},{11,3},{4,12},{12,4},... | collective-permute-start | bytes 12582920 | tf_op jit(solution)/shard_map/ppermute | solution.py:28
  155.1 16.1 %collective-permute-start.4 = (bf16[512,512]{1,0:T(8,128)(2,1)}, bf16[512,512]{1,0:T(8,128)(2,1)S(1)}, u32[]{:S(2)}, u32[]{:S(2)}) collective-permute-start(bf16[512,512]{1,0:T(8,128)(2,1)} %get-tuple-element.10.refs_0_), channel_id=1, source_target_pairs={{0,1},{1,0},{2,3},{3,2},{4,5},{5,4},{6,7},{7,6},{8,9},{9,8},{10,11... | collective-permute-start | bytes 1572872 | tf_op jit(solution)/shard_map/ppermute | solution.py:28
  157.9 16.0 %collective-permute-start.7 = (bf16[512,512]{1,0:T(8,128)(2,1)}, bf16[512,512]{1,0:T(8,128)(2,1)S(1)}, u32[]{:S(2)}, u32[]{:S(2)}) collective-permute-start(bf16[512,512]{1,0:T(8,128)(2,1)} %get-tuple-element.11.refs_1_), channel_id=1, source_target_pairs={{0,2},{2,4},{4,6},{6,0},{8,14},{10,8},{12,10},{14,12},{1,3},{3,5},... | collective-permute-start | bytes 1572872 | tf_op jit(solution)/shard_map/ppermute | solution.py:291
  159.4 15.4 %collective-permute-start.20 = (bf16[512,512]{1,0:T(8,128)(2,1)}, bf16[512,512]{1,0:T(8,128)(2,1)S(1)}, u32[]{:S(2)}, u32[]{:S(2)}) collective-permute-start(bf16[512,512]{1,0:T(8,128)(2,1)} %get-tuple-element.10.refs_0_), channel_id=1, source_target_pairs={{0,2},{2,4},{4,6},{6,0},{8,14},{10,8},{12,10},{14,12},{1,3},{3,5},... | collective-permute-start | bytes 1572872 | tf_op jit(solution)/shard_map/ppermute | solution.py:291
  171.2 39.6 %copy-start = (bf16[512,512]{1,0:T(8,128)(2,1)}, bf16[512,512]{1,0:T(8,128)(2,1)S(1)}, u32[]{:S(2)}) copy-start(bf16[512,512]{1,0:T(8,128)(2,1)S(1)} %collective-permute-done.4.refs_4_) | copy-start | bytes 1572868
  171.2 9.7 %collective-permute-start.23 = (bf16[512,512]{1,0:T(8,128)(2,1)}, bf16[512,512]{1,0:T(8,128)(2,1)S(1)}, u32[]{:S(2)}, u32[]{:S(2)}) collective-permute-start(bf16[512,512]{1,0:T(8,128)(2,1)} %get-tuple-element.11.refs_1_), channel_id=1, source_target_pairs={{0,6},{2,0},{4,2},{6,4},{8,10},{10,12},{12,14},{14,8},{1,7},{3,1},... | collective-permute-start | bytes 1572872 | tf_op jit(solution)/shard_map/ppermute | solution.py:291
  173.9 36.9 %copy-start.1 = (bf16[512,512]{1,0:T(8,128)(2,1)}, bf16[512,512]{1,0:T(8,128)(2,1)S(1)}, u32[]{:S(2)}) copy-start(bf16[512,512]{1,0:T(8,128)(2,1)S(1)} %collective-permute-done.7.refs_2_) | copy-start | bytes 1572868
  173.9 16.9 %collective-permute-start.25 = (bf16[512,512]{1,0:T(8,128)(2,1)}, bf16[512,512]{1,0:T(8,128)(2,1)S(1)}, u32[]{:S(2)}, u32[]{:S(2)}) collective-permute-start(bf16[512,512]{1,0:T(8,128)(2,1)} %get-tuple-element.10.refs_0_), channel_id=1, source_target_pairs={{0,6},{2,0},{4,2},{6,4},{8,10},{10,12},{12,14},{14,8},{1,7},{3,1},... | collective-permute-start | bytes 1572872 | tf_op jit(solution)/shard_map/ppermute | solution.py:291
  174.8 36.0 %copy-start.2 = (bf16[512,512]{1,0:T(8,128)(2,1)}, bf16[512,512]{1,0:T(8,128)(2,1)S(1)}, u32[]{:S(2)}) copy-start(bf16[512,512]{1,0:T(8,128)(2,1)S(1)} %collective-permute-done.20.refs_5_) | copy-start | bytes 1572868
  174.8 17.1 %collective-permute-start.26 = (bf16[512,512]{1,0:T(8,128)(2,1)}, bf16[512,512]{1,0:T(8,128)(2,1)S(1)}, u32[]{:S(2)}, u32[]{:S(2)}) collective-permute-start(bf16[512,512]{1,0:T(8,128)(2,1)} %get-tuple-element.11.refs_1_), channel_id=1, source_target_pairs={{0,1},{1,0},{2,3},{3,2},{4,5},{5,4},{6,7},{7,6},{8,9},{9,8},{10,11... | collective-permute-start | bytes 1572872 | tf_op jit(solution)/shard_map/ppermute | solution.py:28
  180.9 29.9 %copy-start.3 = (bf16[512,512]{1,0:T(8,128)(2,1)}, bf16[512,512]{1,0:T(8,128)(2,1)S(1)}, u32[]{:S(2)}) copy-start(bf16[512,512]{1,0:T(8,128)(2,1)S(1)} %collective-permute-done.23.refs_3_) | copy-start | bytes 1572868
  180.9 13.5 %collective-permute-start.5 = (bf16[512,512]{1,0:T(8,128)(2,1)S(1)}, bf16[512,512]{1,0:T(8,128)(2,1)}, u32[]{:S(2)}, u32[]{:S(2)}) collective-permute-start(bf16[512,512]{1,0:T(8,128)(2,1)S(1)} %collective-permute-done.4.refs_4_), channel_id=1, source_target_pairs={{0,2},{2,4},{4,6},{6,0},{8,14},{10,8},{12,10},{14,12},{1,3},{3,5},... | collective-permute-start | bytes 1572872 | tf_op jit(solution)/shard_map/ppermute | solution.py:291
  190.8 20.0 %copy-start.4 = (bf16[512,512]{1,0:T(8,128)(2,1)}, bf16[512,512]{1,0:T(8,128)(2,1)S(1)}, u32[]{:S(2)}) copy-start(bf16[512,512]{1,0:T(8,128)(2,1)S(1)} %collective-permute-done.25.refs_6_) | copy-start | bytes 1572868
  190.8 12.4 %collective-permute-start.8 = (bf16[512,512]{1,0:T(8,128)(2,1)S(1)}, bf16[512,512]{1,0:T(8,128)(2,1)}, u32[]{:S(2)}, u32[]{:S(2)}) collective-permute-start(bf16[512,512]{1,0:T(8,128)(2,1)S(1)} %collective-permute-done.7.refs_2_), channel_id=1, source_target_pairs={{0,2},{2,4},{4,6},{6,0},{8,14},{10,8},{12,10},{14,12},{1,3},{3,5},... | collective-permute-start | bytes 1572872 | tf_op jit(solution)/shard_map/ppermute | solution.py:291
  191.9 18.9 %copy-start.5 = (bf16[512,512]{1,0:T(8,128)(2,1)}, bf16[512,512]{1,0:T(8,128)(2,1)S(1)}, u32[]{:S(2)}) copy-start(bf16[512,512]{1,0:T(8,128)(2,1)S(1)} %collective-permute-done.26.refs_7_) | copy-start | bytes 1572868
  191.9 11.7 %collective-permute-start.19 = (bf16[512,512]{1,0:T(8,128)(2,1)S(1)}, bf16[512,512]{1,0:T(8,128)(2,1)S(1)}, u32[]{:S(2)}, u32[]{:S(2)}) collective-permute-start(bf16[512,512]{1,0:T(8,128)(2,1)S(1)} %collective-permute-done.4.refs_4_), channel_id=1, source_target_pairs={{0,6},{2,0},{4,2},{6,4},{8,10},{10,12},{12,14},{14,8},{1,7},{3,1},... | collective-permute-start | bytes 1572872 | tf_op jit(solution)/shard_map/ppermute | solution.py:291
  194.4 26.5 %collective-permute-start.22 = (bf16[512,512]{1,0:T(8,128)(2,1)S(1)}, bf16[512,512]{1,0:T(8,128)(2,1)}, u32[]{:S(2)}, u32[]{:S(2)}) collective-permute-start(bf16[512,512]{1,0:T(8,128)(2,1)S(1)} %collective-permute-done.7.refs_2_), channel_id=1, source_target_pairs={{0,1},{1,0},{2,3},{3,2},{4,5},{5,4},{6,7},{7,6},{8,9},{9,8},{10,11... | collective-permute-start | bytes 1572872 | tf_op jit(solution)/shard_map/ppermute | solution.py:28
  203.2 17.8 %collective-permute-start.21 = (bf16[512,512]{1,0:T(8,128)(2,1)S(1)}, bf16[512,512]{1,0:T(8,128)(2,1)}, u32[]{:S(2)}, u32[]{:S(2)}) collective-permute-start(bf16[512,512]{1,0:T(8,128)(2,1)S(1)} %collective-permute-done.20.refs_5_), channel_id=1, source_target_pairs={{0,2},{2,4},{4,6},{6,0},{8,14},{10,8},{12,10},{14,12},{1,3},{3,5},... | collective-permute-start | bytes 1572872 | tf_op jit(solution)/shard_map/ppermute | solution.py:291
  203.6 0.8 copy-start.6
  204.4 16.6 %collective-permute-start.24 = (bf16[512,512]{1,0:T(8,128)(2,1)S(1)}, bf16[512,512]{1,0:T(8,128)(2,1)}, u32[]{:S(2)}, u32[]{:S(2)}) collective-permute-start(bf16[512,512]{1,0:T(8,128)(2,1)S(1)} %collective-permute-done.23.refs_3_), channel_id=1, source_target_pairs={{0,1},{1,0},{2,3},{3,2},{4,5},{5,4},{6,7},{7,6},{8,9},{9,8},{10,11... | collective-permute-start | bytes 1572872 | tf_op jit(solution)/shard_map/ppermute | solution.py:28
  207.1 23.2 %collective-permute-start.6 = (bf16[512,512]{1,0:T(8,128)(2,1)}, bf16[512,512]{1,0:T(8,128)(2,1)}, u32[]{:S(2)}, u32[]{:S(2)}) collective-permute-start(bf16[512,512]{1,0:T(8,128)(2,1)} %collective-permute-done.5.refs_1_), channel_id=1, source_target_pairs={{0,2},{2,4},{4,6},{6,0},{8,14},{10,8},{12,10},{14,12},{1,3},{3,5},... | collective-permute-start | bytes 1572872 | tf_op jit(solution)/shard_map/ppermute | solution.py:291
  209.5 21.4 %collective-permute-start.9 = (bf16[512,512]{1,0:T(8,128)(2,1)}, bf16[512,512]{1,0:T(8,128)(2,1)}, u32[]{:S(2)}, u32[]{:S(2)}) collective-permute-start(bf16[512,512]{1,0:T(8,128)(2,1)} %collective-permute-done.8.refs_0_), channel_id=1, source_target_pairs={{0,1},{1,0},{2,3},{3,2},{4,5},{5,4},{6,7},{7,6},{8,9},{9,8},{10,11... | collective-permute-start | bytes 1572872 | tf_op jit(solution)/shard_map/ppermute | solution.py:28
where the time goes:
time: 238 us; the launch traced here: 237 us
  waiting for transfers between devices  101 us (42%)
  starting transfers between devices  61.9 us (26%)
  Pallas kernels  56 us (24%)
  other arithmetic  11.2 us (5%)
  local copies, waits for them, and re-layouts  4.93 us (2%)
    ppermute x15, waiting for transfers between devices, turn(): return lax.ppermute(array, axes, pairs)  84.8 us
    ppermute x12, starting transfers between devices, shift(): lax.ppermute(array, axis, [(i, (i + step) % size) for i in range(size)])  28 us
    pallas_call x3, Pallas kernels, multiply(): pl.pallas_call(functools.partial(product_kernel, work, acc is not None),...  25.3 us
    ppermute x15, starting transfers between devices, turn(): return lax.ppermute(array, axes, pairs)  24 us
    ppermute x12, waiting for transfers between devices, shift(): lax.ppermute(array, axis, [(i, (i + step) % size) for i in range(size)])  16.3 us
    pallas_call x1, Pallas kernels, partial_blocks(): pl.pallas_call(partial_kernel, grid_spec=pltpu.PrefetchScalarGridSpec(num...  11.1 us
    all_to_all x1, starting transfers between devices, steps(): received = lax.all_to_all(outgoing, ALL, 0, 0, tiled=True)  9.91 us
    pallas_call x1, Pallas kernels, hamiltonian_tile(): pl.pallas_call(sum_kernel, grid_spec=pltpu.PrefetchScalarGridSpec(num_sca...  8.86 us
  transfers between devices with their start and end apart: 28, of which 10 were waited for; matrix products, arithmetic and copies ran while one was open for 5% of the time, Pallas kernels for 21%

commit v1 on v0

v1 whole, which is shorter than its diff:
```python
import functools

import jax
import jax.numpy as jnp
from jax import lax
from jax.experimental import pallas as pl
from jax.experimental.pallas import tpu as pltpu
from jax.sharding import Mesh
from jax.sharding import PartitionSpec as P


NB = 128
ENTRIES = 64
DEVICES = 128
ATOM_ROWS = 4
ATOM_COLS = 8
CELLS = 384
ROW = ("yl", "z", "c")
COL = ("x", "yh")
ALL = ("yl", "z", "c", "x", "yh")


SMEM = pl.BlockSpec(memory_space=pltpu.SMEM)


def shift(array, axis, step):
    size = lax.axis_size(axis)
    return lax.ppermute(array, axis, [(i, (i + step) % size) for i in range(size)])


def turned_pair(slab, first_plane, y0, z0):
    tile = z0 >> 7
    within = z0 & 127
    tile_after = jnp.minimum(tile + 1, 3)
    lane = lax.broadcasted_iota(jnp.int32, (8, 128), 1)
    planes = []
    for k in range(2):
        plane = 2048 * (first_plane + k) + y0
        here = slab[pl.ds(plane + 512 * tile, 8), :]
        after = slab[pl.ds(plane + 512 * tile_after, 8), :]
        turn = (128 + 64 * k - within) & 127
        planes.append(pltpu.roll(jnp.where(lane >= within, here, after), turn, 1))
    return jnp.where(lane < 64, planes[0], planes[1])


def as_rows(windows):
    lane = lax.broadcasted_iota(jnp.int32, windows.shape, 1)
    sub = lax.broadcasted_iota(jnp.int32, windows.shape, 0) & 7
    for bit in range(3):
        windows = jnp.where((sub >> bit) & 1 == 1, pltpu.roll(windows, 8 << bit, 1), windows)
    windows = jnp.where((lane >> 3) & 7 == sub, windows, 0.0)
    return jnp.sum(windows.reshape(-1, 8, 128), axis=1)


def load_columns(potential, slab, sem):
    copies = [
        pltpu.make_async_copy(
            potential.at[p, :, 128 * t : 128 * t + 128],
            slab.at[(p * 4 + t) * 512 : (p * 4 + t) * 512 + 512, :],
            sem.at[p * 4 + t],
        )
        for p in range(4)
        for t in range(4)
    ]
    for copy in copies:
        copy.start()
    for copy in copies:
        copy.wait()


def edge_kernel(prev_ref, next_ref, potential, prev_out, next_out, slab, held, sem):
    load_columns(potential, slab, sem)

    @pl.loop(0, ENTRIES, unroll=8)
    def _(e):
        row = pl.multiple_of(e * 8, 8)
        held[0, pl.ds(row, 8), :] = turned_pair(slab, 0, prev_ref[1, e], prev_ref[2, e])
        held[1, pl.ds(row, 8), :] = turned_pair(slab, 2, next_ref[1, e], next_ref[2, e])

    prev_out[...] = as_rows(held[0])
    next_out[...] = as_rows(held[1])


def own_kernel(own_ref, potential, out, slab, held, sem):
    load_columns(potential, slab, sem)

    @pl.loop(0, ENTRIES, unroll=8)
    def _(e):
        row = pl.multiple_of(e * 8, 8)
        for k in range(2):
            held[k, pl.ds(row, 8), :] = turned_pair(slab, 2 * k, own_ref[1, e], own_ref[2, e])

    for k in range(2):
        out[k] = as_rows(held[k])


CUT_SCRATCH = [
    pltpu.VMEM((16 * 512, 128), jnp.float32),
    pltpu.VMEM((2, ENTRIES * 8, 128), jnp.float32),
    pltpu.SemaphoreType.DMA((16,)),
]


def cut_edges(prev_offsets, next_offsets, potential):
    shape = jax.ShapeDtypeStruct((ENTRIES, 128), jnp.float32)
    return pl.pallas_call(
        edge_kernel,
        out_shape=(shape, shape),
        in_specs=[SMEM, SMEM, pl.BlockSpec(memory_space=pl.ANY)],
        scratch_shapes=CUT_SCRATCH,
        name="cut_edges",
    )(prev_offsets, next_offsets, potential)


def cut_own(offsets, potential):
    return pl.pallas_call(
        own_kernel,
        out_shape=jax.ShapeDtypeStruct((2, ENTRIES, 128), jnp.float32),
        in_specs=[SMEM, pl.BlockSpec(memory_space=pl.ANY)],
        scratch_shapes=CUT_SCRATCH,
        name="cut_own",
    )(offsets, potential)


GROUP = 8


TAIL = 8


def partial_kernel(pair_ref, live_ref, cubes, left, right, out):
    step = pl.program_id(0)

    @pl.when(step == 0)
    def _():
        out[:, NB:, :] = jnp.zeros((DEVICES, TAIL, NB), jnp.bfloat16)

    for g in range(GROUP):
        e = step * GROUP + g
        weighted = (left[g].astype(jnp.float32) * cubes[g : g + 1, :]).astype(jnp.bfloat16)
        block = lax.dot_general(
            weighted, right[g], (((1,), (1,)), ((), ())), preferred_element_type=jnp.float32
        )
        first, second = pair_ref[0, e], pair_ref[1, e]
        owner = (first >> 2) * 8 + (second >> 3)
        mark = jnp.where(e < live_ref[0], (first & 3) * ATOM_COLS + (second & 7) + 1, 0)
        out[owner, :NB, :] = block.astype(jnp.bfloat16)
        out[owner, NB:, :] = jnp.full((TAIL, NB), mark.astype(jnp.float32)).astype(jnp.bfloat16)


def partial_blocks(pairs, live, cubes, left, right):
    return pl.pallas_call(
        partial_kernel,
        grid_spec=pltpu.PrefetchScalarGridSpec(
            num_scalar_prefetch=2,
            grid=(ENTRIES // GROUP,),
            in_specs=[
                pl.BlockSpec((GROUP, CELLS), lambda i, *_: (i, 0)),
                pl.BlockSpec((GROUP, NB, CELLS), lambda i, *_: (i, 0, 0)),
                pl.BlockSpec((GROUP, NB, CELLS), lambda i, *_: (i, 0, 0)),
            ],
            out_specs=pl.BlockSpec((DEVICES, NB + TAIL, NB), lambda i, *_: (0, 0, 0)),
        ),
        out_shape=jax.ShapeDtypeStruct((DEVICES, NB + TAIL, NB), jnp.bfloat16),
        name="partial_blocks",
    )(pairs, live, cubes, left, right)


SUM_GROUP = 16


def sum_kernel(pattern_ref, core, received, full, even, odd):
    step = pl.program_id(0)
    height = ATOM_ROWS * NB

    @pl.when(step == 0)
    def _():
        even[:height, :] = core[...].astype(jnp.float32)
        odd[...] = jnp.zeros_like(odd)

    marks = [
        received[g, NB:, :].astype(jnp.float32)[0, 0].astype(jnp.int32) for g in range(SUM_GROUP)
    ]
    for g, mark in enumerate(marks):
        where = jnp.where(mark > 0, mark - 1, ATOM_ROWS * ATOM_COLS)
        rows = pl.ds(pl.multiple_of((where >> 3) * NB, NB), NB)
        cols = pl.ds(pl.multiple_of((where & 7) * NB, NB), NB)
        total = even if g % 2 == 0 else odd
        total[rows, cols] += received[g, :NB, :].astype(jnp.float32)

    @pl.when(step == pl.num_programs(0) - 1)
    def _():
        for i in range(ATOM_ROWS):
            rows = slice(i * NB, i * NB + NB)
            for j in range(ATOM_COLS):
                cols = slice(j * NB, j * NB + NB)
                keep = pattern_ref[i * ATOM_COLS + j] > 0
                block = even[rows, cols] + odd[rows, cols]
                full[rows, cols] = jnp.where(keep, block, 0.0).astype(jnp.bfloat16)


def hamiltonian_tile(pattern_tile, core, received):
    rows, cols = core.shape
    whole = pl.BlockSpec((rows, cols), lambda i, *_: (0, 0))
    return pl.pallas_call(
        sum_kernel,
        grid_spec=pltpu.PrefetchScalarGridSpec(
            num_scalar_prefetch=1,
            grid=(DEVICES // SUM_GROUP,),
            in_specs=[
                whole,
                pl.BlockSpec((SUM_GROUP, NB + TAIL, NB), lambda i, *_: (i, 0, 0)),
            ],
            out_specs=whole,
            scratch_shapes=[pltpu.VMEM((rows + NB, cols), jnp.float32)] * 2,
        ),
        out_shape=jax.ShapeDtypeStruct((rows, cols), jnp.bfloat16),
        name="sum_blocks",
    )(pattern_tile, core, received)


def product_kernel(count, first, has_acc, index, *refs):
    pieces, own, other = refs[:count], refs[count], refs[count + 1]
    acc = refs[count + 2] if has_acc else None
    out, columns, rows, column_sem, row_sem = refs[-5:]
    mine = pl.multiple_of(index[0] * 512, 512)
    theirs = pl.multiple_of(512 - index[0] * 512, 512)

    for k in range(count):
        pltpu.make_async_copy(pieces[k], columns.at[k], column_sem.at[k]).start()
        for s, (stack, base, at) in enumerate(((own, 1, mine), (other, 9, theirs))):
            pltpu.make_async_copy(
                stack.at[index[base + first + k]], rows.at[k, pl.ds(at, 512), :], row_sem.at[k, s]
            ).start()

    out[...] = acc[...] if has_acc else jnp.zeros_like(out)

    @pl.loop(0, count)
    def _(k):
        pltpu.make_async_copy(pieces[0], columns.at[k], column_sem.at[k]).wait()
        for s, at in enumerate((mine, theirs)):
            pltpu.make_async_copy(
                own.at[0], rows.at[k, pl.ds(at, 512), :], row_sem.at[k, s]
            ).wait()
        out[...] += jnp.dot(columns[k], rows[k], preferred_element_type=jnp.float32)


def multiply(index, first, acc, pieces, own, other):
    count = len(pieces)
    given = [] if acc is None else [acc]
    vmem = pl.BlockSpec(memory_space=pltpu.VMEM)
    return pl.pallas_call(
        functools.partial(product_kernel, count, first, acc is not None),
        in_specs=[SMEM] + [pl.BlockSpec(memory_space=pl.ANY)] * (count + 2) + [vmem] * len(given),
        out_specs=vmem,
        scratch_shapes=[
            pltpu.VMEM((count, 512, 1024), jnp.bfloat16),
            pltpu.VMEM((count, 1024, 1024), jnp.bfloat16),
            pltpu.SemaphoreType.DMA((count,)),
            pltpu.SemaphoreType.DMA((count, 2)),
        ],
        out_shape=jax.ShapeDtypeStruct((512, 1024), jnp.float32),
        name="product",
    )(index, *pieces, own, other, *given)


def block_mask(values, pattern_tile, block_size):
    row_blocks, col_blocks = pattern_tile.shape
    shaped = values.reshape(row_blocks, block_size, col_blocks, block_size)
    selected = (pattern_tile > 0)[:, None, :, None]
    kept = jnp.where(selected, shaped, jnp.zeros((), values.dtype))
    return kept.reshape(row_blocks * block_size, col_blocks * block_size)


ROUTES = (
    (0, (0, 1), (1, 0)),
    (0, (1, 0), (-1, 0)),
    (0, (-1, 0), (0, 1)),
    (1, (-1, 0), (1, 0)),
    (1, (1, 0), (0, 1)),
    (2, (1, 0), (0, 1)),
    (4, (-1, 0), (0, 1)),
)


def come_from(core):
    found = [(0, 0)]
    for source, *moves in ROUTES:
        steps, cross = moves[core]
        at = found[source]
        found.append(((at[0] - steps) % 4, (at[1] + cross) % 2))
    return found


def tile_at(core):
    found = come_from(core)
    return [found.index((i % 4, i // 4)) for i in range(8)]


def send(array, ring, k):
    _, *moves = ROUTES[k]
    axes = ("yl", "z", "c") if ring == "z" else ("c", "x", "yh")
    pairs = []
    for c in range(2):
        steps, cross = moves[c]
        for i in range(4):
            for y in range(2):
                to_i, to_y = (i + steps) % 4, (y + cross) % 2
                if ring == "z":
                    pairs.append(((y * 4 + i) * 2 + c, (to_y * 4 + to_i) * 2 + c))
                else:
                    pairs.append(((c * 4 + i) * 2 + y, (c * 4 + to_i) * 2 + to_y))
    return lax.ppermute(array, axes, pairs)


def steps(
    potential, basis_left, basis_right, core_matrix, density, pattern, pair_atoms, cube_offsets,
    live_count,
):
    x, yh = lax.axis_index("x"), lax.axis_index("yh")
    yl, z, c = lax.axis_index("yl"), lax.axis_index("z"), lax.axis_index("c")

    offsets = cube_offsets.T
    prev_offsets = shift(offsets, ALL, 1)
    next_offsets = shift(offsets, ALL, -1)

    corner = (lax.axis_index(ROW) * ATOM_ROWS, lax.axis_index(COL) * ATOM_COLS)
    pattern_tile = lax.dynamic_slice(pattern, corner, (ATOM_ROWS, ATOM_COLS))
    d = [block_mask(density, pattern_tile, NB)]
    for k in range(7):
        d.append(send(d[ROUTES[k][0]], "z", k))

    for_prev, for_next = cut_edges(prev_offsets, next_offsets, potential)
    high = shift(for_prev, ALL, -1)
    low = shift(for_next, ALL, 1)
    own = cut_own(offsets, potential)
    extended = jnp.concatenate([low, own[0], own[1], high], axis=1)
    along = cube_offsets[:, :1]
    cubes = jnp.where(
        along == 0,
        extended[:, :384],
        jnp.where(along == 1, extended[:, 64:448], extended[:, 128:]),
    )
    outgoing = partial_blocks(pair_atoms.T, live_count, cubes, basis_left, basis_right)
    received = lax.all_to_all(outgoing, ALL, 0, 0, tiled=True)

    own_rows = jnp.stack(d)
    other_rows = shift(own_rows, "c", 1)

    hamiltonian = hamiltonian_tile(pattern_tile.reshape(-1), core_matrix, received)
    h = [hamiltonian]
    for k in range(7):
        h.append(send(h[ROUTES[k][0]], "x", k))

    sources = jnp.where(c == 0, jnp.array(come_from(0)), jnp.array(come_from(1)))
    block = ((x + sources[:, 0]) & 3) * 2 + ((yh + sources[:, 1]) & 1)
    at = (((block >> 2) + yl) & 1) * 4 + ((block - z) & 3)
    first, second = jnp.array(tile_at(0)), jnp.array(tile_at(1))
    hot = (at[:, None] == jnp.arange(8)[None, :]).astype(jnp.int32)
    in_own = jnp.sum(hot * jnp.where(c == 0, first, second)[None, :], axis=1)
    in_other = jnp.sum(hot * jnp.where(c == 0, second, first)[None, :], axis=1)
    index = jnp.concatenate([c.reshape(1), in_own, in_other]).astype(jnp.int32)

    out = multiply(index, 0, None, h[:4], own_rows, other_rows)
    out = multiply(index, 4, out, h[4:7], own_rows, other_rows)
    out = multiply(index, 7, out, h[7:], own_rows, other_rows)
    return hamiltonian, out


def solution(mesh):
    split = Mesh(mesh.devices.reshape(2, 4, 2, 4, 2), ALL)
    placed = (
        P(ALL, None, None),
        P(ALL, None, None),
        P(ALL, None, None),
        P(ROW, COL),
        P(ROW, COL),
        P(),
        P(ALL, None),
        P(ALL, None),
        P(ALL),
    )
    return jax.shard_map(
        steps,
        mesh=split,
        in_specs=placed,
        out_specs=(P(ROW, COL), P(ROW, COL)),
        check_vma=False,
    )
```

time: 238 us -> 275 us (1.16)
  the two profiles are of different devices: /device:TPU:0 before, /device:TPU:3 now
where the time goes in v1:
time: 275 us; the launch traced here: 274 us
  waiting for transfers between devices  160 us (58%)
  Pallas kernels  54.1 us (20%)
  starting transfers between devices  41.2 us (15%)
  local copies, waits for them, and re-layouts  11.2 us (4%)
  other arithmetic  5.8 us (2%)
    ppermute x14, waiting for transfers between devices, send(): return lax.ppermute(array, axes, pairs)  106 us
    all_to_all x1, waiting for transfers between devices, steps(): received = lax.all_to_all(outgoing, ALL, 0, 0, tiled=True)  53.2 us
    pallas_call x3, Pallas kernels, multiply(): pl.pallas_call(functools.partial(product_kernel, count, first, acc is not...  23.7 us
    ppermute x14, starting transfers between devices, send(): return lax.ppermute(array, axes, pairs)  17.3 us
    all_to_all x1, starting transfers between devices, steps(): received = lax.all_to_all(outgoing, ALL, 0, 0, tiled=True)  16 us
    pallas_call x1, Pallas kernels, partial_blocks(): pl.pallas_call(partial_kernel, grid_spec=pltpu.PrefetchScalarGridSpec(num...  11.1 us
    unnamed x26, local copies, waits for them, and re-layouts  8.61 us
    pallas_call x1, Pallas kernels, hamiltonian_tile(): pl.pallas_call(sum_kernel, grid_spec=pltpu.PrefetchScalarGridSpec(num_sca...  8.36 us
  transfers between devices with their start and end apart: 20, of which 11 were waited for; matrix products, arithmetic and copies ran while one was open for 4% of the time, Pallas kernels for 18%

profile of v1, /device:TPU:3, one launch (start us, length us, event | category | flops | bytes accessed | tf_op | source)
XLA Modules:
  0.0 274.1 jit_solution(9663317958265419823)
XLA Ops:
  0.7 0.8 broadcast_compare_fusion
  1.4 0.2 broadcast_in_dim.40
  1.6 2.7 bitcast_dynamic-update-slice_fusion.7
  4.3 1.6 collective-permute-start.7
  6.0 2.1 collective-permute-start.8
  8.1 21.3 %collective-permute-done.7 = bf16[512,1024]{1,0:T(8,128)(2,1)S(1)} collective-permute-done((bf16[512,1024]{1,0:T(8,128)(2,1)S(1)}, bf16[512,1024]{1,0:T(8,128)(2,1)S(1)}, u32[]{:S(2)}, u32[]{:S(2)}) %collective-permute-start.7) | collective-permute-done | bytes 1048608 | tf_op jit(solution)/shard_map/ppermute | solution.py:313
  29.4 2.4 collective-permute-start.9
  31.8 1.4 collective-permute-start.12
  33.3 1.1 bitcast_dynamic-update-slice_fusion.6
  34.3 1.1 bitcast_dynamic-update-slice_fusion.5
  35.4 20.4 %collective-permute-done.10 = bf16[512,1024]{1,0:T(8,128)(2,1)S(1)} collective-permute-done((bf16[512,1024]{1,0:T(8,128)(2,1)S(1)}, bf16[512,1024]{1,0:T(8,128)(2,1)S(1)}, u32[]{:S(2)}, u32[]{:S(2)}) %collective-permute-start.10) | collective-permute-done | bytes 1048608 | tf_op jit(solution)/shard_map/ppermute | solution.py:313
  55.8 2.4 collective-permute-start.13
  58.2 1.1 bitcast_dynamic-update-slice_fusion.4
  59.3 1.1 bitcast_dynamic-update-slice_fusion.3
  60.3 1.1 bitcast_dynamic-update-slice_fusion.2
  61.4 5.1 %collective-permute-done.12 = bf16[512,1024]{1,0:T(8,128)(2,1)S(1)} collective-permute-done((bf16[512,1024]{1,0:T(8,128)(2,1)S(1)}, bf16[512,1024]{1,0:T(8,128)(2,1)S(1)}, u32[]{:S(2)}, u32[]{:S(2)}) %collective-permute-start.12) | collective-permute-done | bytes 1048608 | tf_op jit(solution)/shard_map/ppermute | solution.py:313
  66.5 1.1 bitcast_dynamic-update-slice_fusion.1
  67.5 10.2 %collective-permute-done.13 = bf16[512,1024]{1,0:T(8,128)(2,1)S(1)} collective-permute-done((bf16[512,1024]{1,0:T(8,128)(2,1)S(1)}, bf16[512,1024]{1,0:T(8,128)(2,1)S(1)}, u32[]{:S(2)}, u32[]{:S(2)}) %collective-permute-start.13) | collective-permute-done | bytes 1048608 | tf_op jit(solution)/shard_map/ppermute | solution.py:313
  77.7 1.1 bitcast_dynamic-update-slice_fusion.refs_4_.refs_3_.refs_1_
  78.8 2.3 collective-permute-start
  81.1 1.5 collective-permute-start.1
  82.6 5.5 %cut_own.1 = f32[2,64,128]{2,1,0:T(8,128)} custom-call(s32[3,64]{1,0:T(4,128)} %bitcast.35, f32[4,512,512]{2,1,0:T(8,128)} %potential.3), custom_call_target="tpu_custom_call" | custom-call | tf_op jit(solution)/shard_map/cut_own/pallas_call | solution.py:116
  88.1 0.8 slice_bitcast_fusion.1
  88.9 0.6 copy-done.3
  89.5 0.6 copy-done.4
  90.1 5.5 %cut_edges.1 = (f32[64,128]{1,0:T(8,128)}, f32[64,128]{1,0:T(8,128)}) custom-call(s32[3,64]{1,0:T(4,128)} %copy-done.3, s32[3,64]{1,0:T(4,128)} %copy-done.4, f32[4,512,512]{2,1,0:T(8,128)} %potential.3), custom_call_target="tpu_custom_call" | custom-call | tf_op jit(solution)/shard_map/cut_edges/pallas_call | solution.py:106
  95.6 1.5 collective-permute-start.2
  97.0 2.4 collective-permute-start.3
  99.5 0.7 compare_bitcast_fusion.1
  101.0 0.5 collective-permute-done.3
  101.5 0.8 fusion.1.cubes
  102.3 11.1 %partial_blocks.1 = bf16[128,136,128]{2,1,0:T(8,128)(2,1)} custom-call(s32[2,64]{1,0:T(2,128)} %bitcast.38, s32[1]{0:T(128)S(6)} %copy.25.live_ref, f32[64,384]{1,0:T(8,128)} %fusion.1.cubes, bf16[64,128,384]{2,1,0:T(8,128)(2,1)} %left.1, bf16[64,128,384]{2,1,0:T(8,128)(2,1)} %right.1), custom_call_target="tpu_custom_call" | custom-call | tf_op jit(solution)/shard_map/partial_blocks/pallas_call | solution.py:152
  113.4 16.0 %all-to-all-start = ((bf16[128,136,128]{2,1,0:T(8,128)(2,1)}), bf16[128,136,128]{2,1,0:T(8,128)(2,1)}, u32[]{:S(2)}, u32[]{:S(2)}) async-start(bf16[128,136,128]{2,1,0:T(8,128)(2,1)} %partial_blocks.1), calls=%async_computation | async-start | bytes 8912896 | tf_op jit(solution)/shard_map/all_to_all | solution.py:345
  129.5 0.6 reshape.22.pattern_ref
  130.0 53.2 %all-to-all-done.received = bf16[128,136,128]{2,1,0:T(8,128)(2,1)} async-done(((bf16[128,136,128]{2,1,0:T(8,128)(2,1)}), bf16[128,136,128]{2,1,0:T(8,128)(2,1)}, u32[]{:S(2)}, u32[]{:S(2)}) %all-to-all-start) | async-done | bytes 4456480 | tf_op jit(solution)/shard_map/all_to_all | solution.py:345
  183.3 8.4 %sum_blocks.1.refs_0_ = bf16[512,1024]{1,0:T(8,128)(2,1)} custom-call(s32[32]{0:T(128)} %reshape.22.pattern_ref, bf16[512,1024]{1,0:T(8,128)(2,1)} %core.1, bf16[128,136,128]{2,1,0:T(8,128)(2,1)} %all-to-all-done.received), custom_call_target="tpu_custom_call" | custom-call | tf_op jit(solution)/shard_map/sum_blocks/pallas_call | solution.py:205
  191.6 2.0 collective-permute-start.4
  193.7 22.0 %collective-permute-done.4.refs_1_ = bf16[512,1024]{1,0:T(8,128)(2,1)S(1)} collective-permute-done((bf16[512,1024]{1,0:T(8,128)(2,1)}, bf16[512,1024]{1,0:T(8,128)(2,1)S(1)}, u32[]{:S(2)}, u32[]{:S(2)}) %collective-permute-start.4) | collective-permute-done | bytes 1048608 | tf_op jit(solution)/shard_map/ppermute | solution.py:313
  215.6 2.2 collective-permute-start.5
  217.8 3.0 %collective-permute-start.15 = (bf16[512,1024]{1,0:T(8,128)(2,1)S(1)}, bf16[512,1024]{1,0:T(8,128)(2,1)}, u32[]{:S(2)}, u32[]{:S(2)}) collective-permute-start(bf16[512,1024]{1,0:T(8,128)(2,1)S(1)} %collective-permute-done.4.refs_1_), channel_id=1, source_target_pairs={{0,2},{1,3},{2,4},{3,5},{4,6},{5,7},{6,0},{7,1},{8,9},{9,8},{10,11... | collective-permute-start | bytes 3145736 | tf_op jit(solution)/shard_map/ppermute | solution.py:313
  220.9 20.0 %collective-permute-done.5.refs_0_ = bf16[512,1024]{1,0:T(8,128)(2,1)} collective-permute-done((bf16[512,1024]{1,0:T(8,128)(2,1)S(1)}, bf16[512,1024]{1,0:T(8,128)(2,1)}, u32[]{:S(2)}, u32[]{:S(2)}) %collective-permute-start.5) | collective-permute-done | bytes 1048608 | tf_op jit(solution)/shard_map/ppermute | solution.py:313
  241.2 0.7 pad_add_fusion.index
  241.9 9.0 %product.3.refs_5_ = f32[512,1024]{1,0:T(8,128)} custom-call(s32[17]{0:T(128)} %pad_add_fusion.index, bf16[512,1024]{1,0:T(8,128)(2,1)} %sum_blocks.1.refs_0_, bf16[512,1024]{1,0:T(8,128)(2,1)} %copy-done, bf16[512,1024]{1,0:T(8,128)(2,1)} %copy-done.1, bf16[512,1024]{1,0:T(8,128)(2,1)} %collective-permute-done.18.refs_3_, ...), custom_call_target="tpu_custom_call" | custom-call | tf_op jit(solution)/shard_map/product/pallas_call | solution.py:252
  250.9 4.9 %collective-permute-done.17.refs_2_ = bf16[512,1024]{1,0:T(8,128)(2,1)} collective-permute-done((bf16[512,1024]{1,0:T(8,128)(2,1)S(1)}, bf16[512,1024]{1,0:T(8,128)(2,1)}, u32[]{:S(2)}, u32[]{:S(2)}) %collective-permute-start.17) | collective-permute-done | bytes 1048608 | tf_op jit(solution)/shard_map/ppermute | solution.py:313
  255.8 8.7 %product.4.refs_3_ = f32[512,1024]{1,0:T(8,128)} custom-call(s32[17]{0:T(128)} %pad_add_fusion.index, bf16[512,1024]{1,0:T(8,128)(2,1)} %collective-permute-done.5.refs_0_, bf16[512,1024]{1,0:T(8,128)(2,1)} %collective-permute-done.15.refs_1_, bf16[512,1024]{1,0:T(8,128)(2,1)} %collective-permute-done.17.refs_2_, ...), custom_call_target="tpu_custom_call" | custom-call | tf_op jit(solution)/shard_map/product/pallas_call | solution.py:252
  264.5 2.5 collective-permute-done.6.refs_0_
  266.9 1.0 copy-done.2
  267.9 6.1 %product.5 = f32[512,1024]{1,0:T(8,128)} custom-call(s32[17]{0:T(128)} %pad_add_fusion.index, bf16[512,1024]{1,0:T(8,128)(2,1)} %copy-done.2, bf16[8,512,1024]{2,1,0:T(8,128)(2,1)} %bitcast_dynamic-update-slice_fusion.refs_4_.refs_3_.refs_1_, bf16[8,512,1024]{2,1,0:T(8,128)(2,1)} %collective-permute-done.14.refs_5_.refs_4_.refs_2_, f32[512,1024]{1,0:T(8,128)} %product.4.refs_3_), custom_call_target="tpu_custom_call" | custom-call | tf_op jit(solution)/shard_map/product/pallas_call | solution.py:252
  (38 shorter events, 0.6 us)
Async XLA Ops:
  1.6 77.1 %copy-start.5 = (s32[64,3]{0,1:T(4,128)S(1)}, s32[64,3]{0,1:T(4,128)}, u32[]{:S(2)}) copy-start(s32[64,3]{0,1:T(4,128)} %param.20) | copy-start | bytes 2308
  4.3 25.0 %collective-permute-start.7 = (bf16[512,1024]{1,0:T(8,128)(2,1)S(1)}, bf16[512,1024]{1,0:T(8,128)(2,1)S(1)}, u32[]{:S(2)}, u32[]{:S(2)}) collective-permute-start(bf16[512,1024]{1,0:T(8,128)(2,1)S(1)} %get-tuple-element.9), channel_id=1, source_target_pairs={{0,64},{64,0},{16,80},{80,16},{32,96},{96,32},{48,112},{112,48},{8... | collective-permute-start | bytes 3145736 | tf_op jit(solution)/shard_map/ppermute | solution.py:313
  6.0 25.9 %collective-permute-start.8 = (bf16[512,1024]{1,0:T(8,128)(2,1)S(1)}, bf16[512,1024]{1,0:T(8,128)(2,1)S(1)}, u32[]{:S(2)}, u32[]{:S(2)}) collective-permute-start(bf16[512,1024]{1,0:T(8,128)(2,1)S(1)} %get-tuple-element.9), channel_id=1, source_target_pairs={{0,16},{64,80},{16,32},{80,96},{32,48},{96,112},{48,0},{112,64},{8... | collective-permute-start | bytes 3145736 | tf_op jit(solution)/shard_map/ppermute | solution.py:313
  29.4 26.4 %collective-permute-start.10 = (bf16[512,1024]{1,0:T(8,128)(2,1)S(1)}, bf16[512,1024]{1,0:T(8,128)(2,1)S(1)}, u32[]{:S(2)}, u32[]{:S(2)}) collective-permute-start(bf16[512,1024]{1,0:T(8,128)(2,1)S(1)} %collective-permute-done.7), channel_id=1, source_target_pairs={{0,48},{64,112},{16,0},{80,64},{32,16},{96,80},{48,32},{112,96},{8... | collective-permute-start | bytes 3145736 | tf_op jit(solution)/shard_map/ppermute | solution.py:313
  29.4 28.8 %collective-permute-start.9 = (bf16[512,1024]{1,0:T(8,128)(2,1)S(1)}, bf16[512,1024]{1,0:T(8,128)(2,1)S(1)}, u32[]{:S(2)}, u32[]{:S(2)}) collective-permute-start(bf16[512,1024]{1,0:T(8,128)(2,1)S(1)} %get-tuple-element.9), channel_id=1, source_target_pairs={{0,48},{64,112},{16,0},{80,64},{32,16},{96,80},{48,32},{112,96},{8... | collective-permute-start | bytes 3145736 | tf_op jit(solution)/shard_map/ppermute | solution.py:313
  31.8 28.5 %collective-permute-start.11 = (bf16[512,1024]{1,0:T(8,128)(2,1)S(1)}, bf16[512,1024]{1,0:T(8,128)(2,1)S(1)}, u32[]{:S(2)}, u32[]{:S(2)}) collective-permute-start(bf16[512,1024]{1,0:T(8,128)(2,1)S(1)} %collective-permute-done.7), channel_id=1, source_target_pairs={{0,16},{64,80},{16,32},{80,96},{32,48},{96,112},{48,0},{112,64},{8... | collective-permute-start | bytes 3145736 | tf_op jit(solution)/shard_map/ppermute | solution.py:313
  31.8 34.6 %collective-permute-start.12 = (bf16[512,1024]{1,0:T(8,128)(2,1)S(1)}, bf16[512,1024]{1,0:T(8,128)(2,1)S(1)}, u32[]{:S(2)}, u32[]{:S(2)}) collective-permute-start(bf16[512,1024]{1,0:T(8,128)(2,1)S(1)} %collective-permute-done.8), channel_id=1, source_target_pairs={{0,16},{64,80},{16,32},{80,96},{32,48},{96,112},{48,0},{112,64},{8... | collective-permute-start | bytes 3145736 | tf_op jit(solution)/shard_map/ppermute | solution.py:313
  55.8 21.9 %collective-permute-start.13 = (bf16[512,1024]{1,0:T(8,128)(2,1)S(1)}, bf16[512,1024]{1,0:T(8,128)(2,1)S(1)}, u32[]{:S(2)}, u32[]{:S(2)}) collective-permute-start(bf16[512,1024]{1,0:T(8,128)(2,1)S(1)} %collective-permute-done.10), channel_id=1, source_target_pairs={{0,48},{64,112},{16,0},{80,64},{32,16},{96,80},{48,32},{112,96},{8... | collective-permute-start | bytes 3145736 | tf_op jit(solution)/shard_map/ppermute | solution.py:313
  78.7 163.1 %collective-permute-start.14 = (bf16[8,512,1024]{2,1,0:T(8,128)(2,1)}, bf16[8,512,1024]{2,1,0:T(8,128)(2,1)}, u32[]{:S(2)}, u32[]{:S(2)}) collective-permute-start(bf16[8,512,1024]{2,1,0:T(8,128)(2,1)} %bitcast_dynamic-update-slice_fusion.refs_4_.refs_3_.refs_1_), channel_id=1, source_target_pairs={{0,8},{8,0},{1,9},{9,1},{2,10},{10,2},{3,11},{11,3},{4,12},{12,4},... | collective-permute-start | bytes 25165832 | tf_op jit(solution)/shard_map/ppermute | solution.py:28
  78.8 10.1 %collective-permute-start = (s32[3,64]{1,0:T(4,128)S(1)}, s32[3,64]{1,0:T(4,128)S(1)}, u32[]{:S(2)}, u32[]{:S(2)}) collective-permute-start(s32[3,64]{1,0:T(4,128)S(1)} %bitcast.36), channel_id=1, source_target_pairs={{0,1},{1,2},{2,3},{3,4},{4,5},{5,6},{6,7},{7,8},{8,9},{9,10},{10,1... | collective-permute-start | bytes 2312 | tf_op jit(solution)/shard_map/ppermute | solution.py:28
  81.1 7.8 %collective-permute-start.1 = (s32[3,64]{1,0:T(4,128)S(1)}, s32[3,64]{1,0:T(4,128)S(1)}, u32[]{:S(2)}, u32[]{:S(2)}) collective-permute-start(s32[3,64]{1,0:T(4,128)S(1)} %bitcast.37), channel_id=1, source_target_pairs={{0,127},{1,0},{2,1},{3,2},{4,3},{5,4},{6,5},{7,6},{8,7},{9,8},{10,... | collective-permute-start | bytes 2312 | tf_op jit(solution)/shard_map/ppermute | solution.py:28
  88.9 0.6 copy-start.3
  89.5 0.6 copy-start.4
  95.6 5.5 %collective-permute-start.2 = (f32[64,128]{1,0:T(8,128)}, f32[64,128]{1,0:T(8,128)S(1)}, u32[]{:S(2)}, u32[]{:S(2)}) collective-permute-start(f32[64,128]{1,0:T(8,128)} %get-tuple-element.4), channel_id=1, source_target_pairs={{0,1},{1,2},{2,3},{3,4},{4,5},{5,6},{6,7},{7,8},{8,9},{9,10},{10,1... | collective-permute-start | bytes 98312 | tf_op jit(solution)/shard_map/ppermute | solution.py:28
  97.0 4.5 %collective-permute-start.3 = (f32[64,128]{1,0:T(8,128)}, f32[64,128]{1,0:T(8,128)S(1)}, u32[]{:S(2)}, u32[]{:S(2)}) collective-permute-start(f32[64,128]{1,0:T(8,128)} %get-tuple-element.5), channel_id=1, source_target_pairs={{0,127},{1,0},{2,1},{3,2},{4,3},{5,4},{6,5},{7,6},{8,7},{9,8},{10,... | collective-permute-start | bytes 98312 | tf_op jit(solution)/shard_map/ppermute | solution.py:28
  113.4 127.5 %copy-start.6 = (s32[8,2]{0,1:T(2,128)S(1)}, s32[8,2]{0,1:T(2,128)}, u32[]{:S(2)}) copy-start(s32[8,2]{0,1:T(2,128)} %constant.50.clone) | copy-start | bytes 196
  113.4 127.5 %copy-start.7 = (s32[8,2]{0,1:T(2,128)S(1)}, s32[8,2]{0,1:T(2,128)}, u32[]{:S(2)}) copy-start(s32[8,2]{0,1:T(2,128)} %constant.51.clone) | copy-start | bytes 196
  113.4 127.5 %copy-start.8 = (s32[8]{0:T(128)S(1)}, s32[8]{0:T(128)}, u32[]{:S(2)}) copy-start(s32[8]{0:T(128)} %constant.52.clone) | copy-start | bytes 100
  113.4 127.6 %copy-start.9 = (s32[8]{0:T(128)S(1)}, s32[8]{0:T(128)}, u32[]{:S(2)}) copy-start(s32[8]{0:T(128)} %constant.53.clone) | copy-start | bytes 100
  113.4 69.8 %all-to-all-start = ((bf16[128,136,128]{2,1,0:T(8,128)(2,1)}), bf16[128,136,128]{2,1,0:T(8,128)(2,1)}, u32[]{:S(2)}, u32[]{:S(2)}) async-start(bf16[128,136,128]{2,1,0:T(8,128)(2,1)} %partial_blocks.1), calls=%async_computation | async-start | bytes 8912896 | tf_op jit(solution)/shard_map/all_to_all | solution.py:345
  191.6 24.0 %collective-permute-start.4 = (bf16[512,1024]{1,0:T(8,128)(2,1)}, bf16[512,1024]{1,0:T(8,128)(2,1)S(1)}, u32[]{:S(2)}, u32[]{:S(2)}) collective-permute-start(bf16[512,1024]{1,0:T(8,128)(2,1)} %sum_blocks.1.refs_0_), channel_id=1, source_target_pairs={{0,1},{1,0},{2,3},{3,2},{4,5},{5,4},{6,7},{7,6},{8,10},{9,11},{10,... | collective-permute-start | bytes 3145736 | tf_op jit(solution)/shard_map/ppermute | solution.py:313
  193.7 27.2 %collective-permute-start.16 = (bf16[512,1024]{1,0:T(8,128)(2,1)}, bf16[512,1024]{1,0:T(8,128)(2,1)S(1)}, u32[]{:S(2)}, u32[]{:S(2)}) collective-permute-start(bf16[512,1024]{1,0:T(8,128)(2,1)} %sum_blocks.1.refs_0_), channel_id=1, source_target_pairs={{0,2},{1,3},{2,4},{3,5},{4,6},{5,7},{6,0},{7,1},{8,14},{9,15},{10,... | collective-permute-start | bytes 3145736 | tf_op jit(solution)/shard_map/ppermute | solution.py:313
  215.6 26.2 %copy-start = (bf16[512,1024]{1,0:T(8,128)(2,1)}, bf16[512,1024]{1,0:T(8,128)(2,1)S(1)}, u32[]{:S(2)}) copy-start(bf16[512,1024]{1,0:T(8,128)(2,1)S(1)} %collective-permute-done.4.refs_1_) | copy-start | bytes 3145732
  215.6 25.3 %collective-permute-start.5 = (bf16[512,1024]{1,0:T(8,128)(2,1)S(1)}, bf16[512,1024]{1,0:T(8,128)(2,1)}, u32[]{:S(2)}, u32[]{:S(2)}) collective-permute-start(bf16[512,1024]{1,0:T(8,128)(2,1)S(1)} %collective-permute-done.4.refs_1_), channel_id=1, source_target_pairs={{0,6},{1,7},{2,0},{3,1},{4,2},{5,3},{6,4},{7,5},{8,10},{9,11},{10,... | collective-permute-start | bytes 3145736 | tf_op jit(solution)/shard_map/ppermute | solution.py:313
  217.8 24.0 %collective-permute-start.18 = (bf16[512,1024]{1,0:T(8,128)(2,1)}, bf16[512,1024]{1,0:T(8,128)(2,1)}, u32[]{:S(2)}, u32[]{:S(2)}) collective-permute-start(bf16[512,1024]{1,0:T(8,128)(2,1)} %sum_blocks.1.refs_0_), channel_id=1, source_target_pairs={{0,6},{1,7},{2,0},{3,1},{4,2},{5,3},{6,4},{7,5},{8,9},{9,8},{10,11... | collective-permute-start | bytes 3145736 | tf_op jit(solution)/shard_map/ppermute | solution.py:313
  217.8 33.0 %collective-permute-start.15 = (bf16[512,1024]{1,0:T(8,128)(2,1)S(1)}, bf16[512,1024]{1,0:T(8,128)(2,1)}, u32[]{:S(2)}, u32[]{:S(2)}) collective-permute-start(bf16[512,1024]{1,0:T(8,128)(2,1)S(1)} %collective-permute-done.4.refs_1_), channel_id=1, source_target_pairs={{0,2},{1,3},{2,4},{3,5},{4,6},{5,7},{6,0},{7,1},{8,9},{9,8},{10,11... | collective-permute-start | bytes 3145736 | tf_op jit(solution)/shard_map/ppermute | solution.py:313
  220.8 21.1 %copy-start.1 = (bf16[512,1024]{1,0:T(8,128)(2,1)}, bf16[512,1024]{1,0:T(8,128)(2,1)S(1)}, u32[]{:S(2)}) copy-start(bf16[512,1024]{1,0:T(8,128)(2,1)S(1)} %collective-permute-done.16.refs_2_) | copy-start | bytes 3145732
  220.8 35.0 %collective-permute-start.17 = (bf16[512,1024]{1,0:T(8,128)(2,1)S(1)}, bf16[512,1024]{1,0:T(8,128)(2,1)}, u32[]{:S(2)}, u32[]{:S(2)}) collective-permute-start(bf16[512,1024]{1,0:T(8,128)(2,1)S(1)} %collective-permute-done.16.refs_2_), channel_id=1, source_target_pairs={{0,2},{1,3},{2,4},{3,5},{4,6},{5,7},{6,0},{7,1},{8,9},{9,8},{10,11... | collective-permute-start | bytes 3145736 | tf_op jit(solution)/shard_map/ppermute | solution.py:313
  240.9 26.0 %collective-permute-start.6 = (bf16[512,1024]{1,0:T(8,128)(2,1)}, bf16[512,1024]{1,0:T(8,128)(2,1)S(1)}, u32[]{:S(2)}, u32[]{:S(2)}) collective-permute-start(bf16[512,1024]{1,0:T(8,128)(2,1)} %collective-permute-done.5.refs_0_), channel_id=1, source_target_pairs={{0,6},{1,7},{2,0},{3,1},{4,2},{5,3},{6,4},{7,5},{8,9},{9,8},{10,11... | collective-permute-start | bytes 3145736 | tf_op jit(solution)/shard_map/ppermute | solution.py:313
  266.9 1.0 copy-start.2

commit v2 on v1

v2 whole, which is shorter than its diff:
```python
import functools

import jax
import jax.numpy as jnp
from jax import lax
from jax.experimental import pallas as pl
from jax.experimental.pallas import tpu as pltpu
from jax.sharding import Mesh
from jax.sharding import PartitionSpec as P


NB = 128
ENTRIES = 64
DEVICES = 128
ATOM_ROWS = 4
ATOM_COLS = 8
CELLS = 384
ROW = ("yl", "z", "c")
COL = ("x", "yh")
ALL = ("yl", "z", "c", "x", "yh")


SMEM = pl.BlockSpec(memory_space=pltpu.SMEM)


def shift(array, axis, step):
    size = lax.axis_size(axis)
    return lax.ppermute(array, axis, [(i, (i + step) % size) for i in range(size)])


def turned_pair(slab, first_plane, y0, z0):
    tile = z0 >> 7
    within = z0 & 127
    tile_after = jnp.minimum(tile + 1, 3)
    lane = lax.broadcasted_iota(jnp.int32, (8, 128), 1)
    planes = []
    for k in range(2):
        plane = 2048 * (first_plane + k) + y0
        here = slab[pl.ds(plane + 512 * tile, 8), :]
        after = slab[pl.ds(plane + 512 * tile_after, 8), :]
        turn = (128 + 64 * k - within) & 127
        planes.append(pltpu.roll(jnp.where(lane >= within, here, after), turn, 1))
    return jnp.where(lane < 64, planes[0], planes[1])


def as_rows(windows):
    lane = lax.broadcasted_iota(jnp.int32, windows.shape, 1)
    sub = lax.broadcasted_iota(jnp.int32, windows.shape, 0) & 7
    for bit in range(3):
        windows = jnp.where((sub >> bit) & 1 == 1, pltpu.roll(windows, 8 << bit, 1), windows)
    windows = jnp.where((lane >> 3) & 7 == sub, windows, 0.0)
    return jnp.sum(windows.reshape(-1, 8, 128), axis=1)


def column_copies(potential, slab, sem):
    return [
        pltpu.make_async_copy(
            potential.at[p, :, 128 * t : 128 * t + 128],
            slab.at[(p * 4 + t) * 512 : (p * 4 + t) * 512 + 512, :],
            sem.at[p * 4 + t],
        )
        for p in range(4)
        for t in range(4)
    ]


def cut_both(offset_refs, outs, potential, slab, held, sem):
    copies = column_copies(potential, slab, sem)
    for copy in copies:
        copy.start()
    for k in range(2):
        for copy in copies[8 * k : 8 * k + 8]:
            copy.wait()
        offset_ref = offset_refs[k]

        @pl.loop(0, ENTRIES, unroll=8)
        def _(e, k=k, offset_ref=offset_ref):
            row = pl.multiple_of(e * 8, 8)
            held[k, pl.ds(row, 8), :] = turned_pair(
                slab, 2 * k, offset_ref[1, e], offset_ref[2, e]
            )

        outs[k][...] = as_rows(held[k])


def edge_kernel(prev_ref, next_ref, potential, prev_out, next_out, slab, held, sem):
    cut_both((prev_ref, next_ref), (prev_out, next_out), potential, slab, held, sem)


def own_kernel(own_ref, potential, out, slab, held, sem):
    cut_both((own_ref, own_ref), (out.at[0], out.at[1]), potential, slab, held, sem)


CUT_SCRATCH = [
    pltpu.VMEM((16 * 512, 128), jnp.float32),
    pltpu.VMEM((2, ENTRIES * 8, 128), jnp.float32),
    pltpu.SemaphoreType.DMA((16,)),
]


def cut_edges(prev_offsets, next_offsets, potential):
    shape = jax.ShapeDtypeStruct((ENTRIES, 128), jnp.float32)
    return pl.pallas_call(
        edge_kernel,
        out_shape=(shape, shape),
        in_specs=[SMEM, SMEM, pl.BlockSpec(memory_space=pl.ANY)],
        scratch_shapes=CUT_SCRATCH,
        name="cut_edges",
    )(prev_offsets, next_offsets, potential)


def cut_own(offsets, potential):
    return pl.pallas_call(
        own_kernel,
        out_shape=jax.ShapeDtypeStruct((2, ENTRIES, 128), jnp.float32),
        in_specs=[SMEM, pl.BlockSpec(memory_space=pl.ANY)],
        scratch_shapes=CUT_SCRATCH,
        name="cut_own",
    )(offsets, potential)


GROUP = 8
GROUPS = ENTRIES // GROUP
TAIL = 8


def cube_row(windows, along):
    lane = lax.broadcasted_iota(jnp.int32, (1, 128), 1)
    turned = [pltpu.roll(w, 64, 1) for w in windows]
    cells = []
    for i in range(3):
        between = jnp.where(lane < 64, turned[i], turned[i + 1])
        cells.append(
            jnp.where(along == 0, windows[i], jnp.where(along == 1, between, windows[i + 1]))
        )
    return jnp.concatenate(cells, axis=1)


def partial_kernel(
    pair_ref, live_ref, offset_ref, low, own, high, left, right, out,
    lefts, rights, staged, blank, in_sem, out_sem, blank_sem,
):
    def reads(g):
        rows = pl.ds(g * GROUP, GROUP)
        return (
            pltpu.make_async_copy(left.at[rows], lefts.at[rows], in_sem.at[g, 0]),
            pltpu.make_async_copy(right.at[rows], rights.at[rows], in_sem.at[g, 1]),
        )

    for g in range(GROUPS):
        for copy in reads(g):
            copy.start()
    blank[...] = jnp.zeros_like(blank)
    clear = pltpu.make_async_copy(blank, out.at[:, NB:, :], blank_sem)
    clear.start()
    clear.wait()

    @pl.loop(0, GROUPS)
    def _(g):
        for copy in reads(g):
            copy.wait()
        for i in range(GROUP):
            e = g * GROUP + i
            row = pl.ds(e, 1)
            windows = [low[row, :], own[0, row, :], own[1, row, :], high[row, :]]
            cube = cube_row(windows, offset_ref[0, e])
            weighted = (lefts[e].astype(jnp.float32) * cube).astype(jnp.bfloat16)
            block = lax.dot_general(
                weighted, rights[e], (((1,), (1,)), ((), ())), preferred_element_type=jnp.float32
            )
            first, second = pair_ref[0, e], pair_ref[1, e]
            owner = (first >> 2) * 8 + (second >> 3)
            mark = jnp.where(e < live_ref[0], (first & 3) * ATOM_COLS + (second & 7) + 1, 0)
            staged[e, :NB, :] = block.astype(jnp.bfloat16)
            staged[e, NB:, :] = jnp.full((TAIL, NB), mark.astype(jnp.float32)).astype(jnp.bfloat16)
            pltpu.make_async_copy(staged.at[e], out.at[owner], out_sem.at[e]).start()

    @pl.loop(0, ENTRIES)
    def _(e):
        pltpu.make_async_copy(staged.at[e], out.at[0], out_sem.at[e]).wait()


def partial_blocks(pairs, live, offsets, low, own, high, left, right):
    vmem = pl.BlockSpec(memory_space=pltpu.VMEM)
    hbm = pl.BlockSpec(memory_space=pl.ANY)
    return pl.pallas_call(
        partial_kernel,
        in_specs=[SMEM] * 3 + [vmem] * 3 + [hbm] * 2,
        out_specs=hbm,
        scratch_shapes=[
            pltpu.VMEM((ENTRIES, NB, CELLS), jnp.bfloat16),
            pltpu.VMEM((ENTRIES, NB, CELLS), jnp.bfloat16),
            pltpu.VMEM((ENTRIES, NB + TAIL, NB), jnp.bfloat16),
            pltpu.VMEM((DEVICES, TAIL, NB), jnp.bfloat16),
            pltpu.SemaphoreType.DMA((GROUPS, 2)),
            pltpu.SemaphoreType.DMA((ENTRIES,)),
            pltpu.SemaphoreType.DMA,
        ],
        out_shape=jax.ShapeDtypeStruct((DEVICES, NB + TAIL, NB), jnp.bfloat16),
        name="partial_blocks",
    )(pairs, live, offsets, low, own, high, left, right)


SUM_GROUP = 16
SUM_GROUPS = DEVICES // SUM_GROUP


def sum_kernel(pattern_ref, core, received, full, tile, slots, even, odd, core_sem, slot_sem):
    def read(g):
        rows = pl.ds(g * SUM_GROUP, SUM_GROUP)
        return pltpu.make_async_copy(received.at[rows], slots.at[rows], slot_sem.at[g])

    load = pltpu.make_async_copy(core, tile, core_sem)
    load.start()
    for g in range(SUM_GROUPS):
        read(g).start()
    odd[...] = jnp.zeros_like(odd)
    load.wait()
    for i in range(ATOM_ROWS):
        for j in range(ATOM_COLS):
            block = tile[i * NB : i * NB + NB, j * NB : j * NB + NB]
            even[i * ATOM_COLS + j + 1] = block.astype(jnp.float32)

    @pl.loop(0, SUM_GROUPS)
    def _(g):
        read(g).wait()
        at = [g * SUM_GROUP + i for i in range(SUM_GROUP)]
        marks = [slots[s, NB:, :].astype(jnp.float32)[0, 0].astype(jnp.int32) for s in at]
        for i, mark in enumerate(marks):
            total = even if i % 2 == 0 else odd
            total[mark] += slots[at[i], :NB, :].astype(jnp.float32)

    for i in range(ATOM_ROWS):
        for j in range(ATOM_COLS):
            keep = pattern_ref[i * ATOM_COLS + j] > 0
            block = even[i * ATOM_COLS + j + 1] + odd[i * ATOM_COLS + j + 1]
            full[i * NB : i * NB + NB, j * NB : j * NB + NB] = jnp.where(keep, block, 0.0).astype(
                jnp.bfloat16
            )


def hamiltonian_tile(pattern_tile, core, received):
    hbm = pl.BlockSpec(memory_space=pl.ANY)
    return pl.pallas_call(
        sum_kernel,
        in_specs=[SMEM, hbm, hbm],
        out_specs=pl.BlockSpec(memory_space=pltpu.VMEM),
        scratch_shapes=[
            pltpu.VMEM(core.shape, jnp.bfloat16),
            pltpu.VMEM(received.shape, jnp.bfloat16),
            pltpu.VMEM((ATOM_ROWS * ATOM_COLS + 1, NB, NB), jnp.float32),
            pltpu.VMEM((ATOM_ROWS * ATOM_COLS + 1, NB, NB), jnp.float32),
            pltpu.SemaphoreType.DMA,
            pltpu.SemaphoreType.DMA((SUM_GROUPS,)),
        ],
        out_shape=jax.ShapeDtypeStruct(core.shape, jnp.bfloat16),
        name="sum_blocks",
    )(pattern_tile, core, received)


def product_kernel(count, first, has_acc, index, *refs):
    pieces, stacks = refs[:count], refs[count : count + 4]
    acc = refs[count + 4] if has_acc else None
    out, columns, rows, total, column_sem, row_sem, acc_sem, out_sem = refs[-8:]
    mine = pl.multiple_of(index[0] * 512, 512)
    theirs = pl.multiple_of(512 - index[0] * 512, 512)

    for k in range(count):
        pltpu.make_async_copy(pieces[k], columns.at[k], column_sem.at[k]).start()
        for s, (base, at) in enumerate(((1, mine), (9, theirs))):
            tile = index[base + first + k]
            for half in range(2):

                @pl.when(tile >> 2 == half)
                def _(k=k, s=s, at=at, tile=tile, half=half):
                    pltpu.make_async_copy(
                        stacks[2 * s + half].at[tile & 3],
                        rows.at[k, pl.ds(at, 512), :],
                        row_sem.at[k, s],
                    ).start()

    if has_acc:
        load = pltpu.make_async_copy(acc, total, acc_sem)
        load.start()
    else:
        total[...] = jnp.zeros_like(total)

    def arrive(k):
        pltpu.make_async_copy(pieces[0], columns.at[k], column_sem.at[k]).wait()
        for s, at in enumerate((mine, theirs)):
            pltpu.make_async_copy(
                stacks[0].at[0], rows.at[k, pl.ds(at, 512), :], row_sem.at[k, s]
            ).wait()

    if has_acc:
        load.wait()

    @pl.loop(0, count - 1)
    def _(k):
        arrive(k)
        total[...] += jnp.dot(columns[k], rows[k], preferred_element_type=jnp.float32)

    last = count - 1
    arrive(last)
    writes = []
    for p in range(2):
        part = slice(256 * p, 256 * p + 256)
        total[part, :] += jnp.dot(
            columns[last, part, :], rows[last], preferred_element_type=jnp.float32
        )
        writes.append(
            pltpu.make_async_copy(total.at[part, :], out.at[part, :], out_sem.at[p])
        )
        writes[-1].start()
    for write in writes:
        write.wait()


def multiply(index, first, acc, pieces, stacks):
    count = len(pieces)
    given = [] if acc is None else [acc]
    hbm = pl.BlockSpec(memory_space=pl.ANY)
    return pl.pallas_call(
        functools.partial(product_kernel, count, first, acc is not None),
        in_specs=[SMEM] + [hbm] * (count + 4 + len(given)),
        out_specs=hbm,
        scratch_shapes=[
            pltpu.VMEM((count, 512, 1024), jnp.bfloat16),
            pltpu.VMEM((count, 1024, 1024), jnp.bfloat16),
            pltpu.VMEM((512, 1024), jnp.float32),
            pltpu.SemaphoreType.DMA((count,)),
            pltpu.SemaphoreType.DMA((count, 2)),
            pltpu.SemaphoreType.DMA,
            pltpu.SemaphoreType.DMA((2,)),
        ],
        out_shape=jax.ShapeDtypeStruct((512, 1024), jnp.float32),
        name="product",
    )(index, *pieces, *stacks, *given)


def block_mask(values, pattern_tile, block_size):
    row_blocks, col_blocks = pattern_tile.shape
    shaped = values.reshape(row_blocks, block_size, col_blocks, block_size)
    selected = (pattern_tile > 0)[:, None, :, None]
    kept = jnp.where(selected, shaped, jnp.zeros((), values.dtype))
    return kept.reshape(row_blocks * block_size, col_blocks * block_size)


Z_ROUTES = (
    (0, (0, 1), (0, 1)),
    (0, (1, 0), (-1, 0)),
    (0, (-1, 0), (1, 0)),
    (1, (-1, 0), (1, 0)),
    (1, (1, 0), (-1, 0)),
    (2, (1, 0), (-1, 0)),
    (4, (-1, 0), (1, 0)),
)
X_ROUTES = (
    (0, (0, 1), (1, 0)),
    (0, (1, 0), (-1, 0)),
    (0, (-1, 0), (0, 1)),
    (1, (-1, 0), (1, 0)),
    (1, (1, 0), (0, 1)),
    (2, (1, 0), (0, 1)),
    (4, (-1, 0), (0, 1)),
)


def come_from(routes, core):
    found = [(0, 0)]
    for source, *moves in routes:
        steps, cross = moves[core]
        at = found[source]
        found.append(((at[0] - steps) % 4, (at[1] + cross) % 2))
    return found


def tile_at(routes, core):
    found = come_from(routes, core)
    return [found.index((i % 4, i // 4)) for i in range(8)]


def send(array, ring, k):
    _, *moves = (Z_ROUTES if ring == "z" else X_ROUTES)[k]
    axes = ("yl", "z", "c") if ring == "z" else ("c", "x", "yh")
    pairs = []
    for c in range(2):
        steps, cross = moves[c]
        for i in range(4):
            for y in range(2):
                to_i, to_y = (i + steps) % 4, (y + cross) % 2
                if ring == "z":
                    pairs.append(((y * 4 + i) * 2 + c, (to_y * 4 + to_i) * 2 + c))
                else:
                    pairs.append(((c * 4 + i) * 2 + y, (c * 4 + to_i) * 2 + to_y))
    return lax.ppermute(array, axes, pairs)


def steps(
    potential, basis_left, basis_right, core_matrix, density, pattern, pair_atoms, cube_offsets,
    live_count,
):
    x, yh = lax.axis_index("x"), lax.axis_index("yh")
    yl, z, c = lax.axis_index("yl"), lax.axis_index("z"), lax.axis_index("c")

    offsets = cube_offsets.T
    prev_offsets = shift(offsets, ALL, 1)
    next_offsets = shift(offsets, ALL, -1)

    d = [density]
    for k in range(7):
        d.append(send(d[Z_ROUTES[k][0]], "z", k))

    for_prev, for_next = cut_edges(prev_offsets, next_offsets, potential)
    high = shift(for_prev, ALL, -1)
    low = shift(for_next, ALL, 1)
    own = cut_own(offsets, potential)
    outgoing = partial_blocks(
        pair_atoms.T, live_count, offsets, low, own, high, basis_left, basis_right
    )
    received = lax.all_to_all(outgoing, ALL, 0, 0, tiled=True)

    column = lax.axis_index(COL) * ATOM_COLS
    origins = jnp.where(
        c == 0, jnp.array(come_from(Z_ROUTES, 0)), jnp.array(come_from(Z_ROUTES, 1))
    )
    origin_rows = ((((yl + origins[:, 1]) & 1) * 4 + ((z + origins[:, 0]) & 3)) * 2 + c) * ATOM_ROWS

    def masked(tiles, first):
        return jnp.stack(
            [
                block_mask(
                    tile,
                    lax.dynamic_slice(
                        pattern, (origin_rows[first + k], column), (ATOM_ROWS, ATOM_COLS)
                    ),
                    NB,
                )
                for k, tile in enumerate(tiles)
            ]
        )

    early = masked(d[:4], 0)
    early_other = shift(early, "c", 1)

    corner = (lax.axis_index(ROW) * ATOM_ROWS, column)
    pattern_tile = lax.dynamic_slice(pattern, corner, (ATOM_ROWS, ATOM_COLS))
    hamiltonian = hamiltonian_tile(pattern_tile.reshape(-1), core_matrix, received)
    h = [hamiltonian]
    for k in range(7):
        h.append(send(h[X_ROUTES[k][0]], "x", k))

    late_tiles = lax.optimization_barrier((*d[4:], hamiltonian))[:4]
    late = masked(late_tiles, 4)
    late_other = shift(late, "c", 1)
    stacks = (early, late, early_other, late_other)

    sources = jnp.where(c == 0, jnp.array(come_from(X_ROUTES, 0)), jnp.array(come_from(X_ROUTES, 1)))
    block = ((x + sources[:, 0]) & 3) * 2 + ((yh + sources[:, 1]) & 1)
    at = (((block >> 2) + yl) & 1) * 4 + ((block - z) & 3)
    first, second = jnp.array(tile_at(Z_ROUTES, 0)), jnp.array(tile_at(Z_ROUTES, 1))
    hot = (at[:, None] == jnp.arange(8)[None, :]).astype(jnp.int32)
    in_own = jnp.sum(hot * jnp.where(c == 0, first, second)[None, :], axis=1)
    in_other = jnp.sum(hot * jnp.where(c == 0, second, first)[None, :], axis=1)
    index = jnp.concatenate([c.reshape(1), in_own, in_other]).astype(jnp.int32)

    out = multiply(index, 0, None, h[:4], stacks)
    out = multiply(index, 4, out, h[4:7], stacks)
    out = multiply(index, 7, out, h[7:], stacks)
    return hamiltonian, out


def solution(mesh):
    split = Mesh(mesh.devices.reshape(2, 4, 2, 4, 2), ALL)
    placed = (
        P(ALL, None, None),
        P(ALL, None, None),
        P(ALL, None, None),
        P(ROW, COL),
        P(ROW, COL),
        P(),
        P(ALL, None),
        P(ALL, None),
        P(ALL),
    )
    return jax.shard_map(
        steps,
        mesh=split,
        in_specs=placed,
        out_specs=(P(ROW, COL), P(ROW, COL)),
        check_vma=False,
    )
```

time: 275 us -> 267 us (0.971)
  the two profiles are of different devices: /device:TPU:3 before, /device:TPU:1 now
where the time goes in v2:
time: 267 us; the launch traced here: 266 us
  waiting for transfers between devices  129 us (48%)
  starting transfers between devices  50.7 us (19%)
  Pallas kernels  49 us (18%)
  between operations  16.6 us (6%)
  other arithmetic  12.3 us (5%)
  local copies, waits for them, and re-layouts  7.78 us (3%)
    ppermute x14, waiting for transfers between devices, send(): return lax.ppermute(array, axes, pairs)  128 us
    pallas_call x3, Pallas kernels, multiply(): pl.pallas_call(functools.partial(product_kernel, count, first, acc is not...  24.7 us
    ppermute x14, starting transfers between devices, send(): return lax.ppermute(array, axes, pairs)  22.9 us
    ppermute x6, starting transfers between devices, shift(): lax.ppermute(array, axis, [(i, (i + step) % size) for i in range(size)])  17.8 us
    all_to_all x1, starting transfers between devices, steps(): received = lax.all_to_all(outgoing, ALL, 0, 0, tiled=True)  10 us
    select_n x6, other arithmetic, block_mask(): kept = jnp.where(selected, shaped, jnp.zeros((), values.dtype))  8.42 us
    pallas_call x1, Pallas kernels, partial_blocks(): pl.pallas_call(partial_kernel, in_specs=[SMEM] * 3 + [vmem] * 3 + [hbm] *...  7.9 us
    pallas_call x1, Pallas kernels, hamiltonian_tile(): pl.pallas_call(sum_kernel, in_specs=[SMEM, hbm, hbm], out_specs=pl.BlockS...  5.55 us
  transfers between devices with their start and end apart: 21, of which 6 were waited for; matrix products, arithmetic and copies ran while one was open for 6% of the time, Pallas kernels for 11%

profile of v2, /device:TPU:1, one launch (start us, length us, event | category | flops | bytes accessed | tf_op | source)
XLA Modules:
  0.0 265.9 jit_solution(8976535030346088498)
XLA Ops:
  0.6 3.8 %collective-permute-start = (s32[3,64]{1,0:T(4,128)}, s32[3,64]{1,0:T(4,128)S(1)}, u32[]{:S(2)}, u32[]{:S(2)}) collective-permute-start(s32[3,64]{1,0:T(4,128)} %bitcast.85), channel_id=1, source_target_pairs={{0,1},{1,2},{2,3},{3,4},{4,5},{5,6},{6,7},{7,8},{8,9},{9,10},{10,1... | collective-permute-start | bytes 2312 | tf_op jit(solution)/shard_map/ppermute | solution.py:28
  4.4 2.8 %collective-permute-start.1 = (s32[3,64]{1,0:T(4,128)}, s32[3,64]{1,0:T(4,128)S(1)}, u32[]{:S(2)}, u32[]{:S(2)}) collective-permute-start(s32[3,64]{1,0:T(4,128)} %bitcast.86), channel_id=1, source_target_pairs={{0,127},{1,0},{2,1},{3,2},{4,3},{5,4},{6,5},{7,6},{8,7},{9,8},{10,... | collective-permute-start | bytes 2312 | tf_op jit(solution)/shard_map/ppermute | solution.py:28
  7.3 1.4 collective-permute-done.prev_ref
  8.7 0.6 copy-done.8
  9.3 0.6 copy-done.9
  9.8 5.5 %cut_edges.1 = (f32[64,128]{1,0:T(8,128)}, f32[64,128]{1,0:T(8,128)}) custom-call(s32[3,64]{1,0:T(4,128)} %copy-done.8, s32[3,64]{1,0:T(4,128)} %copy-done.9, f32[4,512,512]{2,1,0:T(8,128)} %potential.3), custom_call_target="tpu_custom_call" | custom-call | tf_op jit(solution)/shard_map/cut_edges/pallas_call | solution.py:103
  15.3 1.3 collective-permute-start.2
  16.6 4.1 %collective-permute-start.3 = (f32[64,128]{1,0:T(8,128)}, f32[64,128]{1,0:T(8,128)S(1)}, u32[]{:S(2)}, u32[]{:S(2)}) collective-permute-start(f32[64,128]{1,0:T(8,128)} %get-tuple-element.9), channel_id=1, source_target_pairs={{0,127},{1,0},{2,1},{3,2},{4,3},{5,4},{6,5},{7,6},{8,7},{9,8},{10,... | collective-permute-start | bytes 98312 | tf_op jit(solution)/shard_map/ppermute | solution.py:28
  20.7 5.5 %cut_own.1.own = f32[2,64,128]{2,1,0:T(8,128)} custom-call(s32[3,64]{1,0:T(4,128)} %bitcast.87, f32[4,512,512]{2,1,0:T(8,128)} %potential.3), custom_call_target="tpu_custom_call" | custom-call | tf_op jit(solution)/shard_map/cut_own/pallas_call | solution.py:113
  26.9 0.6 copy-done.5
  27.5 7.9 %partial_blocks.1 = bf16[128,136,128]{2,1,0:T(8,128)(2,1)} custom-call(s32[2,64]{1,0:T(2,128)} %bitcast.89, s32[1]{0:T(128)S(6)} %copy.49.live_ref, s32[3,64]{1,0:T(4,128)} %bitcast.88, f32[64,128]{1,0:T(8,128)} %copy-done.5, f32[2,64,128]{2,1,0:T(8,128)} %cut_own.1.own, f32[64,128]{1,0:T(8,128)} %copy-done.6, bf16[64,128,384]{2,1,0:T(8,128)(2,1)} %left.1, ...), custom_call_target="tpu_custom_call" | custom-call | tf_op jit(solution)/shard_map/partial_blocks/pallas_call | solution.py:186
  35.4 10.0 %all-to-all-start = ((bf16[128,136,128]{2,1,0:T(8,128)(2,1)}), bf16[128,136,128]{2,1,0:T(8,128)(2,1)}, u32[]{:S(2)}, u32[]{:S(2)}) async-start(bf16[128,136,128]{2,1,0:T(8,128)(2,1)} %partial_blocks.1), calls=%async_computation | async-start | bytes 8912896 | tf_op jit(solution)/shard_map/all_to_all | solution.py:421
  45.5 1.4 collective-permute-start.7
  46.9 3.1 %collective-permute-start.8 = (bf16[512,1024]{1,0:T(8,128)(2,1)}, bf16[512,1024]{1,0:T(8,128)(2,1)}, u32[]{:S(2)}, u32[]{:S(2)}) collective-permute-start(bf16[512,1024]{1,0:T(8,128)(2,1)} %param.19), channel_id=1, source_target_pairs={{0,16},{64,80},{16,32},{80,96},{32,48},{96,112},{48,0},{112,64},{8... | collective-permute-start | bytes 3145736 | tf_op jit(solution)/shard_map/ppermute | solution.py:396
  50.1 67.5 %collective-permute-done.7 = bf16[512,1024]{1,0:T(8,128)(2,1)} collective-permute-done((bf16[512,1024]{1,0:T(8,128)(2,1)}, bf16[512,1024]{1,0:T(8,128)(2,1)}, u32[]{:S(2)}, u32[]{:S(2)}) %collective-permute-start.7) | collective-permute-done | bytes 1048608 | tf_op jit(solution)/shard_map/ppermute | solution.py:396
  117.6 1.9 collective-permute-start.10
  119.5 1.4 collective-permute-start.9
  120.9 0.7 fusion.8
  131.6 0.6 reshape.87.pattern_ref
  137.5 1.5 fusion
  139.0 1.4 collective-permute-start.11
  140.4 0.5 collective-permute-start.12
  140.9 1.0 collective-permute-start.13
  142.1 1.5 fusion.1
  143.8 1.5 fusion.2
  145.5 1.5 fusion.3
  147.0 2.3 pad_maximum_fusion.refs_4_.refs_3_.refs_1_
  149.3 5.7 %collective-permute-start.14 = (bf16[4,512,1024]{2,1,0:T(8,128)(2,1)}, bf16[4,512,1024]{2,1,0:T(8,128)(2,1)}, u32[]{:S(2)}, u32[]{:S(2)}) collective-permute-start(bf16[4,512,1024]{2,1,0:T(8,128)(2,1)} %pad_maximum_fusion.refs_4_.refs_3_.refs_1_), channel_id=1, source_target_pairs={{0,8},{8,0},{1,9},{9,1},{2,10},{10,2},{3,11},{11,3},{4,12},{12,4},... | collective-permute-start | bytes 12582920 | tf_op jit(solution)/shard_map/ppermute | solution.py:28
  155.0 5.6 %sum_blocks.1.refs_0_ = bf16[512,1024]{1,0:T(8,128)(2,1)} custom-call(s32[32]{0:T(128)} %reshape.87.pattern_ref, bf16[512,1024]{1,0:T(8,128)(2,1)} %core.1, bf16[128,136,128]{2,1,0:T(8,128)(2,1)} %all-to-all-done.received), custom_call_target="tpu_custom_call" | custom-call | tf_op jit(solution)/shard_map/sum_blocks/pallas_call | solution.py:244
  160.5 4.0 %collective-permute-done.11 = bf16[512,1024]{1,0:T(8,128)(2,1)S(1)} collective-permute-done((bf16[512,1024]{1,0:T(8,128)(2,1)}, bf16[512,1024]{1,0:T(8,128)(2,1)S(1)}, u32[]{:S(2)}, u32[]{:S(2)}) %collective-permute-start.11) | collective-permute-done | bytes 1048608 | tf_op jit(solution)/shard_map/ppermute | solution.py:396
  164.5 15.0 %collective-permute-done.12 = bf16[512,1024]{1,0:T(8,128)(2,1)S(1)} collective-permute-done((bf16[512,1024]{1,0:T(8,128)(2,1)}, bf16[512,1024]{1,0:T(8,128)(2,1)S(1)}, u32[]{:S(2)}, u32[]{:S(2)}) %collective-permute-start.12) | collective-permute-done | bytes 1048608 | tf_op jit(solution)/shard_map/ppermute | solution.py:396
  180.0 0.6 fusion.4
  181.0 1.8 fusion.6
  182.9 0.6 pad_maximum_fusion.1.refs_5_.refs_4_.refs_2_
  183.5 2.0 copy-done
  185.5 1.6 collective-permute-start.4
  187.0 1.9 collective-permute-start.17
  188.9 20.8 %collective-permute-done.4.refs_1_ = bf16[512,1024]{1,0:T(8,128)(2,1)S(1)} collective-permute-done((bf16[512,1024]{1,0:T(8,128)(2,1)S(1)}, bf16[512,1024]{1,0:T(8,128)(2,1)S(1)}, u32[]{:S(2)}, u32[]{:S(2)}) %collective-permute-start.4) | collective-permute-done | bytes 1048608 | tf_op jit(solution)/shard_map/ppermute | solution.py:396
  210.1 2.5 collective-permute-start.19
  212.6 0.5 collective-permute-start.16
  213.1 2.5 collective-permute-start.18
  215.6 20.7 %collective-permute-done.5.refs_0_ = bf16[512,1024]{1,0:T(8,128)(2,1)} collective-permute-done((bf16[512,1024]{1,0:T(8,128)(2,1)S(1)}, bf16[512,1024]{1,0:T(8,128)(2,1)}, u32[]{:S(2)}, u32[]{:S(2)}) %collective-permute-start.5) | collective-permute-done | bytes 1048608 | tf_op jit(solution)/shard_map/ppermute | solution.py:396
  236.3 2.8 %collective-permute-start.6 = (bf16[512,1024]{1,0:T(8,128)(2,1)}, bf16[512,1024]{1,0:T(8,128)(2,1)}, u32[]{:S(2)}, u32[]{:S(2)}) collective-permute-start(bf16[512,1024]{1,0:T(8,128)(2,1)} %collective-permute-done.5.refs_0_), channel_id=1, source_target_pairs={{0,6},{1,7},{2,0},{3,1},{4,2},{5,3},{6,4},{7,5},{8,9},{9,8},{10,11... | collective-permute-start | bytes 3145736 | tf_op jit(solution)/shard_map/ppermute | solution.py:396
  239.3 0.7 pad_add_fusion.index
  240.0 1.0 copy-done.4
  241.0 9.6 %product.3.refs_7_ = f32[512,1024]{1,0:T(8,128)} custom-call(s32[17]{0:T(128)} %pad_add_fusion.index, bf16[512,1024]{1,0:T(8,128)(2,1)} %sum_blocks.1.refs_0_, bf16[512,1024]{1,0:T(8,128)(2,1)} %copy-done.2, bf16[512,1024]{1,0:T(8,128)(2,1)} %copy-done.3, bf16[512,1024]{1,0:T(8,128)(2,1)} %copy-done.4, ...), custom_call_target="tpu_custom_call" | custom-call | tf_op jit(solution)/shard_map/product/pallas_call | solution.py:323
  250.6 9.6 %product.4.refs_5_ = f32[512,1024]{1,0:T(8,128)} custom-call(s32[17]{0:T(128)} %pad_add_fusion.index, bf16[512,1024]{1,0:T(8,128)(2,1)} %collective-permute-done.5.refs_0_, bf16[512,1024]{1,0:T(8,128)(2,1)} %collective-permute-done.16.refs_1_, bf16[512,1024]{1,0:T(8,128)(2,1)} %collective-permute-done.18.refs_2_, ...), custom_call_target="tpu_custom_call" | custom-call | tf_op jit(solution)/shard_map/product/pallas_call | solution.py:323
  260.3 5.4 %product.5 = f32[512,1024]{1,0:T(8,128)} custom-call(s32[17]{0:T(128)} %pad_add_fusion.index, bf16[512,1024]{1,0:T(8,128)(2,1)} %collective-permute-done.6.refs_0_, bf16[4,512,1024]{2,1,0:T(8,128)(2,1)} %pad_maximum_fusion.refs_4_.refs_3_.refs_1_, bf16[4,512,1024]{2,1,0:T(8,128)(2,1)} %copy-done, ...), custom_call_target="tpu_custom_call" | custom-call | tf_op jit(solution)/shard_map/product/pallas_call | solution.py:323
  (57 shorter events, 2.7 us)
Async XLA Ops:
  0.6 8.0 %collective-permute-start = (s32[3,64]{1,0:T(4,128)}, s32[3,64]{1,0:T(4,128)S(1)}, u32[]{:S(2)}, u32[]{:S(2)}) collective-permute-start(s32[3,64]{1,0:T(4,128)} %bitcast.85), channel_id=1, source_target_pairs={{0,1},{1,2},{2,3},{3,4},{4,5},{5,6},{6,7},{7,8},{8,9},{9,10},{10,1... | collective-permute-start | bytes 2312 | tf_op jit(solution)/shard_map/ppermute | solution.py:28
  4.4 4.2 %collective-permute-start.1 = (s32[3,64]{1,0:T(4,128)}, s32[3,64]{1,0:T(4,128)S(1)}, u32[]{:S(2)}, u32[]{:S(2)}) collective-permute-start(s32[3,64]{1,0:T(4,128)} %bitcast.86), channel_id=1, source_target_pairs={{0,127},{1,0},{2,1},{3,2},{4,3},{5,4},{6,5},{7,6},{8,7},{9,8},{10,... | collective-permute-start | bytes 2312 | tf_op jit(solution)/shard_map/ppermute | solution.py:28
  8.7 0.6 copy-start.8
  9.2 0.6 copy-start.9
  15.3 11.6 %collective-permute-start.2 = (f32[64,128]{1,0:T(8,128)}, f32[64,128]{1,0:T(8,128)S(1)}, u32[]{:S(2)}, u32[]{:S(2)}) collective-permute-start(f32[64,128]{1,0:T(8,128)} %get-tuple-element.8), channel_id=1, source_target_pairs={{0,1},{1,2},{2,3},{3,4},{4,5},{5,6},{6,7},{7,8},{8,9},{9,10},{10,1... | collective-permute-start | bytes 98312 | tf_op jit(solution)/shard_map/ppermute | solution.py:28
  16.6 10.3 %collective-permute-start.3 = (f32[64,128]{1,0:T(8,128)}, f32[64,128]{1,0:T(8,128)S(1)}, u32[]{:S(2)}, u32[]{:S(2)}) collective-permute-start(f32[64,128]{1,0:T(8,128)} %get-tuple-element.9), channel_id=1, source_target_pairs={{0,127},{1,0},{2,1},{3,2},{4,3},{5,4},{6,5},{7,6},{8,7},{9,8},{10,... | collective-permute-start | bytes 98312 | tf_op jit(solution)/shard_map/ppermute | solution.py:28
  26.9 0.6 copy-start.5
  26.9 0.6 copy-start.6
  35.4 85.5 %copy-start.10 = (s32[8,2]{0,1:T(2,128)S(1)}, s32[8,2]{0,1:T(2,128)}, u32[]{:S(2)}) copy-start(s32[8,2]{0,1:T(2,128)} %constant.50.clone) | copy-start | bytes 196
  35.4 85.4 %copy-start.11 = (s32[8,2]{0,1:T(2,128)S(1)}, s32[8,2]{0,1:T(2,128)}, u32[]{:S(2)}) copy-start(s32[8,2]{0,1:T(2,128)} %constant.51.clone) | copy-start | bytes 196
  35.4 85.4 %copy-start.12 = (s32[8,2]{0,1:T(2,128)S(1)}, s32[8,2]{0,1:T(2,128)}, u32[]{:S(2)}) copy-start(s32[8,2]{0,1:T(2,128)} %constant.52.clone) | copy-start | bytes 196
  35.4 96.1 %copy-start.7 = (s32[64,64]{1,0:T(8,128)S(1)}, s32[64,64]{1,0:T(8,128)}, u32[]{:S(2)}) copy-start(s32[64,64]{1,0:T(8,128)} %param.20) | copy-start | bytes 49156
  35.4 119.5 %all-to-all-start = ((bf16[128,136,128]{2,1,0:T(8,128)(2,1)}), bf16[128,136,128]{2,1,0:T(8,128)(2,1)}, u32[]{:S(2)}, u32[]{:S(2)}) async-start(bf16[128,136,128]{2,1,0:T(8,128)(2,1)} %partial_blocks.1), calls=%async_computation | async-start | bytes 8912896 | tf_op jit(solution)/shard_map/all_to_all | solution.py:421
  45.5 72.1 %collective-permute-start.7 = (bf16[512,1024]{1,0:T(8,128)(2,1)}, bf16[512,1024]{1,0:T(8,128)(2,1)}, u32[]{:S(2)}, u32[]{:S(2)}) collective-permute-start(bf16[512,1024]{1,0:T(8,128)(2,1)} %param.19), channel_id=1, source_target_pairs={{0,64},{64,0},{16,80},{80,16},{32,96},{96,32},{48,112},{112,48},{8... | collective-permute-start | bytes 3145736 | tf_op jit(solution)/shard_map/ppermute | solution.py:396
  46.9 93.4 %collective-permute-start.8 = (bf16[512,1024]{1,0:T(8,128)(2,1)}, bf16[512,1024]{1,0:T(8,128)(2,1)}, u32[]{:S(2)}, u32[]{:S(2)}) collective-permute-start(bf16[512,1024]{1,0:T(8,128)(2,1)} %param.19), channel_id=1, source_target_pairs={{0,16},{64,80},{16,32},{80,96},{32,48},{96,112},{48,0},{112,64},{8... | collective-permute-start | bytes 3145736 | tf_op jit(solution)/shard_map/ppermute | solution.py:396
  117.6 23.3 %collective-permute-start.10 = (bf16[512,1024]{1,0:T(8,128)(2,1)}, bf16[512,1024]{1,0:T(8,128)(2,1)S(1)}, u32[]{:S(2)}, u32[]{:S(2)}) collective-permute-start(bf16[512,1024]{1,0:T(8,128)(2,1)} %collective-permute-done.7), channel_id=1, source_target_pairs={{0,48},{64,112},{16,0},{80,64},{32,16},{96,80},{48,32},{112,96},{8... | collective-permute-start | bytes 3145736 | tf_op jit(solution)/shard_map/ppermute | solution.py:396
  119.5 25.8 %collective-permute-start.9 = (bf16[512,1024]{1,0:T(8,128)(2,1)}, bf16[512,1024]{1,0:T(8,128)(2,1)}, u32[]{:S(2)}, u32[]{:S(2)}) collective-permute-start(bf16[512,1024]{1,0:T(8,128)(2,1)} %param.19), channel_id=1, source_target_pairs={{0,48},{64,112},{16,0},{80,64},{32,16},{96,80},{48,32},{112,96},{8... | collective-permute-start | bytes 3145736 | tf_op jit(solution)/shard_map/ppermute | solution.py:396
  139.0 25.6 %collective-permute-start.11 = (bf16[512,1024]{1,0:T(8,128)(2,1)}, bf16[512,1024]{1,0:T(8,128)(2,1)S(1)}, u32[]{:S(2)}, u32[]{:S(2)}) collective-permute-start(bf16[512,1024]{1,0:T(8,128)(2,1)} %collective-permute-done.7), channel_id=1, source_target_pairs={{0,16},{64,80},{16,32},{80,96},{32,48},{96,112},{48,0},{112,64},{8... | collective-permute-start | bytes 3145736 | tf_op jit(solution)/shard_map/ppermute | solution.py:396
  140.4 39.2 %collective-permute-start.12 = (bf16[512,1024]{1,0:T(8,128)(2,1)}, bf16[512,1024]{1,0:T(8,128)(2,1)S(1)}, u32[]{:S(2)}, u32[]{:S(2)}) collective-permute-start(bf16[512,1024]{1,0:T(8,128)(2,1)} %collective-permute-done.8), channel_id=1, source_target_pairs={{0,16},{64,80},{16,32},{80,96},{32,48},{96,112},{48,0},{112,64},{8... | collective-permute-start | bytes 3145736 | tf_op jit(solution)/shard_map/ppermute | solution.py:396
  140.9 38.7 %collective-permute-start.13 = (bf16[512,1024]{1,0:T(8,128)(2,1)S(1)}, bf16[512,1024]{1,0:T(8,128)(2,1)}, u32[]{:S(2)}, u32[]{:S(2)}) collective-permute-start(bf16[512,1024]{1,0:T(8,128)(2,1)S(1)} %collective-permute-done.10), channel_id=1, source_target_pairs={{0,48},{64,112},{16,0},{80,64},{32,16},{96,80},{48,32},{112,96},{8... | collective-permute-start | bytes 3145736 | tf_op jit(solution)/shard_map/ppermute | solution.py:396
  149.3 63.3 %collective-permute-start.14 = (bf16[4,512,1024]{2,1,0:T(8,128)(2,1)}, bf16[4,512,1024]{2,1,0:T(8,128)(2,1)}, u32[]{:S(2)}, u32[]{:S(2)}) collective-permute-start(bf16[4,512,1024]{2,1,0:T(8,128)(2,1)} %pad_maximum_fusion.refs_4_.refs_3_.refs_1_), channel_id=1, source_target_pairs={{0,8},{8,0},{1,9},{9,1},{2,10},{10,2},{3,11},{11,3},{4,12},{12,4},... | collective-permute-start | bytes 12582920 | tf_op jit(solution)/shard_map/ppermute | solution.py:28
  182.9 2.6 copy-start.1
  182.9 56.3 %copy-start.13 = (s32[8]{0:T(128)S(1)}, s32[8]{0:T(128)}, u32[]{:S(2)}) copy-start(s32[8]{0:T(128)} %constant.53.clone) | copy-start | bytes 100
  182.9 56.3 %copy-start.14 = (s32[8]{0:T(128)S(1)}, s32[8]{0:T(128)}, u32[]{:S(2)}) copy-start(s32[8]{0:T(128)} %constant.54.clone) | copy-start | bytes 100
  183.5 2.0 copy-start
  185.5 55.5 %collective-permute-start.15 = (bf16[4,512,1024]{2,1,0:T(8,128)(2,1)S(1)}, bf16[4,512,1024]{2,1,0:T(8,128)(2,1)}, u32[]{:S(2)}, u32[]{:S(2)}) collective-permute-start(bf16[4,512,1024]{2,1,0:T(8,128)(2,1)S(1)} %pad_maximum_fusion.1.refs_5_.refs_4_.refs_2_), channel_id=1, source_target_pairs={{0,8},{8,0},{1,9},{9,1},{2,10},{10,2},{3,11},{11,3},{4,12},{12,4},... | collective-permute-start | bytes 12582920 | tf_op jit(solution)/shard_map/ppermute | solution.py:28
  185.5 24.2 %collective-permute-start.4 = (bf16[512,1024]{1,0:T(8,128)(2,1)S(1)}, bf16[512,1024]{1,0:T(8,128)(2,1)S(1)}, u32[]{:S(2)}, u32[]{:S(2)}) collective-permute-start(bf16[512,1024]{1,0:T(8,128)(2,1)S(1)} %copy-done.1), channel_id=1, source_target_pairs={{0,1},{1,0},{2,3},{3,2},{4,5},{5,4},{6,7},{7,6},{8,10},{9,11},{10,... | collective-permute-start | bytes 3145736 | tf_op jit(solution)/shard_map/ppermute | solution.py:396
  187.0 26.1 %collective-permute-start.17 = (bf16[512,1024]{1,0:T(8,128)(2,1)S(1)}, bf16[512,1024]{1,0:T(8,128)(2,1)S(1)}, u32[]{:S(2)}, u32[]{:S(2)}) collective-permute-start(bf16[512,1024]{1,0:T(8,128)(2,1)S(1)} %copy-done.1), channel_id=1, source_target_pairs={{0,2},{1,3},{2,4},{3,5},{4,6},{5,7},{6,0},{7,1},{8,14},{9,15},{10,... | collective-permute-start | bytes 3145736 | tf_op jit(solution)/shard_map/ppermute | solution.py:396
  209.7 31.3 %copy-start.2 = (bf16[512,1024]{1,0:T(8,128)(2,1)}, bf16[512,1024]{1,0:T(8,128)(2,1)S(1)}, u32[]{:S(2)}) copy-start(bf16[512,1024]{1,0:T(8,128)(2,1)S(1)} %collective-permute-done.4.refs_1_) | copy-start | bytes 3145732
  209.7 26.6 %collective-permute-start.5 = (bf16[512,1024]{1,0:T(8,128)(2,1)S(1)}, bf16[512,1024]{1,0:T(8,128)(2,1)}, u32[]{:S(2)}, u32[]{:S(2)}) collective-permute-start(bf16[512,1024]{1,0:T(8,128)(2,1)S(1)} %collective-permute-done.4.refs_1_), channel_id=1, source_target_pairs={{0,6},{1,7},{2,0},{3,1},{4,2},{5,3},{6,4},{7,5},{8,10},{9,11},{10,... | collective-permute-start | bytes 3145736 | tf_op jit(solution)/shard_map/ppermute | solution.py:396
  210.1 29.9 %collective-permute-start.19 = (bf16[512,1024]{1,0:T(8,128)(2,1)S(1)}, bf16[512,1024]{1,0:T(8,128)(2,1)S(1)}, u32[]{:S(2)}, u32[]{:S(2)}) collective-permute-start(bf16[512,1024]{1,0:T(8,128)(2,1)S(1)} %copy-done.1), channel_id=1, source_target_pairs={{0,6},{1,7},{2,0},{3,1},{4,2},{5,3},{6,4},{7,5},{8,9},{9,8},{10,11... | collective-permute-start | bytes 3145736 | tf_op jit(solution)/shard_map/ppermute | solution.py:396
  212.6 38.0 %collective-permute-start.16 = (bf16[512,1024]{1,0:T(8,128)(2,1)S(1)}, bf16[512,1024]{1,0:T(8,128)(2,1)}, u32[]{:S(2)}, u32[]{:S(2)}) collective-permute-start(bf16[512,1024]{1,0:T(8,128)(2,1)S(1)} %collective-permute-done.4.refs_1_), channel_id=1, source_target_pairs={{0,2},{1,3},{2,4},{3,5},{4,6},{5,7},{6,0},{7,1},{8,9},{9,8},{10,11... | collective-permute-start | bytes 3145736 | tf_op jit(solution)/shard_map/ppermute | solution.py:396
  213.1 27.9 %copy-start.3 = (bf16[512,1024]{1,0:T(8,128)(2,1)}, bf16[512,1024]{1,0:T(8,128)(2,1)S(1)}, u32[]{:S(2)}) copy-start(bf16[512,1024]{1,0:T(8,128)(2,1)S(1)} %collective-permute-done.17.refs_2_) | copy-start | bytes 3145732
  213.1 37.5 %collective-permute-start.18 = (bf16[512,1024]{1,0:T(8,128)(2,1)S(1)}, bf16[512,1024]{1,0:T(8,128)(2,1)}, u32[]{:S(2)}, u32[]{:S(2)}) collective-permute-start(bf16[512,1024]{1,0:T(8,128)(2,1)S(1)} %collective-permute-done.17.refs_2_), channel_id=1, source_target_pairs={{0,2},{1,3},{2,4},{3,5},{4,6},{5,7},{6,0},{7,1},{8,9},{9,8},{10,11... | collective-permute-start | bytes 3145736 | tf_op jit(solution)/shard_map/ppermute | solution.py:396
  236.3 24.0 %collective-permute-start.6 = (bf16[512,1024]{1,0:T(8,128)(2,1)}, bf16[512,1024]{1,0:T(8,128)(2,1)}, u32[]{:S(2)}, u32[]{:S(2)}) collective-permute-start(bf16[512,1024]{1,0:T(8,128)(2,1)} %collective-permute-done.5.refs_0_), channel_id=1, source_target_pairs={{0,6},{1,7},{2,0},{3,1},{4,2},{5,3},{6,4},{7,5},{8,9},{9,8},{10,11... | collective-permute-start | bytes 3145736 | tf_op jit(solution)/shard_map/ppermute | solution.py:396
  240.0 1.0 copy-start.4

commit v3 on v2

--- a/solution.py
+++ b/solution.py
@@ -322,7 +322,9 @@
     hbm = pl.BlockSpec(memory_space=pl.ANY)
     return pl.pallas_call(
         functools.partial(product_kernel, count, first, acc is not None),
-        in_specs=[SMEM] + [hbm] * (count + 4 + len(given)),
+        in_specs=[SMEM]
+        + [pl.BlockSpec(memory_space=pltpu.HBM)] * (count + 4)
+        + [hbm] * len(given),
         out_specs=hbm,
         scratch_shapes=[
             pltpu.VMEM((count, 512, 1024), jnp.bfloat16),
@@ -357,11 +359,11 @@
 )
 X_ROUTES = (
     (0, (0, 1), (1, 0)),
-    (0, (1, 0), (-1, 0)),
-    (0, (-1, 0), (0, 1)),
+    (0, (-1, 0), (-1, 0)),
+    (0, (1, 0), (0, 1)),
     (1, (-1, 0), (1, 0)),
     (1, (1, 0), (0, 1)),
-    (2, (1, 0), (0, 1)),
+    (2, (-1, 0), (0, 1)),
     (4, (-1, 0), (0, 1)),
 )
 

time: 267 us -> 259 us (0.970)
  the two profiles are of different devices: /device:TPU:1 before, /device:TPU:0 now
where the time goes in v3:
time: 259 us; the launch traced here: 256 us
  waiting for transfers between devices  120 us (46%)
  starting transfers between devices  50 us (19%)
  Pallas kernels  49 us (19%)
  between operations  16.6 us (6%)
  other arithmetic  12.2 us (5%)
  local copies, waits for them, and re-layouts  7.71 us (3%)
    ppermute x14, waiting for transfers between devices, send(): return lax.ppermute(array, axes, pairs)  118 us
    ppermute x14, starting transfers between devices, send(): return lax.ppermute(array, axes, pairs)  27.3 us
    pallas_call x3, Pallas kernels, multiply(): pl.pallas_call(functools.partial(product_kernel, count, first, acc is not...  24.7 us
    ppermute x6, starting transfers between devices, shift(): lax.ppermute(array, axis, [(i, (i + step) % size) for i in range(size)])  16.4 us
    select_n x8, other arithmetic, block_mask(): kept = jnp.where(selected, shaped, jnp.zeros((), values.dtype))  8.36 us
    pallas_call x1, Pallas kernels, partial_blocks(): pl.pallas_call(partial_kernel, in_specs=[SMEM] * 3 + [vmem] * 3 + [hbm] *...  7.9 us
    all_to_all x1, starting transfers between devices, steps(): received = lax.all_to_all(outgoing, ALL, 0, 0, tiled=True)  6.23 us
    pallas_call x1, Pallas kernels, hamiltonian_tile(): pl.pallas_call(sum_kernel, in_specs=[SMEM, hbm, hbm], out_specs=pl.BlockS...  5.55 us
  transfers between devices with their start and end apart: 21, of which 10 were waited for; matrix products, arithmetic and copies ran while one was open for 6% of the time, Pallas kernels for 12%

profile of v3, /device:TPU:0, one launch (start us, length us, event | category | flops | bytes accessed | tf_op | source)
XLA Modules:
  0.0 255.6 jit_solution(16075630771848980758)
XLA Ops:
  0.6 3.4 %collective-permute-start = (s32[3,64]{1,0:T(4,128)}, s32[3,64]{1,0:T(4,128)S(1)}, u32[]{:S(2)}, u32[]{:S(2)}) collective-permute-start(s32[3,64]{1,0:T(4,128)} %bitcast.85), channel_id=1, source_target_pairs={{0,1},{1,2},{2,3},{3,4},{4,5},{5,6},{6,7},{7,8},{8,9},{9,10},{10,1... | collective-permute-start | bytes 2312 | tf_op jit(solution)/shard_map/ppermute | solution.py:28
  4.0 5.0 %collective-permute-start.1 = (s32[3,64]{1,0:T(4,128)}, s32[3,64]{1,0:T(4,128)S(1)}, u32[]{:S(2)}, u32[]{:S(2)}) collective-permute-start(s32[3,64]{1,0:T(4,128)} %bitcast.86), channel_id=1, source_target_pairs={{0,127},{1,0},{2,1},{3,2},{4,3},{5,4},{6,5},{7,6},{8,7},{9,8},{10,... | collective-permute-start | bytes 2312 | tf_op jit(solution)/shard_map/ppermute | solution.py:28
  9.0 1.4 collective-permute-done.prev_ref
  11.0 0.6 copy-done.10
  11.6 5.5 %cut_edges.1 = (f32[64,128]{1,0:T(8,128)}, f32[64,128]{1,0:T(8,128)}) custom-call(s32[3,64]{1,0:T(4,128)} %copy-done.9, s32[3,64]{1,0:T(4,128)} %copy-done.10, f32[4,512,512]{2,1,0:T(8,128)} %potential.3), custom_call_target="tpu_custom_call" | custom-call | tf_op jit(solution)/shard_map/cut_edges/pallas_call | solution.py:103
  17.0 0.6 collective-permute-start.2
  17.6 6.7 %collective-permute-start.3 = (f32[64,128]{1,0:T(8,128)}, f32[64,128]{1,0:T(8,128)S(1)}, u32[]{:S(2)}, u32[]{:S(2)}) collective-permute-start(f32[64,128]{1,0:T(8,128)} %get-tuple-element.9), channel_id=1, source_target_pairs={{0,127},{1,0},{2,1},{3,2},{4,3},{5,4},{6,5},{7,6},{8,7},{9,8},{10,... | collective-permute-start | bytes 98312 | tf_op jit(solution)/shard_map/ppermute | solution.py:28
  24.3 5.5 %cut_own.1.own = f32[2,64,128]{2,1,0:T(8,128)} custom-call(s32[3,64]{1,0:T(4,128)} %bitcast.87, f32[4,512,512]{2,1,0:T(8,128)} %potential.3), custom_call_target="tpu_custom_call" | custom-call | tf_op jit(solution)/shard_map/cut_own/pallas_call | solution.py:113
  30.4 0.6 copy-done.6
  31.1 7.9 %partial_blocks.1 = bf16[128,136,128]{2,1,0:T(8,128)(2,1)} custom-call(s32[2,64]{1,0:T(2,128)} %bitcast.89, s32[1]{0:T(128)S(6)} %copy.49.live_ref, s32[3,64]{1,0:T(4,128)} %bitcast.88, f32[64,128]{1,0:T(8,128)} %copy-done.6, f32[2,64,128]{2,1,0:T(8,128)} %cut_own.1.own, f32[64,128]{1,0:T(8,128)} %copy-done.7, bf16[64,128,384]{2,1,0:T(8,128)(2,1)} %left.1, ...), custom_call_target="tpu_custom_call" | custom-call | tf_op jit(solution)/shard_map/partial_blocks/pallas_call | solution.py:186
  39.0 6.2 %all-to-all-start = ((bf16[128,136,128]{2,1,0:T(8,128)(2,1)}), bf16[128,136,128]{2,1,0:T(8,128)(2,1)}, u32[]{:S(2)}, u32[]{:S(2)}) async-start(bf16[128,136,128]{2,1,0:T(8,128)(2,1)} %partial_blocks.1), calls=%async_computation | async-start | bytes 8912896 | tf_op jit(solution)/shard_map/all_to_all | solution.py:423
  45.3 1.0 collective-permute-start.7
  46.3 1.6 collective-permute-start.8
  47.9 69.2 %collective-permute-done.7 = bf16[512,1024]{1,0:T(8,128)(2,1)S(1)} collective-permute-done((bf16[512,1024]{1,0:T(8,128)(2,1)S(1)}, bf16[512,1024]{1,0:T(8,128)(2,1)S(1)}, u32[]{:S(2)}, u32[]{:S(2)}) %collective-permute-start.7) | collective-permute-done | bytes 1048608 | tf_op jit(solution)/shard_map/ppermute | solution.py:398
  117.1 3.9 %collective-permute-start.10 = (bf16[512,1024]{1,0:T(8,128)(2,1)S(1)}, bf16[512,1024]{1,0:T(8,128)(2,1)S(1)}, u32[]{:S(2)}, u32[]{:S(2)}) collective-permute-start(bf16[512,1024]{1,0:T(8,128)(2,1)S(1)} %collective-permute-done.7), channel_id=1, source_target_pairs={{0,48},{64,112},{16,0},{80,64},{32,16},{96,80},{48,32},{112,96},{8... | collective-permute-start | bytes 3145736 | tf_op jit(solution)/shard_map/ppermute | solution.py:398
  121.0 0.6 collective-permute-start.9
  121.6 0.7 fusion.8
  132.3 0.7 reshape.87.pattern_ref
  138.5 1.5 collective-permute-start.11
  140.1 3.1 %collective-permute-start.13 = (bf16[512,1024]{1,0:T(8,128)(2,1)S(1)}, bf16[512,1024]{1,0:T(8,128)(2,1)}, u32[]{:S(2)}, u32[]{:S(2)}) collective-permute-start(bf16[512,1024]{1,0:T(8,128)(2,1)S(1)} %collective-permute-done.10), channel_id=1, source_target_pairs={{0,48},{64,112},{16,0},{80,64},{32,16},{96,80},{48,32},{112,96},{8... | collective-permute-start | bytes 3145736 | tf_op jit(solution)/shard_map/ppermute | solution.py:398
  144.0 1.5 fusion.2
  145.5 4.9 %collective-permute-done.9 = bf16[512,1024]{1,0:T(8,128)(2,1)} collective-permute-done((bf16[512,1024]{1,0:T(8,128)(2,1)S(1)}, bf16[512,1024]{1,0:T(8,128)(2,1)}, u32[]{:S(2)}, u32[]{:S(2)}) %collective-permute-start.9) | collective-permute-done | bytes 1048608 | tf_op jit(solution)/shard_map/ppermute | solution.py:398
  150.6 1.5 fusion.3
  152.1 2.3 pad_maximum_fusion.refs_4_.refs_3_.refs_1_
  154.4 5.6 %sum_blocks.1.refs_0_ = bf16[512,1024]{1,0:T(8,128)(2,1)} custom-call(s32[32]{0:T(128)} %reshape.87.pattern_ref, bf16[512,1024]{1,0:T(8,128)(2,1)} %core.1, bf16[128,136,128]{2,1,0:T(8,128)(2,1)} %all-to-all-done.received), custom_call_target="tpu_custom_call" | custom-call | tf_op jit(solution)/shard_map/sum_blocks/pallas_call | solution.py:244
  159.9 6.0 %collective-permute-done.11 = bf16[512,1024]{1,0:T(8,128)(2,1)} collective-permute-done((bf16[512,1024]{1,0:T(8,128)(2,1)S(1)}, bf16[512,1024]{1,0:T(8,128)(2,1)}, u32[]{:S(2)}, u32[]{:S(2)}) %collective-permute-start.11) | collective-permute-done | bytes 1048608 | tf_op jit(solution)/shard_map/ppermute | solution.py:398
  165.9 11.7 %collective-permute-done.12 = bf16[512,1024]{1,0:T(8,128)(2,1)} collective-permute-done((bf16[512,1024]{1,0:T(8,128)(2,1)}, bf16[512,1024]{1,0:T(8,128)(2,1)}, u32[]{:S(2)}, u32[]{:S(2)}) %collective-permute-start.12) | collective-permute-done | bytes 1048608 | tf_op jit(solution)/shard_map/ppermute | solution.py:398
  178.3 1.5 fusion.5
  180.1 1.5 fusion.6
  181.8 1.5 fusion.7
  183.3 0.6 pad_maximum_fusion.1.refs_5_.refs_4_.refs_2_
  183.9 2.0 copy-done
  185.9 0.8 collective-permute-start.15
  186.7 2.8 %collective-permute-start.4 = (bf16[512,1024]{1,0:T(8,128)(2,1)S(1)}, bf16[512,1024]{1,0:T(8,128)(2,1)S(1)}, u32[]{:S(2)}, u32[]{:S(2)}) collective-permute-start(bf16[512,1024]{1,0:T(8,128)(2,1)S(1)} %copy-done.1), channel_id=1, source_target_pairs={{0,1},{1,0},{2,3},{3,2},{4,5},{5,4},{6,7},{7,6},{8,10},{9,11},{10,... | collective-permute-start | bytes 3145736 | tf_op jit(solution)/shard_map/ppermute | solution.py:398
  189.5 1.9 collective-permute-start.17
  191.3 11.7 %collective-permute-done.4.refs_1_ = bf16[512,1024]{1,0:T(8,128)(2,1)S(1)} collective-permute-done((bf16[512,1024]{1,0:T(8,128)(2,1)S(1)}, bf16[512,1024]{1,0:T(8,128)(2,1)S(1)}, u32[]{:S(2)}, u32[]{:S(2)}) %collective-permute-start.4) | collective-permute-done | bytes 1048608 | tf_op jit(solution)/shard_map/ppermute | solution.py:398
  203.0 3.3 %collective-permute-start.5 = (bf16[512,1024]{1,0:T(8,128)(2,1)S(1)}, bf16[512,1024]{1,0:T(8,128)(2,1)}, u32[]{:S(2)}, u32[]{:S(2)}) collective-permute-start(bf16[512,1024]{1,0:T(8,128)(2,1)S(1)} %collective-permute-done.4.refs_1_), channel_id=1, source_target_pairs={{0,6},{1,7},{2,0},{3,1},{4,2},{5,3},{6,4},{7,5},{8,10},{9,11},{10,... | collective-permute-start | bytes 3145736 | tf_op jit(solution)/shard_map/ppermute | solution.py:398
  206.3 0.5 collective-permute-start.16
  206.9 6.5 %collective-permute-done.17.refs_2_ = bf16[512,1024]{1,0:T(8,128)(2,1)S(1)} collective-permute-done((bf16[512,1024]{1,0:T(8,128)(2,1)S(1)}, bf16[512,1024]{1,0:T(8,128)(2,1)S(1)}, u32[]{:S(2)}, u32[]{:S(2)}) %collective-permute-start.17) | collective-permute-done | bytes 1048608 | tf_op jit(solution)/shard_map/ppermute | solution.py:398
  213.3 3.5 %collective-permute-start.18 = (bf16[512,1024]{1,0:T(8,128)(2,1)S(1)}, bf16[512,1024]{1,0:T(8,128)(2,1)}, u32[]{:S(2)}, u32[]{:S(2)}) collective-permute-start(bf16[512,1024]{1,0:T(8,128)(2,1)S(1)} %collective-permute-done.17.refs_2_), channel_id=1, source_target_pairs={{0,6},{1,7},{2,0},{3,1},{4,2},{5,3},{6,4},{7,5},{8,9},{9,8},{10,11... | collective-permute-start | bytes 3145736 | tf_op jit(solution)/shard_map/ppermute | solution.py:398
  216.8 7.8 %collective-permute-done.5.refs_0_ = bf16[512,1024]{1,0:T(8,128)(2,1)} collective-permute-done((bf16[512,1024]{1,0:T(8,128)(2,1)S(1)}, bf16[512,1024]{1,0:T(8,128)(2,1)}, u32[]{:S(2)}, u32[]{:S(2)}) %collective-permute-start.5) | collective-permute-done | bytes 1048608 | tf_op jit(solution)/shard_map/ppermute | solution.py:398
  224.7 3.5 %collective-permute-start.6 = (bf16[512,1024]{1,0:T(8,128)(2,1)}, bf16[512,1024]{1,0:T(8,128)(2,1)}, u32[]{:S(2)}, u32[]{:S(2)}) collective-permute-start(bf16[512,1024]{1,0:T(8,128)(2,1)} %collective-permute-done.5.refs_0_), channel_id=1, source_target_pairs={{0,6},{1,7},{2,0},{3,1},{4,2},{5,3},{6,4},{7,5},{8,9},{9,8},{10,11... | collective-permute-start | bytes 3145736 | tf_op jit(solution)/shard_map/ppermute | solution.py:398
  228.4 0.7 pad_add_fusion.index
  229.1 1.0 copy-done.4
  230.0 9.6 %product.3.refs_7_ = f32[512,1024]{1,0:T(8,128)} custom-call(s32[17]{0:T(128)} %pad_add_fusion.index, bf16[512,1024]{1,0:T(8,128)(2,1)} %sum_blocks.1.refs_0_, bf16[512,1024]{1,0:T(8,128)(2,1)} %copy-done.2, bf16[512,1024]{1,0:T(8,128)(2,1)} %copy-done.3, bf16[512,1024]{1,0:T(8,128)(2,1)} %copy-done.4, ...), custom_call_target="tpu_custom_call" | custom-call | tf_op jit(solution)/shard_map/product/pallas_call | solution.py:323
  239.7 0.7 collective-permute-done.16.refs_1_
  240.4 9.6 %product.4.refs_5_ = f32[512,1024]{1,0:T(8,128)} custom-call(s32[17]{0:T(128)} %pad_add_fusion.index, bf16[512,1024]{1,0:T(8,128)(2,1)} %collective-permute-done.5.refs_0_, bf16[512,1024]{1,0:T(8,128)(2,1)} %collective-permute-done.16.refs_1_, bf16[512,1024]{1,0:T(8,128)(2,1)} %collective-permute-done.18.refs_2_, ...), custom_call_target="tpu_custom_call" | custom-call | tf_op jit(solution)/shard_map/product/pallas_call | solution.py:323
  250.0 5.4 %product.5 = f32[512,1024]{1,0:T(8,128)} custom-call(s32[17]{0:T(128)} %pad_add_fusion.index, bf16[512,1024]{1,0:T(8,128)(2,1)} %collective-permute-done.6.refs_0_, bf16[4,512,1024]{2,1,0:T(8,128)(2,1)} %pad_maximum_fusion.refs_4_.refs_3_.refs_1_, bf16[4,512,1024]{2,1,0:T(8,128)(2,1)} %copy-done, ...), custom_call_target="tpu_custom_call" | custom-call | tf_op jit(solution)/shard_map/product/pallas_call | solution.py:323
  (63 shorter events, 3.7 us)
Async XLA Ops:
  0.6 9.8 %collective-permute-start = (s32[3,64]{1,0:T(4,128)}, s32[3,64]{1,0:T(4,128)S(1)}, u32[]{:S(2)}, u32[]{:S(2)}) collective-permute-start(s32[3,64]{1,0:T(4,128)} %bitcast.85), channel_id=1, source_target_pairs={{0,1},{1,2},{2,3},{3,4},{4,5},{5,6},{6,7},{7,8},{8,9},{9,10},{10,1... | collective-permute-start | bytes 2312 | tf_op jit(solution)/shard_map/ppermute | solution.py:28
  4.0 6.5 %collective-permute-start.1 = (s32[3,64]{1,0:T(4,128)}, s32[3,64]{1,0:T(4,128)S(1)}, u32[]{:S(2)}, u32[]{:S(2)}) collective-permute-start(s32[3,64]{1,0:T(4,128)} %bitcast.86), channel_id=1, source_target_pairs={{0,127},{1,0},{2,1},{3,2},{4,3},{5,4},{6,5},{7,6},{8,7},{9,8},{10,... | collective-permute-start | bytes 2312 | tf_op jit(solution)/shard_map/ppermute | solution.py:28
  10.4 0.6 copy-start.9
  11.0 0.6 copy-start.10
  17.0 13.4 %collective-permute-start.2 = (f32[64,128]{1,0:T(8,128)}, f32[64,128]{1,0:T(8,128)S(1)}, u32[]{:S(2)}, u32[]{:S(2)}) collective-permute-start(f32[64,128]{1,0:T(8,128)} %get-tuple-element.8), channel_id=1, source_target_pairs={{0,1},{1,2},{2,3},{3,4},{4,5},{5,6},{6,7},{7,8},{8,9},{9,10},{10,1... | collective-permute-start | bytes 98312 | tf_op jit(solution)/shard_map/ppermute | solution.py:28
  17.6 12.8 %collective-permute-start.3 = (f32[64,128]{1,0:T(8,128)}, f32[64,128]{1,0:T(8,128)S(1)}, u32[]{:S(2)}, u32[]{:S(2)}) collective-permute-start(f32[64,128]{1,0:T(8,128)} %get-tuple-element.9), channel_id=1, source_target_pairs={{0,127},{1,0},{2,1},{3,2},{4,3},{5,4},{6,5},{7,6},{8,7},{9,8},{10,... | collective-permute-start | bytes 98312 | tf_op jit(solution)/shard_map/ppermute | solution.py:28
  30.4 0.6 copy-start.6
  30.4 0.6 copy-start.7
  39.0 6.3 %copy-start.5 = (bf16[512,1024]{1,0:T(8,128)(2,1)S(1)}, bf16[512,1024]{1,0:T(8,128)(2,1)}, u32[]{:S(2)}) copy-start(bf16[512,1024]{1,0:T(8,128)(2,1)} %param.19) | copy-start | bytes 3145732
  39.0 82.5 %copy-start.11 = (s32[8,2]{0,1:T(2,128)S(1)}, s32[8,2]{0,1:T(2,128)}, u32[]{:S(2)}) copy-start(s32[8,2]{0,1:T(2,128)} %constant.52.clone) | copy-start | bytes 196
  39.0 82.5 %copy-start.12 = (s32[8,2]{0,1:T(2,128)S(1)}, s32[8,2]{0,1:T(2,128)}, u32[]{:S(2)}) copy-start(s32[8,2]{0,1:T(2,128)} %constant.53.clone) | copy-start | bytes 196
  39.0 82.5 %copy-start.13 = (s32[8,2]{0,1:T(2,128)S(1)}, s32[8,2]{0,1:T(2,128)}, u32[]{:S(2)}) copy-start(s32[8,2]{0,1:T(2,128)} %constant.54.clone) | copy-start | bytes 196
  39.0 82.5 %copy-start.14 = (s32[8,2]{0,1:T(2,128)S(1)}, s32[8,2]{0,1:T(2,128)}, u32[]{:S(2)}) copy-start(s32[8,2]{0,1:T(2,128)} %constant.55.clone) | copy-start | bytes 196
  39.0 93.1 %copy-start.8 = (s32[64,64]{1,0:T(8,128)S(1)}, s32[64,64]{1,0:T(8,128)}, u32[]{:S(2)}) copy-start(s32[64,64]{1,0:T(8,128)} %param.20) | copy-start | bytes 49156
  39.0 115.3 %all-to-all-start = ((bf16[128,136,128]{2,1,0:T(8,128)(2,1)}), bf16[128,136,128]{2,1,0:T(8,128)(2,1)}, u32[]{:S(2)}, u32[]{:S(2)}) async-start(bf16[128,136,128]{2,1,0:T(8,128)(2,1)} %partial_blocks.1), calls=%async_computation | async-start | bytes 8912896 | tf_op jit(solution)/shard_map/all_to_all | solution.py:423
  45.3 71.8 %collective-permute-start.7 = (bf16[512,1024]{1,0:T(8,128)(2,1)S(1)}, bf16[512,1024]{1,0:T(8,128)(2,1)S(1)}, u32[]{:S(2)}, u32[]{:S(2)}) collective-permute-start(bf16[512,1024]{1,0:T(8,128)(2,1)S(1)} %copy-done.5), channel_id=1, source_target_pairs={{0,64},{64,0},{16,80},{80,16},{32,96},{96,32},{48,112},{112,48},{8... | collective-permute-start | bytes 3145736 | tf_op jit(solution)/shard_map/ppermute | solution.py:398
  46.3 93.8 %collective-permute-start.8 = (bf16[512,1024]{1,0:T(8,128)(2,1)S(1)}, bf16[512,1024]{1,0:T(8,128)(2,1)}, u32[]{:S(2)}, u32[]{:S(2)}) collective-permute-start(bf16[512,1024]{1,0:T(8,128)(2,1)S(1)} %copy-done.5), channel_id=1, source_target_pairs={{0,16},{64,80},{16,32},{80,96},{32,48},{96,112},{48,0},{112,64},{8... | collective-permute-start | bytes 3145736 | tf_op jit(solution)/shard_map/ppermute | solution.py:398
  117.1 23.0 %collective-permute-start.10 = (bf16[512,1024]{1,0:T(8,128)(2,1)S(1)}, bf16[512,1024]{1,0:T(8,128)(2,1)S(1)}, u32[]{:S(2)}, u32[]{:S(2)}) collective-permute-start(bf16[512,1024]{1,0:T(8,128)(2,1)S(1)} %collective-permute-done.7), channel_id=1, source_target_pairs={{0,48},{64,112},{16,0},{80,64},{32,16},{96,80},{48,32},{112,96},{8... | collective-permute-start | bytes 3145736 | tf_op jit(solution)/shard_map/ppermute | solution.py:398
  121.0 29.4 %collective-permute-start.9 = (bf16[512,1024]{1,0:T(8,128)(2,1)S(1)}, bf16[512,1024]{1,0:T(8,128)(2,1)}, u32[]{:S(2)}, u32[]{:S(2)}) collective-permute-start(bf16[512,1024]{1,0:T(8,128)(2,1)S(1)} %copy-done.5), channel_id=1, source_target_pairs={{0,48},{64,112},{16,0},{80,64},{32,16},{96,80},{48,32},{112,96},{8... | collective-permute-start | bytes 3145736 | tf_op jit(solution)/shard_map/ppermute | solution.py:398
  138.5 27.4 %collective-permute-start.11 = (bf16[512,1024]{1,0:T(8,128)(2,1)S(1)}, bf16[512,1024]{1,0:T(8,128)(2,1)}, u32[]{:S(2)}, u32[]{:S(2)}) collective-permute-start(bf16[512,1024]{1,0:T(8,128)(2,1)S(1)} %collective-permute-done.7), channel_id=1, source_target_pairs={{0,16},{64,80},{16,32},{80,96},{32,48},{96,112},{48,0},{112,64},{8... | collective-permute-start | bytes 3145736 | tf_op jit(solution)/shard_map/ppermute | solution.py:398
  140.0 37.6 %collective-permute-start.12 = (bf16[512,1024]{1,0:T(8,128)(2,1)}, bf16[512,1024]{1,0:T(8,128)(2,1)}, u32[]{:S(2)}, u32[]{:S(2)}) collective-permute-start(bf16[512,1024]{1,0:T(8,128)(2,1)} %collective-permute-done.8), channel_id=1, source_target_pairs={{0,16},{64,80},{16,32},{80,96},{32,48},{96,112},{48,0},{112,64},{8... | collective-permute-start | bytes 3145736 | tf_op jit(solution)/shard_map/ppermute | solution.py:398
  140.1 37.5 %collective-permute-start.13 = (bf16[512,1024]{1,0:T(8,128)(2,1)S(1)}, bf16[512,1024]{1,0:T(8,128)(2,1)}, u32[]{:S(2)}, u32[]{:S(2)}) collective-permute-start(bf16[512,1024]{1,0:T(8,128)(2,1)S(1)} %collective-permute-done.10), channel_id=1, source_target_pairs={{0,48},{64,112},{16,0},{80,64},{32,16},{96,80},{48,32},{112,96},{8... | collective-permute-start | bytes 3145736 | tf_op jit(solution)/shard_map/ppermute | solution.py:398
  154.4 52.0 %collective-permute-start.14 = (bf16[4,512,1024]{2,1,0:T(8,128)(2,1)}, bf16[4,512,1024]{2,1,0:T(8,128)(2,1)}, u32[]{:S(2)}, u32[]{:S(2)}) collective-permute-start(bf16[4,512,1024]{2,1,0:T(8,128)(2,1)} %pad_maximum_fusion.refs_4_.refs_3_.refs_1_), channel_id=1, source_target_pairs={{0,8},{8,0},{1,9},{9,1},{2,10},{10,2},{3,11},{11,3},{4,12},{12,4},... | collective-permute-start | bytes 12582920 | tf_op jit(solution)/shard_map/ppermute | solution.py:28
  183.3 3.4 %copy-start.1 = (bf16[512,1024]{1,0:T(8,128)(2,1)S(1)}, bf16[512,1024]{1,0:T(8,128)(2,1)}, u32[]{:S(2)}) copy-start(bf16[512,1024]{1,0:T(8,128)(2,1)} %sum_blocks.1.refs_0_) | copy-start | bytes 3145732
  183.3 44.9 %copy-start.15 = (s32[8]{0:T(128)S(1)}, s32[8]{0:T(128)}, u32[]{:S(2)}) copy-start(s32[8]{0:T(128)} %constant.56.clone) | copy-start | bytes 100
  183.3 44.9 %copy-start.16 = (s32[8]{0:T(128)S(1)}, s32[8]{0:T(128)}, u32[]{:S(2)}) copy-start(s32[8]{0:T(128)} %constant.57.clone) | copy-start | bytes 100
  183.9 2.0 copy-start
  185.9 44.1 %collective-permute-start.15 = (bf16[4,512,1024]{2,1,0:T(8,128)(2,1)S(1)}, bf16[4,512,1024]{2,1,0:T(8,128)(2,1)}, u32[]{:S(2)}, u32[]{:S(2)}) collective-permute-start(bf16[4,512,1024]{2,1,0:T(8,128)(2,1)S(1)} %pad_maximum_fusion.1.refs_5_.refs_4_.refs_2_), channel_id=1, source_target_pairs={{0,8},{8,0},{1,9},{9,1},{2,10},{10,2},{3,11},{11,3},{4,12},{12,4},... | collective-permute-start | bytes 12582920 | tf_op jit(solution)/shard_map/ppermute | solution.py:28
  186.7 16.3 %collective-permute-start.4 = (bf16[512,1024]{1,0:T(8,128)(2,1)S(1)}, bf16[512,1024]{1,0:T(8,128)(2,1)S(1)}, u32[]{:S(2)}, u32[]{:S(2)}) collective-permute-start(bf16[512,1024]{1,0:T(8,128)(2,1)S(1)} %copy-done.1), channel_id=1, source_target_pairs={{0,1},{1,0},{2,3},{3,2},{4,5},{5,4},{6,7},{7,6},{8,10},{9,11},{10,... | collective-permute-start | bytes 3145736 | tf_op jit(solution)/shard_map/ppermute | solution.py:398
  189.5 23.8 %collective-permute-start.17 = (bf16[512,1024]{1,0:T(8,128)(2,1)S(1)}, bf16[512,1024]{1,0:T(8,128)(2,1)S(1)}, u32[]{:S(2)}, u32[]{:S(2)}) collective-permute-start(bf16[512,1024]{1,0:T(8,128)(2,1)S(1)} %copy-done.1), channel_id=1, source_target_pairs={{0,6},{1,7},{2,0},{3,1},{4,2},{5,3},{6,4},{7,5},{8,14},{9,15},{10,... | collective-permute-start | bytes 3145736 | tf_op jit(solution)/shard_map/ppermute | solution.py:398
  203.0 27.0 %copy-start.2 = (bf16[512,1024]{1,0:T(8,128)(2,1)}, bf16[512,1024]{1,0:T(8,128)(2,1)S(1)}, u32[]{:S(2)}) copy-start(bf16[512,1024]{1,0:T(8,128)(2,1)S(1)} %collective-permute-done.4.refs_1_) | copy-start | bytes 3145732
  203.0 21.7 %collective-permute-start.5 = (bf16[512,1024]{1,0:T(8,128)(2,1)S(1)}, bf16[512,1024]{1,0:T(8,128)(2,1)}, u32[]{:S(2)}, u32[]{:S(2)}) collective-permute-start(bf16[512,1024]{1,0:T(8,128)(2,1)S(1)} %collective-permute-done.4.refs_1_), channel_id=1, source_target_pairs={{0,6},{1,7},{2,0},{3,1},{4,2},{5,3},{6,4},{7,5},{8,10},{9,11},{10,... | collective-permute-start | bytes 3145736 | tf_op jit(solution)/shard_map/ppermute | solution.py:398
  206.3 22.7 %collective-permute-start.19 = (bf16[512,1024]{1,0:T(8,128)(2,1)S(1)}, bf16[512,1024]{1,0:T(8,128)(2,1)S(1)}, u32[]{:S(2)}, u32[]{:S(2)}) collective-permute-start(bf16[512,1024]{1,0:T(8,128)(2,1)S(1)} %copy-done.1), channel_id=1, source_target_pairs={{0,2},{1,3},{2,4},{3,5},{4,6},{5,7},{6,0},{7,1},{8,9},{9,8},{10,11... | collective-permute-start | bytes 3145736 | tf_op jit(solution)/shard_map/ppermute | solution.py:398
  206.3 34.0 %collective-permute-start.16 = (bf16[512,1024]{1,0:T(8,128)(2,1)S(1)}, bf16[512,1024]{1,0:T(8,128)(2,1)}, u32[]{:S(2)}, u32[]{:S(2)}) collective-permute-start(bf16[512,1024]{1,0:T(8,128)(2,1)S(1)} %collective-permute-done.4.refs_1_), channel_id=1, source_target_pairs={{0,2},{1,3},{2,4},{3,5},{4,6},{5,7},{6,0},{7,1},{8,9},{9,8},{10,11... | collective-permute-start | bytes 3145736 | tf_op jit(solution)/shard_map/ppermute | solution.py:398
  213.3 16.7 %copy-start.3 = (bf16[512,1024]{1,0:T(8,128)(2,1)}, bf16[512,1024]{1,0:T(8,128)(2,1)S(1)}, u32[]{:S(2)}) copy-start(bf16[512,1024]{1,0:T(8,128)(2,1)S(1)} %collective-permute-done.17.refs_2_) | copy-start | bytes 3145732
  213.3 27.1 %collective-permute-start.18 = (bf16[512,1024]{1,0:T(8,128)(2,1)S(1)}, bf16[512,1024]{1,0:T(8,128)(2,1)}, u32[]{:S(2)}, u32[]{:S(2)}) collective-permute-start(bf16[512,1024]{1,0:T(8,128)(2,1)S(1)} %collective-permute-done.17.refs_2_), channel_id=1, source_target_pairs={{0,6},{1,7},{2,0},{3,1},{4,2},{5,3},{6,4},{7,5},{8,9},{9,8},{10,11... | collective-permute-start | bytes 3145736 | tf_op jit(solution)/shard_map/ppermute | solution.py:398
  224.7 25.3 %collective-permute-start.6 = (bf16[512,1024]{1,0:T(8,128)(2,1)}, bf16[512,1024]{1,0:T(8,128)(2,1)}, u32[]{:S(2)}, u32[]{:S(2)}) collective-permute-start(bf16[512,1024]{1,0:T(8,128)(2,1)} %collective-permute-done.5.refs_0_), channel_id=1, source_target_pairs={{0,6},{1,7},{2,0},{3,1},{4,2},{5,3},{6,4},{7,5},{8,9},{9,8},{10,11... | collective-permute-start | bytes 3145736 | tf_op jit(solution)/shard_map/ppermute | solution.py:398
  229.1 1.0 copy-start.4

commit v4 on v3

--- a/solution.py
+++ b/solution.py
@@ -265,6 +265,12 @@
     mine = pl.multiple_of(index[0] * 512, 512)
     theirs = pl.multiple_of(512 - index[0] * 512, 512)
 
+    if has_acc:
+        load = pltpu.make_async_copy(acc, total, acc_sem)
+        load.start()
+    else:
+        total[...] = jnp.zeros_like(total)
+
     for k in range(count):
         pltpu.make_async_copy(pieces[k], columns.at[k], column_sem.at[k]).start()
         for s, (base, at) in enumerate(((1, mine), (9, theirs))):
@@ -278,12 +284,6 @@
                         rows.at[k, pl.ds(at, 512), :],
                         row_sem.at[k, s],
                     ).start()
-
-    if has_acc:
-        load = pltpu.make_async_copy(acc, total, acc_sem)
-        load.start()
-    else:
-        total[...] = jnp.zeros_like(total)
 
     def arrive(k):
         pltpu.make_async_copy(pieces[0], columns.at[k], column_sem.at[k]).wait()
@@ -466,8 +466,9 @@
     in_other = jnp.sum(hot * jnp.where(c == 0, second, first)[None, :], axis=1)
     index = jnp.concatenate([c.reshape(1), in_own, in_other]).astype(jnp.int32)
 
-    out = multiply(index, 0, None, h[:4], stacks)
-    out = multiply(index, 4, out, h[4:7], stacks)
+    out = multiply(index, 0, None, h[:3], stacks)
+    out = multiply(index, 3, out, h[3:5], stacks)
+    out = multiply(index, 5, out, h[5:7], stacks)
     out = multiply(index, 7, out, h[7:], stacks)
     return hamiltonian, out
 

time: 259 us -> 259 us (level)
  Pallas kernels: 49 us -> 52.7 us
    pallas_call x3 -> x4, Pallas kernels: 24.7 us -> 28.3 us  [multiply(): pl.pallas_call(functools.partial(product_kernel, count, first, acc is not...]
  transfers between devices with their start and end apart: 21 -> 21, of which waited for: 10 -> 9; matrix products, arithmetic and copies ran while one was open for 6% -> 6% of each run, Pallas kernels for 12% -> 13%
where the time goes in v4:
time: 259 us; the launch traced here: 257 us
  waiting for transfers between devices  119 us (46%)
  Pallas kernels  52.7 us (20%)
  starting transfers between devices  50 us (19%)
  between operations  17 us (7%)
  other arithmetic  12.2 us (5%)
  local copies, waits for them, and re-layouts  6.68 us (3%)
    ppermute x14, waiting for transfers between devices, send(): return lax.ppermute(array, axes, pairs)  117 us
    pallas_call x4, Pallas kernels, multiply(): pl.pallas_call(functools.partial(product_kernel, count, first, acc is not...  28.3 us
    ppermute x14, starting transfers between devices, send(): return lax.ppermute(array, axes, pairs)  27.3 us
    ppermute x6, starting transfers between devices, shift(): lax.ppermute(array, axis, [(i, (i + step) % size) for i in range(size)])  16.4 us
    select_n x8, other arithmetic, block_mask(): kept = jnp.where(selected, shaped, jnp.zeros((), values.dtype))  8.36 us
    pallas_call x1, Pallas kernels, partial_blocks(): pl.pallas_call(partial_kernel, in_specs=[SMEM] * 3 + [vmem] * 3 + [hbm] *...  7.9 us
    all_to_all x1, starting transfers between devices, steps(): received = lax.all_to_all(outgoing, ALL, 0, 0, tiled=True)  6.21 us
    pallas_call x1, Pallas kernels, hamiltonian_tile(): pl.pallas_call(sum_kernel, in_specs=[SMEM, hbm, hbm], out_specs=pl.BlockS...  5.55 us
  transfers between devices with their start and end apart: 21, of which 9 were waited for; matrix products, arithmetic and copies ran while one was open for 6% of the time, Pallas kernels for 13%

profile of v4, /device:TPU:0, one launch (start us, length us, event | category | flops | bytes accessed | tf_op | source)
XLA Modules:
  0.0 257.5 jit_solution(9589944794213148672)
XLA Ops:
  0.6 3.4 %collective-permute-start = (s32[3,64]{1,0:T(4,128)}, s32[3,64]{1,0:T(4,128)S(1)}, u32[]{:S(2)}, u32[]{:S(2)}) collective-permute-start(s32[3,64]{1,0:T(4,128)} %bitcast.85), channel_id=1, source_target_pairs={{0,1},{1,2},{2,3},{3,4},{4,5},{5,6},{6,7},{7,8},{8,9},{9,10},{10,1... | collective-permute-start | bytes 2312 | tf_op jit(solution)/shard_map/ppermute | solution.py:28
  4.0 5.0 %collective-permute-start.1 = (s32[3,64]{1,0:T(4,128)}, s32[3,64]{1,0:T(4,128)S(1)}, u32[]{:S(2)}, u32[]{:S(2)}) collective-permute-start(s32[3,64]{1,0:T(4,128)} %bitcast.86), channel_id=1, source_target_pairs={{0,127},{1,0},{2,1},{3,2},{4,3},{5,4},{6,5},{7,6},{8,7},{9,8},{10,... | collective-permute-start | bytes 2312 | tf_op jit(solution)/shard_map/ppermute | solution.py:28
  9.0 1.4 collective-permute-done.prev_ref
  10.5 0.5 copy-done.8
  11.0 0.6 copy-done.9
  11.6 5.5 %cut_edges.1 = (f32[64,128]{1,0:T(8,128)}, f32[64,128]{1,0:T(8,128)}) custom-call(s32[3,64]{1,0:T(4,128)} %copy-done.8, s32[3,64]{1,0:T(4,128)} %copy-done.9, f32[4,512,512]{2,1,0:T(8,128)} %potential.3), custom_call_target="tpu_custom_call" | custom-call | tf_op jit(solution)/shard_map/cut_edges/pallas_call | solution.py:103
  17.1 0.6 collective-permute-start.2
  17.6 6.7 %collective-permute-start.3 = (f32[64,128]{1,0:T(8,128)}, f32[64,128]{1,0:T(8,128)S(1)}, u32[]{:S(2)}, u32[]{:S(2)}) collective-permute-start(f32[64,128]{1,0:T(8,128)} %get-tuple-element.9), channel_id=1, source_target_pairs={{0,127},{1,0},{2,1},{3,2},{4,3},{5,4},{6,5},{7,6},{8,7},{9,8},{10,... | collective-permute-start | bytes 98312 | tf_op jit(solution)/shard_map/ppermute | solution.py:28
  24.3 5.5 %cut_own.1.own = f32[2,64,128]{2,1,0:T(8,128)} custom-call(s32[3,64]{1,0:T(4,128)} %bitcast.87, f32[4,512,512]{2,1,0:T(8,128)} %potential.3), custom_call_target="tpu_custom_call" | custom-call | tf_op jit(solution)/shard_map/cut_own/pallas_call | solution.py:113
  30.5 0.6 copy-done.5
  31.1 7.9 %partial_blocks.1 = bf16[128,136,128]{2,1,0:T(8,128)(2,1)} custom-call(s32[2,64]{1,0:T(2,128)} %bitcast.89, s32[1]{0:T(128)S(6)} %copy.49.live_ref, s32[3,64]{1,0:T(4,128)} %bitcast.88, f32[64,128]{1,0:T(8,128)} %copy-done.5, f32[2,64,128]{2,1,0:T(8,128)} %cut_own.1.own, f32[64,128]{1,0:T(8,128)} %copy-done.6, bf16[64,128,384]{2,1,0:T(8,128)(2,1)} %left.1, ...), custom_call_target="tpu_custom_call" | custom-call | tf_op jit(solution)/shard_map/partial_blocks/pallas_call | solution.py:186
  39.1 6.2 %all-to-all-start = ((bf16[128,136,128]{2,1,0:T(8,128)(2,1)}), bf16[128,136,128]{2,1,0:T(8,128)(2,1)}, u32[]{:S(2)}, u32[]{:S(2)}) async-start(bf16[128,136,128]{2,1,0:T(8,128)(2,1)} %partial_blocks.1), calls=%async_computation | async-start | bytes 8912896 | tf_op jit(solution)/shard_map/all_to_all | solution.py:423
  45.3 1.0 collective-permute-start.7
  46.3 1.6 collective-permute-start.8
  47.9 69.2 %collective-permute-done.7 = bf16[512,1024]{1,0:T(8,128)(2,1)S(1)} collective-permute-done((bf16[512,1024]{1,0:T(8,128)(2,1)S(1)}, bf16[512,1024]{1,0:T(8,128)(2,1)S(1)}, u32[]{:S(2)}, u32[]{:S(2)}) %collective-permute-start.7) | collective-permute-done | bytes 1048608 | tf_op jit(solution)/shard_map/ppermute | solution.py:398
  117.1 3.9 %collective-permute-start.10 = (bf16[512,1024]{1,0:T(8,128)(2,1)S(1)}, bf16[512,1024]{1,0:T(8,128)(2,1)S(1)}, u32[]{:S(2)}, u32[]{:S(2)}) collective-permute-start(bf16[512,1024]{1,0:T(8,128)(2,1)S(1)} %collective-permute-done.7), channel_id=1, source_target_pairs={{0,48},{64,112},{16,0},{80,64},{32,16},{96,80},{48,32},{112,96},{8... | collective-permute-start | bytes 3145736 | tf_op jit(solution)/shard_map/ppermute | solution.py:398
  121.0 0.6 collective-permute-start.9
  121.6 0.7 fusion.8
  132.4 0.6 reshape.87.pattern_ref
  138.7 1.5 collective-permute-start.11
  140.3 3.1 %collective-permute-start.13 = (bf16[512,1024]{1,0:T(8,128)(2,1)S(1)}, bf16[512,1024]{1,0:T(8,128)(2,1)}, u32[]{:S(2)}, u32[]{:S(2)}) collective-permute-start(bf16[512,1024]{1,0:T(8,128)(2,1)S(1)} %collective-permute-done.10), channel_id=1, source_target_pairs={{0,48},{64,112},{16,0},{80,64},{32,16},{96,80},{48,32},{112,96},{8... | collective-permute-start | bytes 3145736 | tf_op jit(solution)/shard_map/ppermute | solution.py:398
  144.2 1.5 fusion.2
  145.7 4.5 %collective-permute-done.9 = bf16[512,1024]{1,0:T(8,128)(2,1)} collective-permute-done((bf16[512,1024]{1,0:T(8,128)(2,1)S(1)}, bf16[512,1024]{1,0:T(8,128)(2,1)}, u32[]{:S(2)}, u32[]{:S(2)}) %collective-permute-start.9) | collective-permute-done | bytes 1048608 | tf_op jit(solution)/shard_map/ppermute | solution.py:398
  150.4 1.5 fusion.3
  151.9 2.3 pad_maximum_fusion.refs_3_.refs_2_.refs_1_
  154.2 5.6 %sum_blocks.1.refs_0_ = bf16[512,1024]{1,0:T(8,128)(2,1)} custom-call(s32[32]{0:T(128)} %reshape.87.pattern_ref, bf16[512,1024]{1,0:T(8,128)(2,1)} %core.1, bf16[128,136,128]{2,1,0:T(8,128)(2,1)} %all-to-all-done.received), custom_call_target="tpu_custom_call" | custom-call | tf_op jit(solution)/shard_map/sum_blocks/pallas_call | solution.py:244
  159.8 6.3 %collective-permute-done.11 = bf16[512,1024]{1,0:T(8,128)(2,1)} collective-permute-done((bf16[512,1024]{1,0:T(8,128)(2,1)S(1)}, bf16[512,1024]{1,0:T(8,128)(2,1)}, u32[]{:S(2)}, u32[]{:S(2)}) %collective-permute-start.11) | collective-permute-done | bytes 1048608 | tf_op jit(solution)/shard_map/ppermute | solution.py:398
  166.1 11.5 %collective-permute-done.12 = bf16[512,1024]{1,0:T(8,128)(2,1)} collective-permute-done((bf16[512,1024]{1,0:T(8,128)(2,1)}, bf16[512,1024]{1,0:T(8,128)(2,1)}, u32[]{:S(2)}, u32[]{:S(2)}) %collective-permute-start.12) | collective-permute-done | bytes 1048608 | tf_op jit(solution)/shard_map/ppermute | solution.py:398
  178.3 1.5 fusion.5
  180.1 1.5 fusion.6
  181.8 1.5 fusion.7
  183.3 0.6 pad_maximum_fusion.1.refs_4_.refs_3_.refs_2_
  183.9 2.0 copy-done
  185.9 0.8 collective-permute-start.15
  186.7 2.8 %collective-permute-start.4 = (bf16[512,1024]{1,0:T(8,128)(2,1)S(1)}, bf16[512,1024]{1,0:T(8,128)(2,1)S(1)}, u32[]{:S(2)}, u32[]{:S(2)}) collective-permute-start(bf16[512,1024]{1,0:T(8,128)(2,1)S(1)} %copy-done.1), channel_id=1, source_target_pairs={{0,1},{1,0},{2,3},{3,2},{4,5},{5,4},{6,7},{7,6},{8,10},{9,11},{10,... | collective-permute-start | bytes 3145736 | tf_op jit(solution)/shard_map/ppermute | solution.py:398
  189.5 1.9 collective-permute-start.17
  191.3 11.7 %collective-permute-done.4.refs_1_ = bf16[512,1024]{1,0:T(8,128)(2,1)S(1)} collective-permute-done((bf16[512,1024]{1,0:T(8,128)(2,1)S(1)}, bf16[512,1024]{1,0:T(8,128)(2,1)S(1)}, u32[]{:S(2)}, u32[]{:S(2)}) %collective-permute-start.4) | collective-permute-done | bytes 1048608 | tf_op jit(solution)/shard_map/ppermute | solution.py:398
  203.0 3.3 %collective-permute-start.5 = (bf16[512,1024]{1,0:T(8,128)(2,1)S(1)}, bf16[512,1024]{1,0:T(8,128)(2,1)S(1)}, u32[]{:S(2)}, u32[]{:S(2)}) collective-permute-start(bf16[512,1024]{1,0:T(8,128)(2,1)S(1)} %collective-permute-done.4.refs_1_), channel_id=1, source_target_pairs={{0,6},{1,7},{2,0},{3,1},{4,2},{5,3},{6,4},{7,5},{8,10},{9,11},{10,... | collective-permute-start | bytes 3145736 | tf_op jit(solution)/shard_map/ppermute | solution.py:398
  206.3 0.5 collective-permute-start.16
  206.9 6.6 %collective-permute-done.17.refs_2_ = bf16[512,1024]{1,0:T(8,128)(2,1)} collective-permute-done((bf16[512,1024]{1,0:T(8,128)(2,1)S(1)}, bf16[512,1024]{1,0:T(8,128)(2,1)}, u32[]{:S(2)}, u32[]{:S(2)}) %collective-permute-start.17) | collective-permute-done | bytes 1048608 | tf_op jit(solution)/shard_map/ppermute | solution.py:398
  213.4 3.5 %collective-permute-start.18 = (bf16[512,1024]{1,0:T(8,128)(2,1)}, bf16[512,1024]{1,0:T(8,128)(2,1)}, u32[]{:S(2)}, u32[]{:S(2)}) collective-permute-start(bf16[512,1024]{1,0:T(8,128)(2,1)} %collective-permute-done.17.refs_2_), channel_id=1, source_target_pairs={{0,6},{1,7},{2,0},{3,1},{4,2},{5,3},{6,4},{7,5},{8,9},{9,8},{10,11... | collective-permute-start | bytes 3145736 | tf_op jit(solution)/shard_map/ppermute | solution.py:398
  216.9 7.6 %collective-permute-done.5.refs_1_ = bf16[512,1024]{1,0:T(8,128)(2,1)S(1)} collective-permute-done((bf16[512,1024]{1,0:T(8,128)(2,1)S(1)}, bf16[512,1024]{1,0:T(8,128)(2,1)S(1)}, u32[]{:S(2)}, u32[]{:S(2)}) %collective-permute-start.5) | collective-permute-done | bytes 1048608 | tf_op jit(solution)/shard_map/ppermute | solution.py:398
  224.5 3.5 %collective-permute-start.6 = (bf16[512,1024]{1,0:T(8,128)(2,1)S(1)}, bf16[512,1024]{1,0:T(8,128)(2,1)}, u32[]{:S(2)}, u32[]{:S(2)}) collective-permute-start(bf16[512,1024]{1,0:T(8,128)(2,1)S(1)} %collective-permute-done.5.refs_1_), channel_id=1, source_target_pairs={{0,6},{1,7},{2,0},{3,1},{4,2},{5,3},{6,4},{7,5},{8,9},{9,8},{10,11... | collective-permute-start | bytes 3145736 | tf_op jit(solution)/shard_map/ppermute | solution.py:398
  228.3 0.6 pad_add_fusion.index
  228.9 8.0 %product.4.refs_6_ = f32[512,1024]{1,0:T(8,128)} custom-call(s32[17]{0:T(128)} %pad_add_fusion.index, bf16[512,1024]{1,0:T(8,128)(2,1)} %sum_blocks.1.refs_0_, bf16[512,1024]{1,0:T(8,128)(2,1)} %copy-done.3, bf16[512,1024]{1,0:T(8,128)(2,1)} %collective-permute-done.17.refs_2_, bf16[4,512,1024]{2,1,0:T(8,128)(2,1)} %pad_maximum_fusion.refs_3_.refs_2_.refs_1_, ...), custom_call_target="tpu_custom_call" | custom-call | tf_op jit(solution)/shard_map/product/pallas_call | solution.py:323
  236.9 7.4 %product.5.refs_6_ = f32[512,1024]{1,0:T(8,128)} custom-call(s32[17]{0:T(128)} %pad_add_fusion.index, bf16[512,1024]{1,0:T(8,128)(2,1)} %collective-permute-done.19.refs_0_, bf16[512,1024]{1,0:T(8,128)(2,1)} %copy-done.2, bf16[4,512,1024]{2,1,0:T(8,128)(2,1)} %pad_maximum_fusion.refs_3_.refs_2_.refs_1_, bf16[4,512,1024]{2,1,0:T(8,128)(2,1)} %copy-done, ...), custom_call_target="tpu_custom_call" | custom-call | tf_op jit(solution)/shard_map/product/pallas_call | solution.py:323
  244.4 7.5 %product.6.refs_5_ = f32[512,1024]{1,0:T(8,128)} custom-call(s32[17]{0:T(128)} %pad_add_fusion.index, bf16[512,1024]{1,0:T(8,128)(2,1)} %collective-permute-done.16.refs_0_, bf16[512,1024]{1,0:T(8,128)(2,1)} %collective-permute-done.18.refs_1_, bf16[4,512,1024]{2,1,0:T(8,128)(2,1)} %pad_maximum_fusion.refs_3_.refs_2_.refs_1_, bf16[4,512,1024]{2,1,0:T(8,128)(2,1)} %copy-done, ...), custom_call_target="tpu_custom_call" | custom-call | tf_op jit(solution)/shard_map/product/pallas_call | solution.py:323
  251.9 5.4 %product.7 = f32[512,1024]{1,0:T(8,128)} custom-call(s32[17]{0:T(128)} %pad_add_fusion.index, bf16[512,1024]{1,0:T(8,128)(2,1)} %collective-permute-done.6.refs_0_, bf16[4,512,1024]{2,1,0:T(8,128)(2,1)} %pad_maximum_fusion.refs_3_.refs_2_.refs_1_, bf16[4,512,1024]{2,1,0:T(8,128)(2,1)} %copy-done, ...), custom_call_target="tpu_custom_call" | custom-call | tf_op jit(solution)/shard_map/product/pallas_call | solution.py:323
  (62 shorter events, 3.3 us)
Async XLA Ops:
  0.6 9.8 %collective-permute-start = (s32[3,64]{1,0:T(4,128)}, s32[3,64]{1,0:T(4,128)S(1)}, u32[]{:S(2)}, u32[]{:S(2)}) collective-permute-start(s32[3,64]{1,0:T(4,128)} %bitcast.85), channel_id=1, source_target_pairs={{0,1},{1,2},{2,3},{3,4},{4,5},{5,6},{6,7},{7,8},{8,9},{9,10},{10,1... | collective-permute-start | bytes 2312 | tf_op jit(solution)/shard_map/ppermute | solution.py:28
  4.0 6.5 %collective-permute-start.1 = (s32[3,64]{1,0:T(4,128)}, s32[3,64]{1,0:T(4,128)S(1)}, u32[]{:S(2)}, u32[]{:S(2)}) collective-permute-start(s32[3,64]{1,0:T(4,128)} %bitcast.86), channel_id=1, source_target_pairs={{0,127},{1,0},{2,1},{3,2},{4,3},{5,4},{6,5},{7,6},{8,7},{9,8},{10,... | collective-permute-start | bytes 2312 | tf_op jit(solution)/shard_map/ppermute | solution.py:28
  10.4 0.6 copy-start.8
  11.0 0.6 copy-start.9
  17.1 13.4 %collective-permute-start.2 = (f32[64,128]{1,0:T(8,128)}, f32[64,128]{1,0:T(8,128)S(1)}, u32[]{:S(2)}, u32[]{:S(2)}) collective-permute-start(f32[64,128]{1,0:T(8,128)} %get-tuple-element.8), channel_id=1, source_target_pairs={{0,1},{1,2},{2,3},{3,4},{4,5},{5,6},{6,7},{7,8},{8,9},{9,10},{10,1... | collective-permute-start | bytes 98312 | tf_op jit(solution)/shard_map/ppermute | solution.py:28
  17.6 12.8 %collective-permute-start.3 = (f32[64,128]{1,0:T(8,128)}, f32[64,128]{1,0:T(8,128)S(1)}, u32[]{:S(2)}, u32[]{:S(2)}) collective-permute-start(f32[64,128]{1,0:T(8,128)} %get-tuple-element.9), channel_id=1, source_target_pairs={{0,127},{1,0},{2,1},{3,2},{4,3},{5,4},{6,5},{7,6},{8,7},{9,8},{10,... | collective-permute-start | bytes 98312 | tf_op jit(solution)/shard_map/ppermute | solution.py:28
  30.4 0.6 copy-start.5
  30.5 0.6 copy-start.6
  39.0 6.3 %copy-start.4 = (bf16[512,1024]{1,0:T(8,128)(2,1)S(1)}, bf16[512,1024]{1,0:T(8,128)(2,1)}, u32[]{:S(2)}) copy-start(bf16[512,1024]{1,0:T(8,128)(2,1)} %param.19) | copy-start | bytes 3145732
  39.0 82.5 %copy-start.10 = (s32[8,2]{0,1:T(2,128)S(1)}, s32[8,2]{0,1:T(2,128)}, u32[]{:S(2)}) copy-start(s32[8,2]{0,1:T(2,128)} %constant.52.clone) | copy-start | bytes 196
  39.0 82.5 %copy-start.11 = (s32[8,2]{0,1:T(2,128)S(1)}, s32[8,2]{0,1:T(2,128)}, u32[]{:S(2)}) copy-start(s32[8,2]{0,1:T(2,128)} %constant.53.clone) | copy-start | bytes 196
  39.0 82.5 %copy-start.12 = (s32[8,2]{0,1:T(2,128)S(1)}, s32[8,2]{0,1:T(2,128)}, u32[]{:S(2)}) copy-start(s32[8,2]{0,1:T(2,128)} %constant.54.clone) | copy-start | bytes 196
  39.0 82.5 %copy-start.13 = (s32[8,2]{0,1:T(2,128)S(1)}, s32[8,2]{0,1:T(2,128)}, u32[]{:S(2)}) copy-start(s32[8,2]{0,1:T(2,128)} %constant.55.clone) | copy-start | bytes 196
  39.0 93.3 %copy-start.7 = (s32[64,64]{1,0:T(8,128)S(1)}, s32[64,64]{1,0:T(8,128)}, u32[]{:S(2)}) copy-start(s32[64,64]{1,0:T(8,128)} %param.20) | copy-start | bytes 49156
  39.1 115.2 %all-to-all-start = ((bf16[128,136,128]{2,1,0:T(8,128)(2,1)}), bf16[128,136,128]{2,1,0:T(8,128)(2,1)}, u32[]{:S(2)}, u32[]{:S(2)}) async-start(bf16[128,136,128]{2,1,0:T(8,128)(2,1)} %partial_blocks.1), calls=%async_computation | async-start | bytes 8912896 | tf_op jit(solution)/shard_map/all_to_all | solution.py:423
  45.3 71.8 %collective-permute-start.7 = (bf16[512,1024]{1,0:T(8,128)(2,1)S(1)}, bf16[512,1024]{1,0:T(8,128)(2,1)S(1)}, u32[]{:S(2)}, u32[]{:S(2)}) collective-permute-start(bf16[512,1024]{1,0:T(8,128)(2,1)S(1)} %copy-done.4), channel_id=1, source_target_pairs={{0,64},{64,0},{16,80},{80,16},{32,96},{96,32},{48,112},{112,48},{8... | collective-permute-start | bytes 3145736 | tf_op jit(solution)/shard_map/ppermute | solution.py:398
  46.3 94.0 %collective-permute-start.8 = (bf16[512,1024]{1,0:T(8,128)(2,1)S(1)}, bf16[512,1024]{1,0:T(8,128)(2,1)}, u32[]{:S(2)}, u32[]{:S(2)}) collective-permute-start(bf16[512,1024]{1,0:T(8,128)(2,1)S(1)} %copy-done.4), channel_id=1, source_target_pairs={{0,16},{64,80},{16,32},{80,96},{32,48},{96,112},{48,0},{112,64},{8... | collective-permute-start | bytes 3145736 | tf_op jit(solution)/shard_map/ppermute | solution.py:398
  117.1 23.3 %collective-permute-start.10 = (bf16[512,1024]{1,0:T(8,128)(2,1)S(1)}, bf16[512,1024]{1,0:T(8,128)(2,1)S(1)}, u32[]{:S(2)}, u32[]{:S(2)}) collective-permute-start(bf16[512,1024]{1,0:T(8,128)(2,1)S(1)} %collective-permute-done.7), channel_id=1, source_target_pairs={{0,48},{64,112},{16,0},{80,64},{32,16},{96,80},{48,32},{112,96},{8... | collective-permute-start | bytes 3145736 | tf_op jit(solution)/shard_map/ppermute | solution.py:398
  121.0 29.2 %collective-permute-start.9 = (bf16[512,1024]{1,0:T(8,128)(2,1)S(1)}, bf16[512,1024]{1,0:T(8,128)(2,1)}, u32[]{:S(2)}, u32[]{:S(2)}) collective-permute-start(bf16[512,1024]{1,0:T(8,128)(2,1)S(1)} %copy-done.4), channel_id=1, source_target_pairs={{0,48},{64,112},{16,0},{80,64},{32,16},{96,80},{48,32},{112,96},{8... | collective-permute-start | bytes 3145736 | tf_op jit(solution)/shard_map/ppermute | solution.py:398
  138.7 27.4 %collective-permute-start.11 = (bf16[512,1024]{1,0:T(8,128)(2,1)S(1)}, bf16[512,1024]{1,0:T(8,128)(2,1)}, u32[]{:S(2)}, u32[]{:S(2)}) collective-permute-start(bf16[512,1024]{1,0:T(8,128)(2,1)S(1)} %collective-permute-done.7), channel_id=1, source_target_pairs={{0,16},{64,80},{16,32},{80,96},{32,48},{96,112},{48,0},{112,64},{8... | collective-permute-start | bytes 3145736 | tf_op jit(solution)/shard_map/ppermute | solution.py:398
  140.2 37.4 %collective-permute-start.12 = (bf16[512,1024]{1,0:T(8,128)(2,1)}, bf16[512,1024]{1,0:T(8,128)(2,1)}, u32[]{:S(2)}, u32[]{:S(2)}) collective-permute-start(bf16[512,1024]{1,0:T(8,128)(2,1)} %collective-permute-done.8), channel_id=1, source_target_pairs={{0,16},{64,80},{16,32},{80,96},{32,48},{96,112},{48,0},{112,64},{8... | collective-permute-start | bytes 3145736 | tf_op jit(solution)/shard_map/ppermute | solution.py:398
  140.3 37.3 %collective-permute-start.13 = (bf16[512,1024]{1,0:T(8,128)(2,1)S(1)}, bf16[512,1024]{1,0:T(8,128)(2,1)}, u32[]{:S(2)}, u32[]{:S(2)}) collective-permute-start(bf16[512,1024]{1,0:T(8,128)(2,1)S(1)} %collective-permute-done.10), channel_id=1, source_target_pairs={{0,48},{64,112},{16,0},{80,64},{32,16},{96,80},{48,32},{112,96},{8... | collective-permute-start | bytes 3145736 | tf_op jit(solution)/shard_map/ppermute | solution.py:398
  154.2 52.1 %collective-permute-start.14 = (bf16[4,512,1024]{2,1,0:T(8,128)(2,1)}, bf16[4,512,1024]{2,1,0:T(8,128)(2,1)}, u32[]{:S(2)}, u32[]{:S(2)}) collective-permute-start(bf16[4,512,1024]{2,1,0:T(8,128)(2,1)} %pad_maximum_fusion.refs_3_.refs_2_.refs_1_), channel_id=1, source_target_pairs={{0,8},{8,0},{1,9},{9,1},{2,10},{10,2},{3,11},{11,3},{4,12},{12,4},... | collective-permute-start | bytes 12582920 | tf_op jit(solution)/shard_map/ppermute | solution.py:28
  183.3 3.4 %copy-start.1 = (bf16[512,1024]{1,0:T(8,128)(2,1)S(1)}, bf16[512,1024]{1,0:T(8,128)(2,1)}, u32[]{:S(2)}) copy-start(bf16[512,1024]{1,0:T(8,128)(2,1)} %sum_blocks.1.refs_0_) | copy-start | bytes 3145732
  183.3 44.8 %copy-start.14 = (s32[8]{0:T(128)S(1)}, s32[8]{0:T(128)}, u32[]{:S(2)}) copy-start(s32[8]{0:T(128)} %constant.56.clone) | copy-start | bytes 100
  183.3 44.8 %copy-start.15 = (s32[8]{0:T(128)S(1)}, s32[8]{0:T(128)}, u32[]{:S(2)}) copy-start(s32[8]{0:T(128)} %constant.57.clone) | copy-start | bytes 100
  183.9 2.0 copy-start
  185.9 43.0 %collective-permute-start.15 = (bf16[4,512,1024]{2,1,0:T(8,128)(2,1)S(1)}, bf16[4,512,1024]{2,1,0:T(8,128)(2,1)}, u32[]{:S(2)}, u32[]{:S(2)}) collective-permute-start(bf16[4,512,1024]{2,1,0:T(8,128)(2,1)S(1)} %pad_maximum_fusion.1.refs_4_.refs_3_.refs_2_), channel_id=1, source_target_pairs={{0,8},{8,0},{1,9},{9,1},{2,10},{10,2},{3,11},{11,3},{4,12},{12,4},... | collective-permute-start | bytes 12582920 | tf_op jit(solution)/shard_map/ppermute | solution.py:28
  186.7 16.3 %collective-permute-start.4 = (bf16[512,1024]{1,0:T(8,128)(2,1)S(1)}, bf16[512,1024]{1,0:T(8,128)(2,1)S(1)}, u32[]{:S(2)}, u32[]{:S(2)}) collective-permute-start(bf16[512,1024]{1,0:T(8,128)(2,1)S(1)} %copy-done.1), channel_id=1, source_target_pairs={{0,1},{1,0},{2,3},{3,2},{4,5},{5,4},{6,7},{7,6},{8,10},{9,11},{10,... | collective-permute-start | bytes 3145736 | tf_op jit(solution)/shard_map/ppermute | solution.py:398
  189.5 23.9 %collective-permute-start.17 = (bf16[512,1024]{1,0:T(8,128)(2,1)S(1)}, bf16[512,1024]{1,0:T(8,128)(2,1)}, u32[]{:S(2)}, u32[]{:S(2)}) collective-permute-start(bf16[512,1024]{1,0:T(8,128)(2,1)S(1)} %copy-done.1), channel_id=1, source_target_pairs={{0,6},{1,7},{2,0},{3,1},{4,2},{5,3},{6,4},{7,5},{8,14},{9,15},{10,... | collective-permute-start | bytes 3145736 | tf_op jit(solution)/shard_map/ppermute | solution.py:398
  203.0 25.9 %copy-start.3 = (bf16[512,1024]{1,0:T(8,128)(2,1)}, bf16[512,1024]{1,0:T(8,128)(2,1)S(1)}, u32[]{:S(2)}) copy-start(bf16[512,1024]{1,0:T(8,128)(2,1)S(1)} %collective-permute-done.4.refs_1_) | copy-start | bytes 3145732
  203.0 21.5 %collective-permute-start.5 = (bf16[512,1024]{1,0:T(8,128)(2,1)S(1)}, bf16[512,1024]{1,0:T(8,128)(2,1)S(1)}, u32[]{:S(2)}, u32[]{:S(2)}) collective-permute-start(bf16[512,1024]{1,0:T(8,128)(2,1)S(1)} %collective-permute-done.4.refs_1_), channel_id=1, source_target_pairs={{0,6},{1,7},{2,0},{3,1},{4,2},{5,3},{6,4},{7,5},{8,10},{9,11},{10,... | collective-permute-start | bytes 3145736 | tf_op jit(solution)/shard_map/ppermute | solution.py:398
  206.3 30.6 %collective-permute-start.19 = (bf16[512,1024]{1,0:T(8,128)(2,1)S(1)}, bf16[512,1024]{1,0:T(8,128)(2,1)}, u32[]{:S(2)}, u32[]{:S(2)}) collective-permute-start(bf16[512,1024]{1,0:T(8,128)(2,1)S(1)} %copy-done.1), channel_id=1, source_target_pairs={{0,2},{1,3},{2,4},{3,5},{4,6},{5,7},{6,0},{7,1},{8,9},{9,8},{10,11... | collective-permute-start | bytes 3145736 | tf_op jit(solution)/shard_map/ppermute | solution.py:398
  206.3 38.0 %collective-permute-start.16 = (bf16[512,1024]{1,0:T(8,128)(2,1)S(1)}, bf16[512,1024]{1,0:T(8,128)(2,1)}, u32[]{:S(2)}, u32[]{:S(2)}) collective-permute-start(bf16[512,1024]{1,0:T(8,128)(2,1)S(1)} %collective-permute-done.4.refs_1_), channel_id=1, source_target_pairs={{0,2},{1,3},{2,4},{3,5},{4,6},{5,7},{6,0},{7,1},{8,9},{9,8},{10,11... | collective-permute-start | bytes 3145736 | tf_op jit(solution)/shard_map/ppermute | solution.py:398
  213.4 31.0 %collective-permute-start.18 = (bf16[512,1024]{1,0:T(8,128)(2,1)}, bf16[512,1024]{1,0:T(8,128)(2,1)}, u32[]{:S(2)}, u32[]{:S(2)}) collective-permute-start(bf16[512,1024]{1,0:T(8,128)(2,1)} %collective-permute-done.17.refs_2_), channel_id=1, source_target_pairs={{0,6},{1,7},{2,0},{3,1},{4,2},{5,3},{6,4},{7,5},{8,9},{9,8},{10,11... | collective-permute-start | bytes 3145736 | tf_op jit(solution)/shard_map/ppermute | solution.py:398
  224.5 12.4 %copy-start.2 = (bf16[512,1024]{1,0:T(8,128)(2,1)}, bf16[512,1024]{1,0:T(8,128)(2,1)S(1)}, u32[]{:S(2)}) copy-start(bf16[512,1024]{1,0:T(8,128)(2,1)S(1)} %collective-permute-done.5.refs_1_) | copy-start | bytes 3145732
  224.5 27.3 %collective-permute-start.6 = (bf16[512,1024]{1,0:T(8,128)(2,1)S(1)}, bf16[512,1024]{1,0:T(8,128)(2,1)}, u32[]{:S(2)}, u32[]{:S(2)}) collective-permute-start(bf16[512,1024]{1,0:T(8,128)(2,1)S(1)} %collective-permute-done.5.refs_1_), channel_id=1, source_target_pairs={{0,6},{1,7},{2,0},{3,1},{4,2},{5,3},{6,4},{7,5},{8,9},{9,8},{10,11... | collective-permute-start | bytes 3145736 | tf_op jit(solution)/shard_map/ppermute | solution.py:398
